TPU v7x, 256 devices: a whole 4x4x8 slice. The times are simulated.
256 devices in a mesh: tm: 32 (over y, z), tensor: 8 (over x, core).
Axes of the slice: x: 4, y: 4, z: 8, core: 2. Of those that a mesh axis runs over, the one named last changes fastest.
Arguments:
- frames_in: bfloat16 [32, 520, 1024], P('tm'), may hold values from -6 to 6
- frame_time: int32 [16], replicated, may hold values from 0 to 15, each once
- cond_count: int32 [16], replicated, may hold values from 0 to 2
- ln1_gain: float32 [2, 1024], replicated, may hold values from 0.5 to 1.5
- ln1_bias: float32 [2, 1024], replicated, may hold values from -1.75 to 1.75
- qkv_weight: bfloat16 [2, 3, 1024, 1024], P(None, None, None, 'tensor'), may hold values from -17 to 17
- qkv_bias: float32 [2, 3, 1024], P(None, None, 'tensor'), may hold values from -1.75 to 1.75
- out_weight: bfloat16 [2, 1024, 1024], P(None, 'tensor'), may hold values from -0.1875 to 0.1875
- out_bias: float32 [2, 1024], replicated, may hold values from -1.75 to 1.75
- ln2_gain: float32 [2, 1024], replicated, may hold values from 0.5 to 1.5
- ln2_bias: float32 [2, 1024], replicated, may hold values from -1.75 to 1.75
- fc1_weight: bfloat16 [2, 1024, 4096], P(None, None, 'tensor'), may hold values from -0.1875 to 0.1875
- fc1_bias: float32 [2, 4096], P(None, 'tensor'), may hold values from -3 to 3
- fc2_weight: bfloat16 [2, 4096, 1024], P(None, 'tensor'), may hold values from -0.09375 to 0.09375
- fc2_bias: float32 [2, 1024], replicated, may hold values from -1.75 to 1.75
Outputs:
- frames_out: bfloat16 [32, 520, 1024], P('tm', 'tensor')
Inputs may be any that keep to these rules, and one draw needn't show every extreme that they name: `frame_time`: every time index 0 to 15 appears once. `cond_count`: the valid action and state tokens of a frame are its first ones.
All inputs are finite; a program needn't handle non-finite values.
Results may differ from a plain program's by a relative error of at most 0.04.
Values may be sent and summed in bfloat16 or wider, within the bound.
No kernel may reach another device: no remote copies, remote signals or barrier semaphores. Data moves between devices by JAX's collectives and lax.ppermute only.
A program may use at most 128 MiB of HBM per device.

v0:
```python
import functools

import jax
import jax.numpy as jnp
from jax import lax
from jax.experimental import pallas as pl
from jax.experimental.pallas import tpu as pltpu
from jax.sharding import PartitionSpec as P

D = 1024
LAYERS = 2
PARTS = 32
FRAMES = 16
BLOCK = 65
PAD = 72
KEYS = 2176
NX = 4
HELD = 1032
LOG2E = 1.4426950408889634
SCALE = 0.125 * LOG2E
NEG = -1e30

GROUPS = ((0,), (1, 3), (2,))


def lanes(shape):
    return lax.broadcasted_iota(jnp.int32, shape, len(shape) - 1)


def subs(shape):
    return lax.broadcasted_iota(jnp.int32, shape, len(shape) - 2)


def norm(rows, gain, bias):
    center = jnp.mean(rows, axis=-1, keepdims=True)
    off = rows - center
    spread = jnp.mean(off * off, axis=-1, keepdims=True)
    return off * lax.rsqrt(spread + 1e-06) * gain + bias


def tables_kernel(frame_time, cond_count, w1_ref, b1_ref, w2_ref, order, mask, row_time, packed, bias, sems):
    copies = [
        pltpu.make_async_copy(w1_ref.at[1], packed.at[0, 0:D], sems.at[0]),
        pltpu.make_async_copy(w2_ref.at[1, :, 0:512], packed.at[1, 0:512], sems.at[1]),
        pltpu.make_async_copy(w2_ref.at[1, :, 512:D], packed.at[1, 512:D], sems.at[2]),
        pltpu.make_async_copy(b1_ref, bias, sems.at[3]),
    ]
    for copy in copies:
        copy.start()
    for f in range(FRAMES):
        order[frame_time[f]] = f
    slot_time = jnp.full((FRAMES, 128), FRAMES, jnp.int32)
    times = jnp.zeros((PARTS, 128), jnp.int32)
    for g in range(PARTS):
        time = frame_time[g // 2]
        seen = jnp.where(g % 2 < cond_count[g // 2], time, FRAMES)
        slot_time = jnp.where(lanes(slot_time.shape) == g, seen, slot_time)
        times = jnp.where(subs(times.shape) == g, time, times)
    row_time[...] = times
    mask[:, 0:128] = jnp.where(slot_time <= subs(slot_time.shape), 0.0, NEG).astype(jnp.bfloat16)
    for t in range(FRAMES):
        seen = jnp.where(subs((FRAMES, 128)) >= t, 0.0, NEG)
        mask[:, 128 * t + 128 : 128 * t + 256] = seen.astype(jnp.bfloat16)
    for copy in copies:
        copy.wait()
    packed[0, D:HELD, :] = split_rows(bias[1:2, :])
    packed[1, D:HELD, :] = jnp.zeros((8, 512), jnp.bfloat16)


def split_rows(row):
    high = row.astype(jnp.bfloat16).astype(jnp.float32)
    middle = (row - high).astype(jnp.bfloat16).astype(jnp.float32)
    lowest = (row - high) - middle
    sub = subs((8, row.shape[1]))
    rows = jnp.where(sub == 0, high, jnp.where(sub == 1, middle, jnp.where(sub == 2, lowest, 0.0)))
    return rows.astype(jnp.bfloat16)


def from_row(ref, base, off, count):
    return pltpu.roll(ref[pl.ds(pl.multiple_of(base, 8), count), :], lax.rem(count - off, count), 0)


def emit(out, q, key, val, places, tails):
    low = lanes(q.shape) < 64
    low8 = lanes((8, 128)) < 64
    sub = lax.broadcasted_iota(jnp.int32, (8, 128), 0)
    q_r, key_r, val_r = (pltpu.roll(a, 64, 1) for a in (q, key, val))
    for hl in range(2):
        if hl == 0:
            kv = jnp.where(low, key, val_r)
            q_lo, q_hi = q, q_r
        else:
            kv = jnp.where(low, key_r, val)
            q_lo, q_hi = q_r, q
        for slot, at in places:
            out[slot + hl, 0:32, :] = kv[at : at + 32].astype(jnp.bfloat16)
            out[slot + hl, 32:48, :] = jnp.where(
                low[:16], q_lo[at : at + 16], q_hi[at + 16 : at + 32]
            ).astype(jnp.bfloat16)
            out[slot + hl, 48:56, :] = jnp.zeros((8, 128), jnp.bfloat16)
        for slot, at in tails:
            tail = jnp.where(
                sub == 0,
                jnp.broadcast_to(kv[at : at + 1], (8, 128)),
                jnp.where((sub == 1) & low8, jnp.broadcast_to(q_lo[at : at + 1], (8, 128)), 0.0),
            )
            out[slot + hl, 48:56, :] = tail.astype(jnp.bfloat16)


def start_kernel(
    idx, x_ref, w_ref, wo_ref, bias_ref, g_ref, b_ref, rows, own, out, held, raw, wide, w, biases, norms, sems
):
    x, k = idx[0], idx[1]
    copies = [
        pltpu.make_async_copy(x_ref.at[0], raw, sems.at[0]),
        pltpu.make_async_copy(w_ref.at[0, 0], w.at[0], sems.at[1]),
        pltpu.make_async_copy(w_ref.at[0, 1], w.at[1], sems.at[2]),
        pltpu.make_async_copy(w_ref.at[0, 2], w.at[2], sems.at[15]),
        pltpu.make_async_copy(bias_ref, biases, sems.at[14]),
        pltpu.make_async_copy(w_ref.at[1], held.at[0:3, 0:D, :], sems.at[3]),
    ]
    for j in range(8):
        cols = slice(128 * j, 128 * j + 128)
        copies.append(pltpu.make_async_copy(wo_ref.at[1, :, cols], held.at[3, cols, :], sems.at[4 + j]))
    first = [
        pltpu.make_async_copy(g_ref, norms.at[0], sems.at[12]),
        pltpu.make_async_copy(b_ref, norms.at[1], sems.at[13]),
    ]
    for copy in first + copies:
        copy.start()
    copies[0].wait()
    wide[...] = raw[...].astype(jnp.float32)
    for copy in first:
        copy.wait()
    gain, bias = norms[0, 0:1, :], norms[1, 0:1, :]
    for s in range(NX):
        chip = lax.rem(x + s, NX)
        for b in range(2):
            part = from_row(wide, 64 * (2 * chip + b) + 32 * k, 2 * chip + b, 40)[:32]
            at = PAD * s + 32 * b
            rows[at : at + 32, :] = norm(part, gain, bias).astype(jnp.bfloat16)
            if s == 0:
                own[32 * b : 32 * b + 32, :] = part.astype(jnp.bfloat16)
        part = from_row(wide, 64 * (2 * chip + k) + 64, 2 * chip + k, 8)
        rows[PAD * s + 64 : PAD * s + 72, :] = norm(part, gain, bias).astype(jnp.bfloat16)
        if s == 0:
            own[64:65, :] = part[:1].astype(jnp.bfloat16)
    copies[4].wait()
    heads_of(k, k, rows, w, biases, out, copies[1:4])
    for copy in copies[5:]:
        copy.wait()
    for i in range(3):
        held[i, D:HELD, :] = split_rows(biases[i, 1:2, :])
    held[3, D:HELD, :] = jnp.zeros((8, 128), jnp.bfloat16)


def heads_of(k, side, rows, w, biases, out, copies):
    places = [(s * 8 + b * 4 + 2 * side, 72 * s + 32 * b) for s in range(NX) for b in range(2)]
    tails = [(s * 8 + k * 4 + 2 * side, 72 * s + 64) for s in range(NX)]
    parts = []
    for i in range(3):
        copies[i].wait()
        parts.append(jnp.dot(rows[...], w[i], preferred_element_type=jnp.float32) + biases[i, 0:1, :])
    emit(out, *parts, places, tails)


def partner_kernel(idx, rows, w_ref, biases, other, out, w, sems):
    k = idx[1]
    copies = [pltpu.make_async_copy(w_ref.at[0, i], w.at[i], sems.at[i]) for i in range(3)]
    for copy in copies:
        copy.start()
    heads_of(k, 1 - k, rows, w, biases, out, copies)


def turn_kernel(idx, first, y0, y1, y2, y3, o_bias, gain, bias, *rest):
    owns, pars, (stream, out, rows, w, acc, sems) = rest[:NX], rest[NX : 2 * NX], rest[2 * NX :]
    k = idx[1]
    copies = [pltpu.make_async_copy(owns[s].at[0:3], w.at[s], sems.at[s]) for s in range(NX)]
    for copy in copies:
        copy.start()
    summed = (y0[...].astype(jnp.float32) + y1[...].astype(jnp.float32)) + (
        y2[...].astype(jnp.float32) + y3[...].astype(jnp.float32)
    )
    new = (first[...] + summed + o_bias[0:1, :]).astype(jnp.bfloat16)
    stream[...] = new
    rows[0:65, :] = norm(new.astype(jnp.float32), gain[1:2, :], bias[1:2, :]).astype(jnp.bfloat16)

    def project(c, weight):
        for i in range(3):
            bias_row = jnp.sum(weight[i, D:HELD, :].astype(jnp.float32), axis=0, keepdims=True)
            acc[c, i] = jnp.dot(rows[...], weight[i, 0:D, :], preferred_element_type=jnp.float32) + bias_row

    for s in range(NX):
        project(2 * s + 1, pars[s])

    def arrived(s, carry):
        pltpu.make_async_copy(owns[0].at[0:3], w.at[s], sems.at[s]).wait()
        project(2 * s, w.at[s])
        return carry

    lax.fori_loop(0, NX, arrived, 0)

    def one(c, carry):
        base = c // 2 * 4 + 2 * lax.rem(k + c, 2)
        emit(out, acc[c, 0], acc[c, 1], acc[c, 2], [(base, 0), (16 + base, 32)], [(k * 16 + base, 64)])
        return carry

    lax.fori_loop(0, 2 * NX, one, 0)


def attn_kernel(layer, idx, order, mask, part_time, r_own, r_par, out, kt, vals, score, prob):
    mine = idx[2 + layer]
    low = lanes((128, 128)) < 64

    def place(at, block):
        key, val = block.astype(jnp.float32), block
        both = jnp.where(low, key, pltpu.roll(key, 64, 1))
        kt[0:128, at : at + 128] = both.T.astype(jnp.bfloat16)
        vals[at : at + 128, :] = jnp.where(low, jnp.ones_like(val), val)

    def queries(packed, which):
        scaled = packed * SCALE
        high = scaled.astype(jnp.bfloat16).astype(jnp.float32)
        rest = scaled - high
        left = jnp.where(lanes(packed.shape) < 64, high, pltpu.roll(rest, 64, 1))
        return jnp.concatenate([left.astype(jnp.bfloat16), which.astype(jnp.bfloat16)], axis=1)

    sub = lax.broadcasted_iota(jnp.int32, (PARTS, 8, 128), 1)
    tail_own = r_own[:, 48:56, :].astype(jnp.float32)
    tail_par = r_par[:, 48:56, :].astype(jnp.float32)
    extra = jnp.sum(jnp.where(sub == 0, jnp.where(mine == 1, tail_own, tail_par), 0.0), axis=1)
    place(0, jnp.concatenate([extra, jnp.zeros((96, 128), jnp.float32)], axis=0).astype(jnp.bfloat16))
    kt[128:144, :] = mask[...]
    kt[144:256, :] = jnp.zeros((112, KEYS), jnp.bfloat16)
    for t in range(FRAMES):
        at = pl.ds(2 * order[t], 2)
        own = r_own[at, 0:32, :].reshape(64, 128)
        par = r_par[at, 0:32, :].reshape(64, 128)
        place(128 * t + 128, jnp.concatenate([own, par], axis=0))

    def attend(lhs, rows, n, buf):
        score[buf, 0:rows, 0:n] = jnp.dot(lhs, kt[:, 0:n], preferred_element_type=jnp.float32)
        for r in range(0, rows, 16):
            now = score[buf, r : r + 16, 0:n]
            now = jnp.exp2(now - jnp.max(now, axis=1, keepdims=True))
            prob[buf, r : r + 16, 0:n] = now.astype(jnp.bfloat16)
        mixed = jnp.dot(prob[buf, 0:rows, 0:n], vals[0:n, :], preferred_element_type=jnp.float32)
        return mixed / pltpu.roll(mixed, 64, 1)

    row = lax.broadcasted_iota(jnp.int32, (256, 128), 0)
    for i in range(4):
        packed = jnp.concatenate(
            [r_own[pl.ds(2 * order[4 * i + t], 2), 32:48, :].reshape(32, 128) for t in range(4)], axis=0
        ).astype(jnp.float32)
        packed = jnp.concatenate([packed, pltpu.roll(packed, 64, 1)], axis=0)
        which = jnp.where(lanes((256, 128)) == 4 * i + (row % 128) // 32, 1.0, 0.0)
        res = attend(queries(packed, which), 256, 128 + 512 * (i + 1), i % 2)
        merged = jnp.where(low, pltpu.roll(res[:128], 64, 1), res[128:]).astype(jnp.bfloat16)
        for t in range(4):
            out[pl.ds(2 * order[4 * i + t], 2), 0:16, :] = merged[32 * t : 32 * t + 32].reshape(2, 16, 128)
    packed = jnp.sum(jnp.where(sub == 1, tail_own, 0.0), axis=1)
    which = jnp.where(lanes((PARTS, 128)) == part_time[...], 1.0, 0.0)
    res = pltpu.roll(attend(queries(packed, which), PARTS, KEYS, 0), 64, 1)
    out[:, 16:24, :] = jnp.broadcast_to(res[:, None, :], (PARTS, 8, 128)).astype(jnp.bfloat16)


def pair(first, second):
    low = lanes((24, 128)) < 64
    first, second = first.astype(jnp.float32), second.astype(jnp.float32)
    return (
        jnp.where(low, first, pltpu.roll(second, 64, 1)).astype(jnp.bfloat16),
        jnp.where(low, pltpu.roll(first, 64, 1), second).astype(jnp.bfloat16),
    )


def gather_heads(dst, at, back, patches, tail):
    for b, slot in enumerate(patches):
        lo, hi = pair(back[slot], back[slot + 1])
        dst[at + 32 * b : at + 32 * b + 16, :] = lo[:16]
        dst[at + 32 * b + 16 : at + 32 * b + 32, :] = hi[:16]
    lo, _ = pair(back[tail], back[tail + 1])
    dst[at + 64 : at + 72, :] = lo[16:24]


def out_kernel(idx, back, w_own, w_par, p0, p1, p2, p3, left, right):
    k = idx[1]
    for dst, side in ((left, k), (right, 1 - k)):
        for s in range(NX):
            slots = [s * 8 + b * 4 + 2 * side for b in range(2)]
            gather_heads(dst, 72 * s, back, slots, s * 8 + k * 4 + 2 * side)
    for j in range(4):
        cols = slice(256 * j, 256 * j + 256)
        partial = jnp.dot(left[...], w_own[0, :, cols], preferred_element_type=jnp.float32) + jnp.dot(
            right[...], w_par[0, :, cols], preferred_element_type=jnp.float32
        )
        for s, out in enumerate((p0, p1, p2, p3)):
            out[:, cols] = partial[72 * s : 72 * s + 65].astype(jnp.bfloat16)


def mid_kernel(layer, own, p0, p1, p2, p3, o_bias, gain, bias, first, normed):
    rows = own[...].astype(jnp.float32)
    summed = (p0[...].astype(jnp.float32) + p1[...].astype(jnp.float32)) + (
        p2[...].astype(jnp.float32) + p3[...].astype(jnp.float32)
    )
    rows = rows + summed + o_bias[layer : layer + 1, :]
    first[...] = rows
    normed[...] = norm(rows, gain[layer : layer + 1, :], bias[layer : layer + 1, :]).astype(jnp.bfloat16)


def whole_out_kernel(idx, back, own, o_bias, gain, bias, *rest):
    owns, pars, (first, normed, heads, w, sems) = rest[:NX], rest[NX : 2 * NX], rest[2 * NX :]
    k = idx[1]
    copies = [pltpu.make_async_copy(owns[s].at[3, 0:D], w.at[s], sems.at[s]) for s in range(NX)]
    for copy in copies:
        copy.start()
    total = None
    for c, side in ((1, 1 - k), (0, k)):
        for s in range(NX):
            base = s * 4 + 2 * side
            gather_heads(heads.at[2 * s + c], 0, back, [base, 16 + base], k * 16 + base)
            if c == 0:
                copies[s].wait()
            source = w.at[s] if c == 0 else pars[s].at[3]
            weight = jnp.concatenate([source[128 * j : 128 * j + 128, :] for j in range(8)], axis=1)
            part = jnp.dot(heads[2 * s + c], weight, preferred_element_type=jnp.float32)
            total = part if total is None else total + part
    rows = own[...].astype(jnp.float32) + total[:65] + o_bias[1:2, :]
    first[...] = rows
    normed[...] = norm(rows, gain[1:2, :], bias[1:2, :]).astype(jnp.bfloat16)


def mlp_kernel(layer, count, *refs):
    blocks, (w1_own, w1_par, b1_own, b1_par, w2_own, w2_par), outs, rows = (
        refs[:count],
        refs[count : count + 6],
        refs[count + 6 : 2 * count + 6],
        refs[-1],
    )
    for c, n in enumerate(blocks):
        rows[PAD * c : PAD * c + 65, :] = n[...]
    total = None
    for w1, b1, w2 in ((w1_own, b1_own, w2_own), (w1_par, b1_par, w2_par)):
        inner = jnp.dot(rows[...], w1[layer], preferred_element_type=jnp.float32) + b1[layer : layer + 1, :]
        inner = (0.5 * inner * (1.0 + lax.erf(inner * 0.7071067811865476))).astype(jnp.bfloat16)
        part = jnp.dot(inner, w2[layer], preferred_element_type=jnp.float32)
        total = part if total is None else total + part
    for c, y in enumerate(outs):
        y[...] = total[PAD * c : PAD * c + 65].astype(jnp.bfloat16)


def pair_mlp_kernel(n, w1_own, w1_par, b1_own, b1_par, w2_own, w2_par, far, far_par, y, rows):
    rows[0:65, :] = n[...]

    def hidden(w1, b1):
        inner = jnp.dot(rows[...], w1, preferred_element_type=jnp.float32) + b1
        return (0.5 * inner * (1.0 + lax.erf(inner * 0.7071067811865476))).astype(jnp.bfloat16)

    total = None
    for w1, b1, w2 in ((w1_own, b1_own, w2_own), (w1_par, b1_par, w2_par)):
        part = jnp.dot(hidden(w1[1], b1[1:2, :]), w2[1], preferred_element_type=jnp.float32)
        total = part if total is None else total + part
    for w in (far, far_par):
        bias = jnp.sum(w[0, D:HELD, :].astype(jnp.float32), axis=0, keepdims=True)
        inner = hidden(w[0, 0:D, :], bias)
        total += jnp.concatenate(
            [
                jnp.dot(inner, w[1, 512 * j : 512 * j + 512, :], preferred_element_type=jnp.float32)
                for j in range(2)
            ],
            axis=1,
        )
    y[...] = total[:65].astype(jnp.bfloat16)


def last_kernel(idx, first, y0, y1, o_bias, stream, send):
    k = idx[1]
    summed = y0[...].astype(jnp.float32) + y1[...].astype(jnp.float32)
    rows = (first[...] + summed + o_bias[1:2, :]).astype(jnp.bfloat16)
    stream[...] = rows
    send[...] = jnp.where(k == 0, rows[32:64], rows[0:32])


def place_kernel(idx, stream, recv, out):
    k = idx[1]
    out[0, 0:32, :] = jnp.where(k == 0, stream[0:32, :], recv[...])
    out[0, 32:64, :] = jnp.where(k == 0, recv[...], stream[32:64, :])
    out[0, 64:65, :] = stream[64:65, :]


VMEM = pl.BlockSpec(memory_space=pltpu.VMEM)
SMEM = pl.BlockSpec(memory_space=pltpu.SMEM)
HBM = pl.BlockSpec(memory_space=pltpu.HBM)


def block(dtype=jnp.bfloat16, rows=BLOCK):
    return jax.ShapeDtypeStruct((rows, D), dtype)


def call(kernel, args, out_shape, scratch=(), scalars=1, limit=8, out_specs=None, in_specs=None, aliases=None):
    return pl.pallas_call(
        kernel,
        out_shape=out_shape,
        in_specs=in_specs or [SMEM] * scalars + [VMEM] * (len(args) - scalars),
        out_specs=out_specs or ([VMEM] * len(out_shape) if isinstance(out_shape, list) else VMEM),
        scratch_shapes=list(scratch),
        input_output_aliases=aliases or {},
        compiler_params=pltpu.CompilerParams(vmem_limit_bytes=limit << 20),
    )(*args)


def of_layer(layer, array):
    rest = array.shape[1:]
    zeros = (0,) * len(rest)
    return pl.BlockSpec((1, *rest), lambda i: (layer, *zeros))


def shards(
    frames_in,
    frame_time,
    cond_count,
    ln1_gain,
    ln1_bias,
    qkv_weight,
    qkv_bias,
    out_weight,
    out_bias,
    ln2_gain,
    ln2_bias,
    fc1_weight,
    fc1_bias,
    fc2_weight,
    fc2_bias,
):
    part = lax.axis_index("tm")
    pos = lax.axis_index("tensor")
    x, k = pos // 2, pos % 2

    def shift(array, s):
        pairs = [(t, ((t // 2 + s) % NX) * 2 + t % 2) for t in range(2 * NX)]
        return lax.ppermute(array, "tensor", pairs)

    def swap(array):
        return lax.ppermute(array, "tensor", [(t, t ^ 1) for t in range(2 * NX)])

    def spread(array):
        return [array] + [shift(array, -s) for s in (1, 2, 3)]

    def collect(parts):
        return [parts[0]] + [shift(parts[s], s) for s in (1, 2, 3)]

    tie = lax.optimization_barrier
    seen = []

    def attention(layer, message, *late):
        arrived = lax.all_to_all(message, "tm", 0, 0, tiled=True)
        arrived, *late = tie((arrived, *late))
        arrived_par = swap(arrived)
        if layer == 0:
            seen.extend(
                call(
                    tables_kernel,
                    (frame_time, cond_count, *in_hbm(fc1_weight, fc1_bias, fc2_weight)),
                    [
                        jax.ShapeDtypeStruct((FRAMES,), jnp.int32),
                        jax.ShapeDtypeStruct((FRAMES, KEYS), jnp.bfloat16),
                        jax.ShapeDtypeStruct((PARTS, 128), jnp.int32),
                        jax.ShapeDtypeStruct((2, HELD, 512), jnp.bfloat16),
                    ],
                    [pltpu.VMEM((LAYERS, 512), jnp.float32), pltpu.SemaphoreType.DMA((4,))],
                    in_specs=[SMEM] * 2 + [HBM] * 3,
                    out_specs=[SMEM, VMEM, VMEM, VMEM],
                )
            )
        order, mask, row_time, _ = seen
        arrived, arrived_par, *late = tie((arrived, arrived_par, *late))
        late = [swap(a) for a in late]
        mixed = call(
            functools.partial(attn_kernel, layer),
            (idx, order, mask, row_time, arrived, arrived_par),
            jax.ShapeDtypeStruct((PARTS, 24, 128), jnp.bfloat16),
            [
                pltpu.VMEM((256, KEYS), jnp.bfloat16),
                pltpu.VMEM((KEYS, 128), jnp.bfloat16),
                pltpu.VMEM((2, 256, KEYS), jnp.float32),
                pltpu.VMEM((2, 256, KEYS), jnp.bfloat16),
            ],
            scalars=2,
            limit=24,
        )
        mixed, *late = tie((mixed, *late))
        back = lax.all_to_all(mixed, "tm", 0, 0, tiled=True)
        return tie((back, *late))

    message_shape = jax.ShapeDtypeStruct((PARTS, 56, 128), jnp.bfloat16)

    def mlp(layer, blocks):
        outs = {}
        for group in GROUPS:
            done = call(
                functools.partial(mlp_kernel, layer, len(group)),
                (*(blocks[s] for s in group), *(fc1_weight, fc1_par, fc1_bias, fc1_bias_par, fc2_weight, fc2_par)),
                [block()] * len(group),
                [pltpu.VMEM((PAD * len(group), D), jnp.bfloat16)],
                scalars=0,
            )
            outs.update(zip(group, done))
        return [outs[s] for s in range(NX)]

    def in_hbm(*arrays):
        return [pltpu.with_memory_space_constraint(a, pltpu.HBM) for a in arrays]

    biases = jnp.transpose(qkv_bias, (1, 0, 2))
    qkv_par = swap(qkv_weight)
    biases_par = swap(biases)
    fc2_par = swap(fc2_weight)
    idx = jnp.stack([x, k, k == (part // 4) % 2, k == part // 16]).astype(jnp.int32)
    rows, stream, message, held = call(
        start_kernel,
        (idx, *in_hbm(frames_in, qkv_weight, out_weight, biases, ln1_gain, ln1_bias)),
        [
            block(rows=NX * PAD),
            block(),
            message_shape,
            jax.ShapeDtypeStruct((4, HELD, 128), jnp.bfloat16),
        ],
        [
            pltpu.VMEM((8 * BLOCK, D), jnp.bfloat16),
            pltpu.VMEM((8 * BLOCK, D), jnp.float32),
            pltpu.VMEM((3, D, 128), jnp.bfloat16),
            pltpu.VMEM((3, 2, 128), jnp.float32),
            pltpu.VMEM((2, LAYERS, D), jnp.float32),
            pltpu.SemaphoreType.DMA((16,)),
        ],
        in_specs=[SMEM] + [HBM] * 6,
    )
    helds = spread(held)
    held_par = swap(held)
    qkv_par, biases_par, message = tie((qkv_par, biases_par, message))
    message = call(
        partner_kernel,
        (idx, rows, *in_hbm(qkv_par), biases_par, message),
        message_shape,
        [pltpu.VMEM((3, D, 128), jnp.bfloat16), pltpu.SemaphoreType.DMA((3,))],
        in_specs=[SMEM, VMEM, HBM, VMEM, VMEM],
        aliases={4: 0},
    )
    message, fc2_par, held_par, idx, frame_time, cond_count = tie(
        (message, fc2_par, held_par, idx, frame_time, cond_count)
    )
    back, out_par, fc1_par, fc1_bias_par = attention(0, message, out_weight, fc1_weight, fc1_bias)
    partial = pl.pallas_call(
        out_kernel,
        grid=(1,),
        out_shape=[block()] * 4,
        in_specs=[SMEM, VMEM, of_layer(0, out_weight), of_layer(0, out_par)],
        out_specs=[VMEM] * 4,
        scratch_shapes=[pltpu.VMEM((NX * PAD, 128), jnp.bfloat16)] * 2,
        compiler_params=pltpu.CompilerParams(vmem_limit_bytes=12 << 20),
    )(idx, back, out_weight, out_par)
    partial = collect(partial)
    first, normed_two = call(
        functools.partial(mid_kernel, 0),
        (stream, *partial, out_bias, ln2_gain, ln2_bias),
        [block(jnp.float32), block()],
        scalars=0,
    )
    partial = mlp(0, spread(normed_two))
    partial = collect(partial)
    held_pars = [held_par] + [swap(helds[s]) for s in (1, 2, 3)]
    everything = (*in_hbm(*helds), *held_pars)
    stream, message = call(
        turn_kernel,
        (idx, first, *partial, fc2_bias, ln1_gain, ln1_bias, *everything),
        [block(), message_shape],
        [
            pltpu.VMEM((PAD, D), jnp.bfloat16),
            pltpu.VMEM((NX, 3, HELD, 128), jnp.bfloat16),
            pltpu.VMEM((2 * NX, 3, PAD, 128), jnp.float32),
            pltpu.SemaphoreType.DMA((NX,)),
        ],
        in_specs=[SMEM] + [VMEM] * 8 + [HBM] * 4 + [VMEM] * 4,
        limit=14,
    )
    message, packed = tie((message, seen[3]))

    def pair(array, other):
        return lax.ppermute(array, "tensor", [(t, other(t // 2) * 2 + t % 2) for t in range(2 * NX)])

    far = pair(packed, lambda c: c ^ 1)
    (back,) = attention(1, message)
    back, far = tie((back, far))
    far_par = swap(far)
    first, normed_two = call(
        whole_out_kernel,
        (idx, back, stream, out_bias, ln2_gain, ln2_bias, *everything),
        [block(jnp.float32), block()],
        [
            pltpu.VMEM((2 * NX, PAD, 128), jnp.bfloat16),
            pltpu.VMEM((NX, D, 128), jnp.bfloat16),
            pltpu.SemaphoreType.DMA((NX,)),
        ],
        in_specs=[SMEM] + [VMEM] * 5 + [HBM] * 4 + [VMEM] * 4,
    )
    weights = (fc1_weight, fc1_par, fc1_bias, fc1_bias_par, fc2_weight, fc2_par, far, far_par)
    partial = []
    for n in (normed_two, pair(normed_two, lambda c: 3 - c)):
        partial.append(
            call(
                pair_mlp_kernel,
                (n, *weights),
                block(),
                [pltpu.VMEM((PAD, D), jnp.bfloat16)],
                scalars=0,
            )
        )
    added = pair(partial[1], lambda c: 3 - c)
    stream, send = call(
        last_kernel, (idx, first, partial[0], added, fc2_bias), [block(), block(rows=32)]
    )
    recv = swap(send)
    return call(place_kernel, (idx, stream, recv), jax.ShapeDtypeStruct((1, BLOCK, D), jnp.bfloat16))


def solution(mesh):
    in_specs = (
        P("tm", None, None),
        P(),
        P(),
        P(),
        P(),
        P(None, None, None, "tensor"),
        P(None, None, "tensor"),
        P(None, "tensor", None),
        P(),
        P(),
        P(),
        P(None, None, "tensor"),
        P(None, "tensor"),
        P(None, "tensor", None),
        P(),
    )
    out_specs = P("tm", "tensor", None)
    return jax.shard_map(shards, mesh=mesh, in_specs=in_specs, out_specs=out_specs, check_vma=False)
```

profile of v0, /device:TPU:35, one launch (start us, length us, event | category | flops | bytes accessed | tf_op | source)
XLA Modules:
  0.0 220.9 jit_solution(7447465250503690779)
XLA Ops:
  0.8 4.0 %shard_map.145 = (bf16[288,1024]{1,0:T(8,128)(2,1)S(1)}, bf16[65,1024]{1,0:T(8,128)(2,1)S(1)}, bf16[32,56,128]{2,1,0:T(8,128)(2,1)S(1)}, bf16[4,1032,128]{2,1,0:T(8,128)(2,1)S(1)}) custom-call(s32[4]{0:T(128)S(1)} %pad_add_fusion.idx, bf16[1,520,1024]{2,1,0:T(8,128)(2,1)} %x_ref.1, bf16[2,3,1024,128]{3,2,1,0:T(8,128)(2,1)} %w_ref.1, ...), custom_call_target="tpu_custom_call" | custom-call | tf_op jit(solution)/shard_map/pallas_call | solution.py:400
  5.5 2.9 %collective-permute-done.1.biases = f32[3,2,128]{2,1,0:T(2,128)S(1)} collective-permute-done((f32[3,2,128]{2,1,0:T(2,128)S(1)}, f32[3,2,128]{2,1,0:T(2,128)S(1)}, u32[]{:S(2)}, u32[]{:S(2)}) %collective-permute-start.1) | collective-permute-done | bytes 3104 | tf_op jit(solution)/shard_map/ppermute | solution.py:443
  8.5 2.8 %shard_map.146 = bf16[32,56,128]{2,1,0:T(8,128)(2,1)S(1)} custom-call(s32[4]{0:T(128)S(1)} %pad_add_fusion.idx, bf16[288,1024]{1,0:T(8,128)(2,1)S(1)} %get-tuple-element.59.rows, bf16[2,3,1024,128]{3,2,1,0:T(8,128)(2,1)} %collective-permute-done.w_ref, f32[3,2,128]{2,1,0:T(2,128)S(1)} %collective-permute-done.1.biases, ...), custom_call_target="tpu_custom_call", output_to_operand_aliasing={{}: (4, {})} | custom-call | tf_op jit(solution)/shard_map/pallas_call | solution.py:400
  11.3 25.7 %all_to_all.20.r_own = bf16[32,56,128]{2,1,0:T(8,128)(2,1)S(1)} all-to-all(bf16[32,56,128]{2,1,0:T(8,128)(2,1)S(1)} %shard_map.146), channel_id=1, replica_groups=mesh['tm'=32,'tensor'=8] {'tm'}, dimensions={0} | all-to-all | bytes 917504 | tf_op jit(solution)/shard_map/all_to_all | solution.py:455
  37.0 2.4 %collective-permute-start.4 = (bf16[32,56,128]{2,1,0:T(8,128)(2,1)S(1)}, bf16[32,56,128]{2,1,0:T(8,128)(2,1)S(1)}, u32[]{:S(2)}, u32[]{:S(2)}) collective-permute-start(bf16[32,56,128]{2,1,0:T(8,128)(2,1)S(1)} %all_to_all.20.r_own), channel_id=1, source_target_pairs={{0,1},{1,0},{2,3},{3,2},{4,5},{5,4},{6,7},{7,6},{8,9},{9,8},{10,11... | collective-permute-start | bytes 1376264 | tf_op jit(solution)/shard_map/ppermute | solution.py:443
  46.2 19.9 %collective-permute-done.19.rest_3_ = bf16[4,1032,128]{2,1,0:T(8,128)(2,1)S(1)} collective-permute-done((bf16[4,1032,128]{2,1,0:T(8,128)(2,1)S(1)}, bf16[4,1032,128]{2,1,0:T(8,128)(2,1)S(1)}, u32[]{:S(2)}, u32[]{:S(2)}) %collective-permute-start.19) | collective-permute-done | bytes 1056800 | tf_op jit(solution)/shard_map/ppermute | solution.py:440
  70.7 19.9 %collective-permute-done.17.rest_1_ = bf16[4,1032,128]{2,1,0:T(8,128)(2,1)S(1)} collective-permute-done((bf16[4,1032,128]{2,1,0:T(8,128)(2,1)S(1)}, bf16[4,1032,128]{2,1,0:T(8,128)(2,1)S(1)}, u32[]{:S(2)}, u32[]{:S(2)}) %collective-permute-start.17) | collective-permute-done | bytes 1056800 | tf_op jit(solution)/shard_map/ppermute | solution.py:440
  92.0 2.7 %shard_map.147 = (s32[16]{0:T(128)S(1)}, bf16[16,2176]{1,0:T(8,128)(2,1)S(1)}, s32[32,128]{1,0:T(8,128)S(1)}, bf16[2,1032,512]{2,1,0:T(8,128)(2,1)S(1)}) custom-call(s32[16]{0:T(128)S(1)} %copy-done.11, s32[16]{0:T(128)S(1)} %copy-done.12, bf16[2,1024,512]{2,1,0:T(8,128)(2,1)} %w1_own.3, f32[2,512]{1,0:T(2,128)} %b1_own.3, bf16[2,512,1024]{2,1,0:T(8,128)(2,1)} %w2_own.3), custom_call_target="tpu_custom_call" | custom-call | tf_op jit(solution)/shard_map/pallas_call | solution.py:400
  94.8 4.3 %shard_map.148 = bf16[32,24,128]{2,1,0:T(8,128)(2,1)S(1)} custom-call(s32[4]{0:T(128)S(1)} %pad_add_fusion.idx, s32[16]{0:T(128)S(1)} %get-tuple-element.68.order, bf16[16,2176]{1,0:T(8,128)(2,1)S(1)} %get-tuple-element.69.mask, s32[32,128]{1,0:T(8,128)S(1)} %get-tuple-element.70.part_time, bf16[32,56,128]{2,1,0:T(8,128)(2,1)S(1)} %all_to_all.20.r_own, ...), custom_call_target="tpu_custom_call" | custom-call | tf_op jit(solution)/shard_map/pallas_call | solution.py:400
  99.1 14.7 %all_to_all.21.back = bf16[32,24,128]{2,1,0:T(8,128)(2,1)S(1)} all-to-all(bf16[32,24,128]{2,1,0:T(8,128)(2,1)S(1)} %shard_map.148), channel_id=1, replica_groups=mesh['tm'=32,'tensor'=8] {'tm'}, dimensions={0} | all-to-all | bytes 393216 | tf_op jit(solution)/shard_map/all_to_all | solution.py:491
  118.9 4.7 %collective-permute-start.10 = (bf16[65,1024]{1,0:T(8,128)(2,1)S(1)}, bf16[65,1024]{1,0:T(8,128)(2,1)S(1)}, u32[]{:S(2)}, u32[]{:S(2)}) collective-permute-start(bf16[65,1024]{1,0:T(8,128)(2,1)S(1)} %get-tuple-element.91), channel_id=1, source_target_pairs={{0,6},{1,7},{2,0},{3,1},{4,2},{5,3},{6,4},{7,5},{8,14},{9,15},{10,... | collective-permute-start | bytes 399368 | tf_op jit(solution)/shard_map/ppermute | solution.py:440
  133.6 2.5 %shard_map.153 = bf16[65,1024]{1,0:T(8,128)(2,1)S(1)} custom-call(bf16[65,1024]{1,0:T(8,128)(2,1)S(1)} %collective-permute-done.14.refs_0_, bf16[2,1024,512]{2,1,0:T(8,128)(2,1)} %w1_own.3, bf16[2,1024,512]{2,1,0:T(8,128)(2,1)S(1)} %collective-permute-done.6.refs_2_.refs_3_.w1_par, f32[2,512]{1,0:T(2,128)S(1)} %copy-done.4, ...), custom_call_target="tpu_custom_call" | custom-call | tf_op jit(solution)/shard_map/pallas_call | solution.py:400
  137.2 2.5 %shard_map.152 = (bf16[65,1024]{1,0:T(8,128)(2,1)S(1)}, bf16[65,1024]{1,0:T(8,128)(2,1)S(1)}) custom-call(bf16[65,1024]{1,0:T(8,128)(2,1)S(1)} %collective-permute-done.11.refs_0_, bf16[65,1024]{1,0:T(8,128)(2,1)S(1)} %collective-permute-done.12.refs_1_, bf16[2,1024,512]{2,1,0:T(8,128)(2,1)} %w1_own.3, ...), custom_call_target="tpu_custom_call" | custom-call | tf_op jit(solution)/shard_map/pallas_call | solution.py:400
  142.2 2.5 %shard_map.151.y0 = bf16[65,1024]{1,0:T(8,128)(2,1)S(1)} custom-call(bf16[65,1024]{1,0:T(8,128)(2,1)S(1)} %get-tuple-element.93.refs_0_, bf16[2,1024,512]{2,1,0:T(8,128)(2,1)} %w1_own.3, bf16[2,1024,512]{2,1,0:T(8,128)(2,1)S(1)} %collective-permute-done.6.refs_2_.refs_3_.w1_par, f32[2,512]{1,0:T(2,128)S(1)} %copy-done.4, ...), custom_call_target="tpu_custom_call" | custom-call | tf_op jit(solution)/shard_map/pallas_call | solution.py:400
  146.2 3.6 %shard_map.154 = (bf16[65,1024]{1,0:T(8,128)(2,1)S(1)}, bf16[32,56,128]{2,1,0:T(8,128)(2,1)S(1)}) custom-call(s32[4]{0:T(128)S(1)} %pad_add_fusion.idx, f32[65,1024]{1,0:T(8,128)S(1)} %get-tuple-element.92.first, bf16[65,1024]{1,0:T(8,128)(2,1)S(1)} %shard_map.151.y0, bf16[65,1024]{1,0:T(8,128)(2,1)S(1)} %collective-permute-done.13.y1, ...), custom_call_target="tpu_custom_call" | custom-call | tf_op jit(solution)/shard_map/pallas_call | solution.py:400
  151.9 16.0 %all_to_all.22.r_own = bf16[32,56,128]{2,1,0:T(8,128)(2,1)S(1)} all-to-all(bf16[32,56,128]{2,1,0:T(8,128)(2,1)S(1)} %get-tuple-element.102), channel_id=1, replica_groups=mesh['tm'=32,'tensor'=8] {'tm'}, dimensions={0} | all-to-all | bytes 917504 | tf_op jit(solution)/shard_map/all_to_all | solution.py:455
  167.9 8.9 %collective-permute-start.23 = (bf16[32,56,128]{2,1,0:T(8,128)(2,1)S(1)}, bf16[32,56,128]{2,1,0:T(8,128)(2,1)S(1)}, u32[]{:S(2)}, u32[]{:S(2)}) collective-permute-start(bf16[32,56,128]{2,1,0:T(8,128)(2,1)S(1)} %all_to_all.22.r_own), channel_id=1, source_target_pairs={{0,1},{1,0},{2,3},{3,2},{4,5},{5,4},{6,7},{7,6},{8,9},{9,8},{10,11... | collective-permute-start | bytes 1376264 | tf_op jit(solution)/shard_map/ppermute | solution.py:443
  178.3 4.3 %shard_map.155 = bf16[32,24,128]{2,1,0:T(8,128)(2,1)S(1)} custom-call(s32[4]{0:T(128)S(1)} %pad_add_fusion.idx, s32[16]{0:T(128)S(1)} %get-tuple-element.68.order, bf16[16,2176]{1,0:T(8,128)(2,1)S(1)} %get-tuple-element.69.mask, s32[32,128]{1,0:T(8,128)S(1)} %get-tuple-element.70.part_time, bf16[32,56,128]{2,1,0:T(8,128)(2,1)S(1)} %all_to_all.22.r_own, ...), custom_call_target="tpu_custom_call" | custom-call | tf_op jit(solution)/shard_map/pallas_call | solution.py:400
  182.6 14.7 %all_to_all.23.back = bf16[32,24,128]{2,1,0:T(8,128)(2,1)S(1)} all-to-all(bf16[32,24,128]{2,1,0:T(8,128)(2,1)S(1)} %shard_map.155), channel_id=1, replica_groups=mesh['tm'=32,'tensor'=8] {'tm'}, dimensions={0} | all-to-all | bytes 393216 | tf_op jit(solution)/shard_map/all_to_all | solution.py:491
  198.8 2.6 %shard_map.156 = (f32[65,1024]{1,0:T(8,128)S(1)}, bf16[65,1024]{1,0:T(8,128)(2,1)S(1)}) custom-call(s32[4]{0:T(128)S(1)} %pad_add_fusion.idx, bf16[32,24,128]{2,1,0:T(8,128)(2,1)S(1)} %all_to_all.23.back, bf16[65,1024]{1,0:T(8,128)(2,1)S(1)} %get-tuple-element.107.own, f32[2,1024]{1,0:T(2,128)S(1)} %copy-done.7, f32[2,1024]{1,0:T(2,128)S(1)} %copy-done.8, ...), custom_call_target="tpu_custom_call" | custom-call | tf_op jit(solution)/shard_map/pallas_call | solution.py:400
  201.5 2.6 %collective-permute-start.26 = (bf16[65,1024]{1,0:T(8,128)(2,1)S(1)}, bf16[65,1024]{1,0:T(8,128)(2,1)S(1)}, u32[]{:S(2)}, u32[]{:S(2)}) collective-permute-start(bf16[65,1024]{1,0:T(8,128)(2,1)S(1)} %get-tuple-element.109.n), channel_id=1, source_target_pairs={{0,6},{1,7},{2,4},{3,5},{4,2},{5,3},{6,0},{7,1},{8,14},{9,15},{10,... | collective-permute-start | bytes 399368 | tf_op jit(solution)/shard_map/ppermute | solution.py:587
  204.1 4.2 %collective-permute-done.26.n = bf16[65,1024]{1,0:T(8,128)(2,1)S(1)} collective-permute-done((bf16[65,1024]{1,0:T(8,128)(2,1)S(1)}, bf16[65,1024]{1,0:T(8,128)(2,1)S(1)}, u32[]{:S(2)}, u32[]{:S(2)}) %collective-permute-start.26) | collective-permute-done | bytes 133152 | tf_op jit(solution)/shard_map/ppermute | solution.py:587
  208.3 3.4 %shard_map.158 = bf16[65,1024]{1,0:T(8,128)(2,1)S(1)} custom-call(bf16[65,1024]{1,0:T(8,128)(2,1)S(1)} %collective-permute-done.26.n, bf16[2,1024,512]{2,1,0:T(8,128)(2,1)} %w1_own.3, bf16[2,1024,512]{2,1,0:T(8,128)(2,1)S(1)} %collective-permute-done.6.refs_2_.refs_3_.w1_par, f32[2,512]{1,0:T(2,128)S(1)} %copy-done.4, ...), custom_call_target="tpu_custom_call" | custom-call | tf_op jit(solution)/shard_map/pallas_call | solution.py:400
  213.0 3.4 %shard_map.157.y0 = bf16[65,1024]{1,0:T(8,128)(2,1)S(1)} custom-call(bf16[65,1024]{1,0:T(8,128)(2,1)S(1)} %get-tuple-element.109.n, bf16[2,1024,512]{2,1,0:T(8,128)(2,1)} %w1_own.3, bf16[2,1024,512]{2,1,0:T(8,128)(2,1)S(1)} %collective-permute-done.6.refs_2_.refs_3_.w1_par, f32[2,512]{1,0:T(2,128)S(1)} %copy-done.4, ...), custom_call_target="tpu_custom_call" | custom-call | tf_op jit(solution)/shard_map/pallas_call | solution.py:400
  (89 shorter events, 45.2 us)
Async XLA Ops:
  0.0 11.3 %collective-permute-start.2 = (bf16[2,512,1024]{2,1,0:T(8,128)(2,1)}, bf16[2,512,1024]{2,1,0:T(8,128)(2,1)S(1)}, u32[]{:S(2)}, u32[]{:S(2)}) collective-permute-start(bf16[2,512,1024]{2,1,0:T(8,128)(2,1)} %w2_own.3), channel_id=1, source_target_pairs={{0,1},{1,0},{2,3},{3,2},{4,5},{5,4},{6,7},{7,6},{8,9},{9,8},{10,11... | collective-permute-start | bytes 6291464 | tf_op jit(solution)/shard_map/ppermute | solution.py:443
  0.7 7.8 %collective-permute-start = (bf16[2,3,1024,128]{3,2,1,0:T(8,128)(2,1)}, bf16[2,3,1024,128]{3,2,1,0:T(8,128)(2,1)}, u32[]{:S(2)}, u32[]{:S(2)}) collective-permute-start(bf16[2,3,1024,128]{3,2,1,0:T(8,128)(2,1)} %w_ref.1), channel_id=1, source_target_pairs={{0,1},{1,0},{2,3},{3,2},{4,5},{5,4},{6,7},{7,6},{8,9},{9,8},{10,11... | collective-permute-start | bytes 4718600 | tf_op jit(solution)/shard_map/ppermute | solution.py:443
  4.8 6.5 %collective-permute-start.3 = (bf16[4,1032,128]{2,1,0:T(8,128)(2,1)S(1)}, bf16[4,1032,128]{2,1,0:T(8,128)(2,1)S(1)}, u32[]{:S(2)}, u32[]{:S(2)}) collective-permute-start(bf16[4,1032,128]{2,1,0:T(8,128)(2,1)S(1)} %get-tuple-element.64.rest_0_), channel_id=1, source_target_pairs={{0,1},{1,0},{2,3},{3,2},{4,5},{5,4},{6,7},{7,6},{8,9},{9,8},{10,11... | collective-permute-start | bytes 3170312 | tf_op jit(solution)/shard_map/ppermute | solution.py:443
  40.9 58.2 %collective-permute-start.6 = (bf16[2,1024,512]{2,1,0:T(8,128)(2,1)}, bf16[2,1024,512]{2,1,0:T(8,128)(2,1)S(1)}, u32[]{:S(2)}, u32[]{:S(2)}) collective-permute-start(bf16[2,1024,512]{2,1,0:T(8,128)(2,1)} %w1_own.3), channel_id=1, source_target_pairs={{0,1},{1,0},{2,3},{3,2},{4,5},{5,4},{6,7},{7,6},{8,9},{9,8},{10,11... | collective-permute-start | bytes 6291464 | tf_op jit(solution)/shard_map/ppermute | solution.py:443
  41.3 24.8 %collective-permute-start.19 = (bf16[4,1032,128]{2,1,0:T(8,128)(2,1)S(1)}, bf16[4,1032,128]{2,1,0:T(8,128)(2,1)S(1)}, u32[]{:S(2)}, u32[]{:S(2)}) collective-permute-start(bf16[4,1032,128]{2,1,0:T(8,128)(2,1)S(1)} %get-tuple-element.64.rest_0_), channel_id=1, source_target_pairs={{0,2},{1,3},{2,4},{3,5},{4,6},{5,7},{6,0},{7,1},{8,10},{9,11},{10,... | collective-permute-start | bytes 3170312 | tf_op jit(solution)/shard_map/ppermute | solution.py:440
  42.5 26.0 %collective-permute-start.18 = (bf16[4,1032,128]{2,1,0:T(8,128)(2,1)S(1)}, bf16[4,1032,128]{2,1,0:T(8,128)(2,1)S(1)}, u32[]{:S(2)}, u32[]{:S(2)}) collective-permute-start(bf16[4,1032,128]{2,1,0:T(8,128)(2,1)S(1)} %get-tuple-element.64.rest_0_), channel_id=1, source_target_pairs={{0,4},{1,5},{2,6},{3,7},{4,0},{5,1},{6,2},{7,3},{8,12},{9,13},{10,... | collective-permute-start | bytes 3170312 | tf_op jit(solution)/shard_map/ppermute | solution.py:440
  43.3 47.2 %collective-permute-start.17 = (bf16[4,1032,128]{2,1,0:T(8,128)(2,1)S(1)}, bf16[4,1032,128]{2,1,0:T(8,128)(2,1)S(1)}, u32[]{:S(2)}, u32[]{:S(2)}) collective-permute-start(bf16[4,1032,128]{2,1,0:T(8,128)(2,1)S(1)} %get-tuple-element.64.rest_0_), channel_id=1, source_target_pairs={{0,6},{1,7},{2,0},{3,1},{4,2},{5,3},{6,4},{7,5},{8,14},{9,15},{10,... | collective-permute-start | bytes 3170312 | tf_op jit(solution)/shard_map/ppermute | solution.py:440
  45.2 53.9 %collective-permute-start.5 = (bf16[2,128,1024]{2,1,0:T(8,128)(2,1)S(1)}, bf16[2,128,1024]{2,1,0:T(8,128)(2,1)S(1)}, u32[]{:S(2)}, u32[]{:S(2)}) collective-permute-start(bf16[2,128,1024]{2,1,0:T(8,128)(2,1)S(1)} %copy-done.2), channel_id=1, source_target_pairs={{0,1},{1,0},{2,3},{3,2},{4,5},{5,4},{6,7},{7,6},{8,9},{9,8},{10,11... | collective-permute-start | bytes 1572872 | tf_op jit(solution)/shard_map/ppermute | solution.py:443
  66.0 75.8 %collective-permute-start.22 = (bf16[4,1032,128]{2,1,0:T(8,128)(2,1)S(1)}, bf16[4,1032,128]{2,1,0:T(8,128)(2,1)S(1)}, u32[]{:S(2)}, u32[]{:S(2)}) collective-permute-start(bf16[4,1032,128]{2,1,0:T(8,128)(2,1)S(1)} %collective-permute-done.19.rest_3_), channel_id=1, source_target_pairs={{0,1},{1,0},{2,3},{3,2},{4,5},{5,4},{6,7},{7,6},{8,9},{9,8},{10,11... | collective-permute-start | bytes 3170312 | tf_op jit(solution)/shard_map/ppermute | solution.py:443
  68.5 23.2 %collective-permute-start.7 = (f32[2,512]{1,0:T(2,128)S(1)}, f32[2,512]{1,0:T(2,128)S(1)}, u32[]{:S(2)}, u32[]{:S(2)}) collective-permute-start(f32[2,512]{1,0:T(2,128)S(1)} %copy-done.3), channel_id=1, source_target_pairs={{0,1},{1,0},{2,3},{3,2},{4,5},{5,4},{6,7},{7,6},{8,9},{9,8},{10,11... | collective-permute-start | bytes 12296 | tf_op jit(solution)/shard_map/ppermute | solution.py:443
  90.6 54.2 %collective-permute-start.21 = (bf16[4,1032,128]{2,1,0:T(8,128)(2,1)S(1)}, bf16[4,1032,128]{2,1,0:T(8,128)(2,1)S(1)}, u32[]{:S(2)}, u32[]{:S(2)}) collective-permute-start(bf16[4,1032,128]{2,1,0:T(8,128)(2,1)S(1)} %collective-permute-done.18.rest_2_), channel_id=1, source_target_pairs={{0,1},{1,0},{2,3},{3,2},{4,5},{5,4},{6,7},{7,6},{8,9},{9,8},{10,11... | collective-permute-start | bytes 3170312 | tf_op jit(solution)/shard_map/ppermute | solution.py:443
  91.7 53.0 %collective-permute-start.20 = (bf16[4,1032,128]{2,1,0:T(8,128)(2,1)S(1)}, bf16[4,1032,128]{2,1,0:T(8,128)(2,1)S(1)}, u32[]{:S(2)}, u32[]{:S(2)}) collective-permute-start(bf16[4,1032,128]{2,1,0:T(8,128)(2,1)S(1)} %collective-permute-done.17.rest_1_), channel_id=1, source_target_pairs={{0,1},{1,0},{2,3},{3,2},{4,5},{5,4},{6,7},{7,6},{8,9},{9,8},{10,11... | collective-permute-start | bytes 3170312 | tf_op jit(solution)/shard_map/ppermute | solution.py:443
  115.9 7.7 %collective-permute-start.9 = (bf16[65,1024]{1,0:T(8,128)(2,1)S(1)}, bf16[65,1024]{1,0:T(8,128)(2,1)S(1)}, u32[]{:S(2)}, u32[]{:S(2)}) collective-permute-start(bf16[65,1024]{1,0:T(8,128)(2,1)S(1)} %get-tuple-element.90), channel_id=1, source_target_pairs={{0,4},{1,5},{2,6},{3,7},{4,0},{5,1},{6,2},{7,3},{8,12},{9,13},{10,... | collective-permute-start | bytes 399368 | tf_op jit(solution)/shard_map/ppermute | solution.py:440
  118.9 6.8 %collective-permute-start.10 = (bf16[65,1024]{1,0:T(8,128)(2,1)S(1)}, bf16[65,1024]{1,0:T(8,128)(2,1)S(1)}, u32[]{:S(2)}, u32[]{:S(2)}) collective-permute-start(bf16[65,1024]{1,0:T(8,128)(2,1)S(1)} %get-tuple-element.91), channel_id=1, source_target_pairs={{0,6},{1,7},{2,0},{3,1},{4,2},{5,3},{6,4},{7,5},{8,14},{9,15},{10,... | collective-permute-start | bytes 399368 | tf_op jit(solution)/shard_map/ppermute | solution.py:440
  126.0 5.6 %collective-permute-start.14 = (bf16[65,1024]{1,0:T(8,128)(2,1)S(1)}, bf16[65,1024]{1,0:T(8,128)(2,1)S(1)}, u32[]{:S(2)}, u32[]{:S(2)}) collective-permute-start(bf16[65,1024]{1,0:T(8,128)(2,1)S(1)} %get-tuple-element.93.refs_0_), channel_id=1, source_target_pairs={{0,4},{1,5},{2,6},{3,7},{4,0},{5,1},{6,2},{7,3},{8,12},{9,13},{10,... | collective-permute-start | bytes 399368 | tf_op jit(solution)/shard_map/ppermute | solution.py:440
  128.3 7.8 %collective-permute-start.12 = (bf16[65,1024]{1,0:T(8,128)(2,1)S(1)}, bf16[65,1024]{1,0:T(8,128)(2,1)S(1)}, u32[]{:S(2)}, u32[]{:S(2)}) collective-permute-start(bf16[65,1024]{1,0:T(8,128)(2,1)S(1)} %get-tuple-element.93.refs_0_), channel_id=1, source_target_pairs={{0,2},{1,3},{2,4},{3,5},{4,6},{5,7},{6,0},{7,1},{8,10},{9,11},{10,... | collective-permute-start | bytes 399368 | tf_op jit(solution)/shard_map/ppermute | solution.py:440
  131.6 5.6 %collective-permute-start.11 = (bf16[65,1024]{1,0:T(8,128)(2,1)S(1)}, bf16[65,1024]{1,0:T(8,128)(2,1)S(1)}, u32[]{:S(2)}, u32[]{:S(2)}) collective-permute-start(bf16[65,1024]{1,0:T(8,128)(2,1)S(1)} %get-tuple-element.93.refs_0_), channel_id=1, source_target_pairs={{0,6},{1,7},{2,0},{3,1},{4,2},{5,3},{6,4},{7,5},{8,14},{9,15},{10,... | collective-permute-start | bytes 399368 | tf_op jit(solution)/shard_map/ppermute | solution.py:440
  136.1 8.6 %collective-permute-start.15 = (bf16[65,1024]{1,0:T(8,128)(2,1)S(1)}, bf16[65,1024]{1,0:T(8,128)(2,1)S(1)}, u32[]{:S(2)}, u32[]{:S(2)}) collective-permute-start(bf16[65,1024]{1,0:T(8,128)(2,1)S(1)} %shard_map.153), channel_id=1, source_target_pairs={{0,4},{1,5},{2,6},{3,7},{4,0},{5,1},{6,2},{7,3},{8,12},{9,13},{10,... | collective-permute-start | bytes 399368 | tf_op jit(solution)/shard_map/ppermute | solution.py:440
  139.7 5.0 %collective-permute-start.13 = (bf16[65,1024]{1,0:T(8,128)(2,1)S(1)}, bf16[65,1024]{1,0:T(8,128)(2,1)S(1)}, u32[]{:S(2)}, u32[]{:S(2)}) collective-permute-start(bf16[65,1024]{1,0:T(8,128)(2,1)S(1)} %get-tuple-element.97), channel_id=1, source_target_pairs={{0,2},{1,3},{2,4},{3,5},{4,6},{5,7},{6,0},{7,1},{8,10},{9,11},{10,... | collective-permute-start | bytes 399368 | tf_op jit(solution)/shard_map/ppermute | solution.py:440
  149.9 47.4 %collective-permute-start.24 = (bf16[2,1032,512]{2,1,0:T(8,128)(2,1)S(1)}, bf16[2,1032,512]{2,1,0:T(8,128)(2,1)S(1)}, u32[]{:S(2)}, u32[]{:S(2)}) collective-permute-start(bf16[2,1032,512]{2,1,0:T(8,128)(2,1)S(1)} %get-tuple-element.105), channel_id=1, source_target_pairs={{0,2},{1,3},{2,0},{3,1},{4,6},{5,7},{6,4},{7,5},{8,10},{9,11},{10,... | collective-permute-start | bytes 6340616 | tf_op jit(solution)/shard_map/ppermute | solution.py:587
  167.9 10.4 %collective-permute-start.23 = (bf16[32,56,128]{2,1,0:T(8,128)(2,1)S(1)}, bf16[32,56,128]{2,1,0:T(8,128)(2,1)S(1)}, u32[]{:S(2)}, u32[]{:S(2)}) collective-permute-start(bf16[32,56,128]{2,1,0:T(8,128)(2,1)S(1)} %all_to_all.22.r_own), channel_id=1, source_target_pairs={{0,1},{1,0},{2,3},{3,2},{4,5},{5,4},{6,7},{7,6},{8,9},{9,8},{10,11... | collective-permute-start | bytes 1376264 | tf_op jit(solution)/shard_map/ppermute | solution.py:443
  197.3 11.0 %collective-permute-start.25 = (bf16[2,1032,512]{2,1,0:T(8,128)(2,1)S(1)}, bf16[2,1032,512]{2,1,0:T(8,128)(2,1)S(1)}, u32[]{:S(2)}, u32[]{:S(2)}) collective-permute-start(bf16[2,1032,512]{2,1,0:T(8,128)(2,1)S(1)} %collective-permute-done.24.far), channel_id=1, source_target_pairs={{0,1},{1,0},{2,3},{3,2},{4,5},{5,4},{6,7},{7,6},{8,9},{9,8},{10,11... | collective-permute-start | bytes 6340616 | tf_op jit(solution)/shard_map/ppermute | solution.py:443
  201.5 6.8 %collective-permute-start.26 = (bf16[65,1024]{1,0:T(8,128)(2,1)S(1)}, bf16[65,1024]{1,0:T(8,128)(2,1)S(1)}, u32[]{:S(2)}, u32[]{:S(2)}) collective-permute-start(bf16[65,1024]{1,0:T(8,128)(2,1)S(1)} %get-tuple-element.109.n), channel_id=1, source_target_pairs={{0,6},{1,7},{2,4},{3,5},{4,2},{5,3},{6,0},{7,1},{8,14},{9,15},{10,... | collective-permute-start | bytes 399368 | tf_op jit(solution)/shard_map/ppermute | solution.py:587
  211.8 4.9 %collective-permute-start.27 = (bf16[65,1024]{1,0:T(8,128)(2,1)S(1)}, bf16[65,1024]{1,0:T(8,128)(2,1)S(1)}, u32[]{:S(2)}, u32[]{:S(2)}) collective-permute-start(bf16[65,1024]{1,0:T(8,128)(2,1)S(1)} %shard_map.158), channel_id=1, source_target_pairs={{0,6},{1,7},{2,4},{3,5},{4,2},{5,3},{6,0},{7,1},{8,14},{9,15},{10,... | collective-permute-start | bytes 399368 | tf_op jit(solution)/shard_map/ppermute | solution.py:587
  (22 other events, 567.4 us)
where the time goes:
time: 225 us; the launch traced here: 221 us
  blocking collectives  71.1 us (32%)
  waiting for transfers between devices  58.5 us (26%)
  starting transfers between devices  48.9 us (22%)
  Pallas kernels  42 us (19%)
    ppermute x12, waiting for transfers between devices, shift(): return lax.ppermute(array, 'tensor', pairs)  47.3 us
    all_to_all x2, blocking collectives, attention(): arrived = lax.all_to_all(message, 'tm', 0, 0, tiled=True)  41.7 us
    pallas_call x15, Pallas kernels, call(): pl.pallas_call(kernel, out_shape=out_shape, in_specs=in_specs or [SMEM] *...  40.9 us
    all_to_all x2, blocking collectives, attention(): back = lax.all_to_all(mixed, 'tm', 0, 0, tiled=True)  29.4 us
    ppermute x14, starting transfers between devices, swap(): return lax.ppermute(array, 'tensor', [(t, t ^ 1) for t in range(2 * NX)])  22.4 us
    ppermute x12, starting transfers between devices, shift(): return lax.ppermute(array, 'tensor', pairs)  20.6 us
    ppermute x14, waiting for transfers between devices, swap(): return lax.ppermute(array, 'tensor', [(t, t ^ 1) for t in range(2 * NX)])  6.73 us
    ppermute x3, starting transfers between devices, pair(): lax.ppermute(array, 'tensor', [(t, other(t // 2) * 2 + t % 2) for t in ra...  5.93 us
  transfers between devices with their start and end apart: 29, of which 13 were waited for; matrix products, arithmetic and copies ran while one was open for 0% of the time, Pallas kernels for 15%

commit v1 on v0

--- a/solution.py
+++ b/solution.py
@@ -20,7 +20,7 @@
 SCALE = 0.125 * LOG2E
 NEG = -1e30
 
-GROUPS = ((0,), (1, 3), (2,))
+GROUPS = ((1, 3), (2, 0))
 
 
 def lanes(shape):
@@ -38,15 +38,30 @@
     return off * lax.rsqrt(spread + 1e-06) * gain + bias
 
 
-def tables_kernel(frame_time, cond_count, w1_ref, b1_ref, w2_ref, order, mask, row_time, packed, bias, sems):
+def pack_kernel(w_ref, wo_ref, bias_ref, held, biases, sems):
     copies = [
-        pltpu.make_async_copy(w1_ref.at[1], packed.at[0, 0:D], sems.at[0]),
-        pltpu.make_async_copy(w2_ref.at[1, :, 0:512], packed.at[1, 0:512], sems.at[1]),
-        pltpu.make_async_copy(w2_ref.at[1, :, 512:D], packed.at[1, 512:D], sems.at[2]),
-        pltpu.make_async_copy(b1_ref, bias, sems.at[3]),
+        pltpu.make_async_copy(w_ref.at[1], held.at[0:3, 0:D, :], sems.at[0]),
+        pltpu.make_async_copy(bias_ref, biases, sems.at[1]),
     ]
+    for layer in range(LAYERS):
+        for j in range(8):
+            cols = slice(128 * j, 128 * j + 128)
+            copies.append(
+                pltpu.make_async_copy(
+                    wo_ref.at[layer, :, cols], held.at[4 - layer, cols, :], sems.at[2 + 8 * layer + j]
+                )
+            )
     for copy in copies:
         copy.start()
+    for copy in copies:
+        copy.wait()
+    for i in range(3):
+        held[i, D:HELD, :] = split_rows(biases[i, 1:2, :])
+    for i in (3, 4):
+        held[i, D:HELD, :] = jnp.zeros((8, 128), jnp.bfloat16)
+
+
+def tables_kernel(frame_time, cond_count, order, mask, row_time):
     for f in range(FRAMES):
         order[frame_time[f]] = f
     slot_time = jnp.full((FRAMES, 128), FRAMES, jnp.int32)
@@ -61,6 +76,30 @@
     for t in range(FRAMES):
         seen = jnp.where(subs((FRAMES, 128)) >= t, 0.0, NEG)
         mask[:, 128 * t + 128 : 128 * t + 256] = seen.astype(jnp.bfloat16)
+
+
+def load_kernel(planes, *refs):
+    held, (out, sems) = refs[:5], refs[5:]
+    copies = [pltpu.make_async_copy(ref.at[planes], out.at[c], sems.at[c]) for c, ref in enumerate(held)]
+    for copy in copies:
+        copy.start()
+    for copy in copies:
+        copy.wait()
+
+
+def load_far_kernel(h0, h1, h2, h3, h4, w1_ref, b1_ref, w2_ref, out, packed, bias, sems):
+    copies = [
+        pltpu.make_async_copy(ref.at[4:5], out.at[c], sems.at[4 + c])
+        for c, ref in enumerate((h0, h1, h2, h3, h4))
+    ]
+    copies += [
+        pltpu.make_async_copy(w1_ref.at[1], packed.at[0, 0:D], sems.at[0]),
+        pltpu.make_async_copy(w2_ref.at[1, :, 0:512], packed.at[1, 0:512], sems.at[1]),
+        pltpu.make_async_copy(w2_ref.at[1, :, 512:D], packed.at[1, 512:D], sems.at[2]),
+        pltpu.make_async_copy(b1_ref, bias, sems.at[3]),
+    ]
+    for copy in copies:
+        copy.start()
     for copy in copies:
         copy.wait()
     packed[0, D:HELD, :] = split_rows(bias[1:2, :])
@@ -108,30 +147,21 @@
 
 
 def start_kernel(
-    idx, x_ref, w_ref, wo_ref, bias_ref, g_ref, b_ref, rows, own, out, held, raw, wide, w, biases, norms, sems
+    idx, x_ref, w_own, w_par, b_own, b_par, g_ref, b_ref, xrows, out, raw, wide, rows, w, biases, norms, sems
 ):
     x, k = idx[0], idx[1]
-    copies = [
+    first = [
         pltpu.make_async_copy(x_ref.at[0], raw, sems.at[0]),
-        pltpu.make_async_copy(w_ref.at[0, 0], w.at[0], sems.at[1]),
-        pltpu.make_async_copy(w_ref.at[0, 1], w.at[1], sems.at[2]),
-        pltpu.make_async_copy(w_ref.at[0, 2], w.at[2], sems.at[15]),
-        pltpu.make_async_copy(bias_ref, biases, sems.at[14]),
-        pltpu.make_async_copy(w_ref.at[1], held.at[0:3, 0:D, :], sems.at[3]),
+        pltpu.make_async_copy(g_ref, norms.at[0], sems.at[1]),
+        pltpu.make_async_copy(b_ref, norms.at[1], sems.at[2]),
+        pltpu.make_async_copy(b_own, biases, sems.at[3]),
     ]
-    for j in range(8):
-        cols = slice(128 * j, 128 * j + 128)
-        copies.append(pltpu.make_async_copy(wo_ref.at[1, :, cols], held.at[3, cols, :], sems.at[4 + j]))
-    first = [
-        pltpu.make_async_copy(g_ref, norms.at[0], sems.at[12]),
-        pltpu.make_async_copy(b_ref, norms.at[1], sems.at[13]),
-    ]
-    for copy in first + copies:
+    weights = [pltpu.make_async_copy(ref.at[0], w.at[c], sems.at[4 + c]) for c, ref in enumerate((w_own, w_par))]
+    for copy in first + weights:
         copy.start()
-    copies[0].wait()
-    wide[...] = raw[...].astype(jnp.float32)
     for copy in first:
         copy.wait()
+    wide[...] = raw[...].astype(jnp.float32)
     gain, bias = norms[0, 0:1, :], norms[1, 0:1, :]
     for s in range(NX):
         chip = lax.rem(x + s, NX)
@@ -139,45 +169,25 @@
             part = from_row(wide, 64 * (2 * chip + b) + 32 * k, 2 * chip + b, 40)[:32]
             at = PAD * s + 32 * b
             rows[at : at + 32, :] = norm(part, gain, bias).astype(jnp.bfloat16)
-            if s == 0:
-                own[32 * b : 32 * b + 32, :] = part.astype(jnp.bfloat16)
+            xrows[at : at + 32, :] = part.astype(jnp.bfloat16)
         part = from_row(wide, 64 * (2 * chip + k) + 64, 2 * chip + k, 8)
-        rows[PAD * s + 64 : PAD * s + 72, :] = norm(part, gain, bias).astype(jnp.bfloat16)
-        if s == 0:
-            own[64:65, :] = part[:1].astype(jnp.bfloat16)
-    copies[4].wait()
-    heads_of(k, k, rows, w, biases, out, copies[1:4])
-    for copy in copies[5:]:
+        at = PAD * s + 64
+        rows[at : at + 8, :] = norm(part, gain, bias).astype(jnp.bfloat16)
+        xrows[at : at + 8, :] = part.astype(jnp.bfloat16)
+    for copy in weights:
         copy.wait()
-    for i in range(3):
-        held[i, D:HELD, :] = split_rows(biases[i, 1:2, :])
-    held[3, D:HELD, :] = jnp.zeros((8, 128), jnp.bfloat16)
-
-
-def heads_of(k, side, rows, w, biases, out, copies):
-    places = [(s * 8 + b * 4 + 2 * side, 72 * s + 32 * b) for s in range(NX) for b in range(2)]
-    tails = [(s * 8 + k * 4 + 2 * side, 72 * s + 64) for s in range(NX)]
-    parts = []
-    for i in range(3):
-        copies[i].wait()
-        parts.append(jnp.dot(rows[...], w[i], preferred_element_type=jnp.float32) + biases[i, 0:1, :])
-    emit(out, *parts, places, tails)
-
-
-def partner_kernel(idx, rows, w_ref, biases, other, out, w, sems):
+    both = jnp.concatenate([w[c, i] for c in range(2) for i in range(3)], axis=1)
+    both = jnp.dot(rows[...], both, preferred_element_type=jnp.float32)
+    for c, (side, row) in enumerate(((k, biases), (1 - k, b_par))):
+        places = [(s * 8 + b * 4 + 2 * side, PAD * s + 32 * b) for s in range(NX) for b in range(2)]
+        tails = [(s * 8 + k * 4 + 2 * side, PAD * s + 64) for s in range(NX)]
+        parts = [both[:, 384 * c + 128 * i : 384 * c + 128 * i + 128] + row[i, 0:1, :] for i in range(3)]
+        emit(out, *parts, places, tails)
+
+
+def turn_kernel(idx, first, y0, y1, y2, y3, o_bias, gain, bias, *rest):
+    w, *near, stream, out, rows, acc = rest
     k = idx[1]
-    copies = [pltpu.make_async_copy(w_ref.at[0, i], w.at[i], sems.at[i]) for i in range(3)]
-    for copy in copies:
-        copy.start()
-    heads_of(k, 1 - k, rows, w, biases, out, copies)
-
-
-def turn_kernel(idx, first, y0, y1, y2, y3, o_bias, gain, bias, *rest):
-    owns, pars, (stream, out, rows, w, acc, sems) = rest[:NX], rest[NX : 2 * NX], rest[2 * NX :]
-    k = idx[1]
-    copies = [pltpu.make_async_copy(owns[s].at[0:3], w.at[s], sems.at[s]) for s in range(NX)]
-    for copy in copies:
-        copy.start()
     summed = (y0[...].astype(jnp.float32) + y1[...].astype(jnp.float32)) + (
         y2[...].astype(jnp.float32) + y3[...].astype(jnp.float32)
     )
@@ -185,20 +195,19 @@
     stream[...] = new
     rows[0:65, :] = norm(new.astype(jnp.float32), gain[1:2, :], bias[1:2, :]).astype(jnp.bfloat16)
 
-    def project(c, weight):
-        for i in range(3):
-            bias_row = jnp.sum(weight[i, D:HELD, :].astype(jnp.float32), axis=0, keepdims=True)
-            acc[c, i] = jnp.dot(rows[...], weight[i, 0:D, :], preferred_element_type=jnp.float32) + bias_row
-
-    for s in range(NX):
-        project(2 * s + 1, pars[s])
-
-    def arrived(s, carry):
-        pltpu.make_async_copy(owns[0].at[0:3], w.at[s], sems.at[s]).wait()
-        project(2 * s, w.at[s])
-        return carry
-
-    lax.fori_loop(0, NX, arrived, 0)
+    def project(slots, refs):
+        weight = jnp.concatenate([ref[i, 0:D, :] for ref in refs for i in range(3)], axis=1)
+        total = jnp.dot(rows[...], weight, preferred_element_type=jnp.float32)
+        for c, (slot, ref) in enumerate(zip(slots, refs)):
+            for i in range(3):
+                row = jnp.sum(ref[i, D:HELD, :].astype(jnp.float32), axis=0, keepdims=True)
+                at = 384 * c + 128 * i
+                acc[slot, i] = total[:, at : at + 128] + row
+
+    project((3, 5), near[0:2])
+    project((7, 1), (near[2], w.at[4]))
+    project((0, 2), (w.at[0], w.at[1]))
+    project((4, 6), (w.at[2], w.at[3]))
 
     def one(c, carry):
         base = c // 2 * 4 + 2 * lax.rem(k + c, 2)
@@ -282,67 +291,60 @@
     dst[at + 64 : at + 72, :] = lo[16:24]
 
 
-def out_kernel(idx, back, w_own, w_par, p0, p1, p2, p3, left, right):
+def heads_kernel(idx, back, out):
     k = idx[1]
-    for dst, side in ((left, k), (right, 1 - k)):
+    for c, side in enumerate((k, 1 - k)):
         for s in range(NX):
             slots = [s * 8 + b * 4 + 2 * side for b in range(2)]
-            gather_heads(dst, 72 * s, back, slots, s * 8 + k * 4 + 2 * side)
-    for j in range(4):
-        cols = slice(256 * j, 256 * j + 256)
-        partial = jnp.dot(left[...], w_own[0, :, cols], preferred_element_type=jnp.float32) + jnp.dot(
-            right[...], w_par[0, :, cols], preferred_element_type=jnp.float32
-        )
-        for s, out in enumerate((p0, p1, p2, p3)):
-            out[:, cols] = partial[72 * s : 72 * s + 65].astype(jnp.bfloat16)
-
-
-def mid_kernel(layer, own, p0, p1, p2, p3, o_bias, gain, bias, first, normed):
-    rows = own[...].astype(jnp.float32)
-    summed = (p0[...].astype(jnp.float32) + p1[...].astype(jnp.float32)) + (
-        p2[...].astype(jnp.float32) + p3[...].astype(jnp.float32)
-    )
-    rows = rows + summed + o_bias[layer : layer + 1, :]
-    first[...] = rows
-    normed[...] = norm(rows, gain[layer : layer + 1, :], bias[layer : layer + 1, :]).astype(jnp.bfloat16)
+            cols = slice(128 * c, 128 * c + 128)
+            gather_heads(out.at[:, cols], PAD * s, back, slots, s * 8 + k * 4 + 2 * side)
+
+
+def blocks_of(plane):
+    return jnp.concatenate([plane[128 * j : 128 * j + 128, :] for j in range(8)], axis=1)
+
+
+def every_out_kernel(h0, h1, h2, h3, xrows, o_bias, gain, bias, *rest):
+    w, *near, first, normed, lhs = rest
+    for s, heads in enumerate((h0, h1, h2, h3)):
+        for r in range(NX):
+            at = PAD * ((r - s) % NX)
+            lhs[PAD * r : PAD * r + PAD, 256 * s : 256 * s + 256] = heads[at : at + PAD, :]
+    weight = jnp.concatenate(
+        [blocks_of(p) for s in range(NX) for p in (w.at[s, 0], near[s - 1].at[4] if s else w.at[4, 0])], axis=0
+    )
+    total = jnp.dot(lhs[...], weight, preferred_element_type=jnp.float32)
+    rows = xrows[...].astype(jnp.float32) + total + o_bias[0:1, :]
+    first[...] = rows[0:65]
+    normed[...] = norm(rows, gain[0:1, :], bias[0:1, :]).astype(jnp.bfloat16)
 
 
 def whole_out_kernel(idx, back, own, o_bias, gain, bias, *rest):
-    owns, pars, (first, normed, heads, w, sems) = rest[:NX], rest[NX : 2 * NX], rest[2 * NX :]
+    w, *near, first, normed, heads = rest
     k = idx[1]
-    copies = [pltpu.make_async_copy(owns[s].at[3, 0:D], w.at[s], sems.at[s]) for s in range(NX)]
-    for copy in copies:
-        copy.start()
-    total = None
-    for c, side in ((1, 1 - k), (0, k)):
-        for s in range(NX):
+    for s in range(NX):
+        for c, side in enumerate((k, 1 - k)):
             base = s * 4 + 2 * side
-            gather_heads(heads.at[2 * s + c], 0, back, [base, 16 + base], k * 16 + base)
-            if c == 0:
-                copies[s].wait()
-            source = w.at[s] if c == 0 else pars[s].at[3]
-            weight = jnp.concatenate([source[128 * j : 128 * j + 128, :] for j in range(8)], axis=1)
-            part = jnp.dot(heads[2 * s + c], weight, preferred_element_type=jnp.float32)
-            total = part if total is None else total + part
+            at = 256 * s + 128 * c
+            gather_heads(heads.at[:, at : at + 128], 0, back, [base, 16 + base], k * 16 + base)
+    weight = jnp.concatenate(
+        [blocks_of(p) for s in range(NX) for p in (w.at[s, 0], near[s - 1].at[3] if s else w.at[4, 0])], axis=0
+    )
+    total = jnp.dot(heads[...], weight, preferred_element_type=jnp.float32)
     rows = own[...].astype(jnp.float32) + total[:65] + o_bias[1:2, :]
     first[...] = rows
     normed[...] = norm(rows, gain[1:2, :], bias[1:2, :]).astype(jnp.bfloat16)
 
 
-def mlp_kernel(layer, count, *refs):
-    blocks, (w1_own, w1_par, b1_own, b1_par, w2_own, w2_par), outs, rows = (
-        refs[:count],
-        refs[count : count + 6],
-        refs[count + 6 : 2 * count + 6],
-        refs[-1],
-    )
-    for c, n in enumerate(blocks):
-        rows[PAD * c : PAD * c + 65, :] = n[...]
+def mlp_kernel(group, n, w1_own, w1_par, b1_own, b1_par, w2_own, w2_par, *rest):
+    outs, rows = rest[:-1], rest[-1]
+    for c, s in enumerate(group):
+        rows[PAD * c : PAD * c + PAD, :] = n[PAD * s : PAD * s + PAD, :]
     total = None
     for w1, b1, w2 in ((w1_own, b1_own, w2_own), (w1_par, b1_par, w2_par)):
-        inner = jnp.dot(rows[...], w1[layer], preferred_element_type=jnp.float32) + b1[layer : layer + 1, :]
+        inner = jnp.dot(rows[...], w1[0], preferred_element_type=jnp.float32) + b1[0:1, :]
         inner = (0.5 * inner * (1.0 + lax.erf(inner * 0.7071067811865476))).astype(jnp.bfloat16)
-        part = jnp.dot(inner, w2[layer], preferred_element_type=jnp.float32)
+        part = jnp.dot(inner, w2[0], preferred_element_type=jnp.float32)
         total = part if total is None else total + part
     for c, y in enumerate(outs):
         y[...] = total[PAD * c : PAD * c + 65].astype(jnp.bfloat16)
@@ -406,12 +408,6 @@
         input_output_aliases=aliases or {},
         compiler_params=pltpu.CompilerParams(vmem_limit_bytes=limit << 20),
     )(*args)
-
-
-def of_layer(layer, array):
-    rest = array.shape[1:]
-    zeros = (0,) * len(rest)
-    return pl.BlockSpec((1, *rest), lambda i: (layer, *zeros))
 
 
 def shards(
@@ -449,29 +445,15 @@
         return [parts[0]] + [shift(parts[s], s) for s in (1, 2, 3)]
 
     tie = lax.optimization_barrier
+
     seen = []
 
-    def attention(layer, message, *late):
+    def attention(layer, message, beside, *late):
         arrived = lax.all_to_all(message, "tm", 0, 0, tiled=True)
         arrived, *late = tie((arrived, *late))
         arrived_par = swap(arrived)
-        if layer == 0:
-            seen.extend(
-                call(
-                    tables_kernel,
-                    (frame_time, cond_count, *in_hbm(fc1_weight, fc1_bias, fc2_weight)),
-                    [
-                        jax.ShapeDtypeStruct((FRAMES,), jnp.int32),
-                        jax.ShapeDtypeStruct((FRAMES, KEYS), jnp.bfloat16),
-                        jax.ShapeDtypeStruct((PARTS, 128), jnp.int32),
-                        jax.ShapeDtypeStruct((2, HELD, 512), jnp.bfloat16),
-                    ],
-                    [pltpu.VMEM((LAYERS, 512), jnp.float32), pltpu.SemaphoreType.DMA((4,))],
-                    in_specs=[SMEM] * 2 + [HBM] * 3,
-                    out_specs=[SMEM, VMEM, VMEM, VMEM],
-                )
-            )
-        order, mask, row_time, _ = seen
+        seen.append(beside())
+        order, mask, row_time = seen[0]
         arrived, arrived_par, *late = tie((arrived, arrived_par, *late))
         late = [swap(a) for a in late]
         mixed = call(
@@ -493,19 +475,6 @@
 
     message_shape = jax.ShapeDtypeStruct((PARTS, 56, 128), jnp.bfloat16)
 
-    def mlp(layer, blocks):
-        outs = {}
-        for group in GROUPS:
-            done = call(
-                functools.partial(mlp_kernel, layer, len(group)),
-                (*(blocks[s] for s in group), *(fc1_weight, fc1_par, fc1_bias, fc1_bias_par, fc2_weight, fc2_par)),
-                [block()] * len(group),
-                [pltpu.VMEM((PAD * len(group), D), jnp.bfloat16)],
-                scalars=0,
-            )
-            outs.update(zip(group, done))
-        return [outs[s] for s in range(NX)]
-
     def in_hbm(*arrays):
         return [pltpu.with_memory_space_constraint(a, pltpu.HBM) for a in arrays]
 
@@ -514,92 +483,107 @@
     biases_par = swap(biases)
     fc2_par = swap(fc2_weight)
     idx = jnp.stack([x, k, k == (part // 4) % 2, k == part // 16]).astype(jnp.int32)
-    rows, stream, message, held = call(
+    held = call(
+        pack_kernel,
+        in_hbm(qkv_weight, out_weight, biases),
+        jax.ShapeDtypeStruct((5, HELD, 128), jnp.bfloat16),
+        [pltpu.VMEM((3, LAYERS, 128), jnp.float32), pltpu.SemaphoreType.DMA((18,))],
+        in_specs=[HBM] * 3,
+    )
+    helds = spread(held)
+    held_par = swap(held)
+    xrows, message = call(
         start_kernel,
-        (idx, *in_hbm(frames_in, qkv_weight, out_weight, biases, ln1_gain, ln1_bias)),
-        [
-            block(rows=NX * PAD),
-            block(),
-            message_shape,
-            jax.ShapeDtypeStruct((4, HELD, 128), jnp.bfloat16),
-        ],
+        (idx, *in_hbm(frames_in, qkv_weight, qkv_par, biases), biases_par, *in_hbm(ln1_gain, ln1_bias)),
+        [block(rows=NX * PAD), message_shape],
         [
             pltpu.VMEM((8 * BLOCK, D), jnp.bfloat16),
             pltpu.VMEM((8 * BLOCK, D), jnp.float32),
-            pltpu.VMEM((3, D, 128), jnp.bfloat16),
-            pltpu.VMEM((3, 2, 128), jnp.float32),
+            pltpu.VMEM((NX * PAD, D), jnp.bfloat16),
+            pltpu.VMEM((2, 3, D, 128), jnp.bfloat16),
+            pltpu.VMEM((3, LAYERS, 128), jnp.float32),
             pltpu.VMEM((2, LAYERS, D), jnp.float32),
-            pltpu.SemaphoreType.DMA((16,)),
+            pltpu.SemaphoreType.DMA((6,)),
         ],
-        in_specs=[SMEM] + [HBM] * 6,
-    )
-    helds = spread(held)
-    held_par = swap(held)
-    qkv_par, biases_par, message = tie((qkv_par, biases_par, message))
-    message = call(
-        partner_kernel,
-        (idx, rows, *in_hbm(qkv_par), biases_par, message),
-        message_shape,
-        [pltpu.VMEM((3, D, 128), jnp.bfloat16), pltpu.SemaphoreType.DMA((3,))],
-        in_specs=[SMEM, VMEM, HBM, VMEM, VMEM],
-        aliases={4: 0},
-    )
-    message, fc2_par, held_par, idx, frame_time, cond_count = tie(
-        (message, fc2_par, held_par, idx, frame_time, cond_count)
-    )
-    back, out_par, fc1_par, fc1_bias_par = attention(0, message, out_weight, fc1_weight, fc1_bias)
-    partial = pl.pallas_call(
-        out_kernel,
-        grid=(1,),
-        out_shape=[block()] * 4,
-        in_specs=[SMEM, VMEM, of_layer(0, out_weight), of_layer(0, out_par)],
-        out_specs=[VMEM] * 4,
-        scratch_shapes=[pltpu.VMEM((NX * PAD, 128), jnp.bfloat16)] * 2,
-        compiler_params=pltpu.CompilerParams(vmem_limit_bytes=12 << 20),
-    )(idx, back, out_weight, out_par)
+        in_specs=[SMEM, HBM, HBM, HBM, HBM, VMEM, HBM, HBM],
+        limit=12,
+    )
+    message, fc2_par, held_par = tie((message, fc2_par, held_par))
+
+    def tables():
+        return call(
+            tables_kernel,
+            (frame_time, cond_count),
+            [
+                jax.ShapeDtypeStruct((FRAMES,), jnp.int32),
+                jax.ShapeDtypeStruct((FRAMES, KEYS), jnp.bfloat16),
+                jax.ShapeDtypeStruct((PARTS, 128), jnp.int32),
+            ],
+            scalars=2,
+            out_specs=[SMEM, VMEM, VMEM],
+        )
+
+    def load(planes, count, rows):
+        return call(
+            functools.partial(load_kernel, planes),
+            far_refs,
+            jax.ShapeDtypeStruct((5, count, rows, 128), jnp.bfloat16),
+            [pltpu.SemaphoreType.DMA((5,))],
+            in_specs=[HBM] * 5,
+        )
+
+    back, fc1_par, fc1_bias_par = attention(0, message, tables, fc1_weight, fc1_bias)
+    heads = call(heads_kernel, (idx, back), jax.ShapeDtypeStruct((NX * PAD, 256), jnp.bfloat16))
+    heads = spread(heads)
+    held_pars = [held_par] + [swap(helds[s]) for s in (1, 2, 3)]
+    far_refs = in_hbm(*helds, held_pars[0])
+    near = held_pars[1:]
+    loaded, packed = call(
+        load_far_kernel,
+        (*far_refs, *in_hbm(fc1_weight, fc1_bias, fc2_weight)),
+        [jax.ShapeDtypeStruct((5, 1, HELD, 128), jnp.bfloat16), jax.ShapeDtypeStruct((2, HELD, 512), jnp.bfloat16)],
+        [pltpu.VMEM((LAYERS, 512), jnp.float32), pltpu.SemaphoreType.DMA((9,))],
+        in_specs=[HBM] * 8,
+    )
+    first, normed_two = call(
+        every_out_kernel,
+        (*heads, xrows, out_bias, ln2_gain, ln2_bias, loaded, *near),
+        [block(jnp.float32), block(rows=NX * PAD)],
+        [pltpu.VMEM((NX * PAD, D), jnp.bfloat16)],
+        scalars=0,
+    )
+    partial = {}
+    for group in GROUPS:
+        done = call(
+            functools.partial(mlp_kernel, group),
+            (normed_two, fc1_weight, fc1_par, fc1_bias, fc1_bias_par, fc2_weight, fc2_par),
+            [block()] * len(group),
+            [pltpu.VMEM((PAD * len(group), D), jnp.bfloat16)],
+            scalars=0,
+        )
+        partial.update(zip(group, done))
+    loaded = load(slice(0, 3), 3, HELD)
     partial = collect(partial)
-    first, normed_two = call(
-        functools.partial(mid_kernel, 0),
-        (stream, *partial, out_bias, ln2_gain, ln2_bias),
-        [block(jnp.float32), block()],
-        scalars=0,
-    )
-    partial = mlp(0, spread(normed_two))
-    partial = collect(partial)
-    held_pars = [held_par] + [swap(helds[s]) for s in (1, 2, 3)]
-    everything = (*in_hbm(*helds), *held_pars)
     stream, message = call(
         turn_kernel,
-        (idx, first, *partial, fc2_bias, ln1_gain, ln1_bias, *everything),
+        (idx, first, *partial, fc2_bias, ln1_gain, ln1_bias, loaded, *near),
         [block(), message_shape],
-        [
-            pltpu.VMEM((PAD, D), jnp.bfloat16),
-            pltpu.VMEM((NX, 3, HELD, 128), jnp.bfloat16),
-            pltpu.VMEM((2 * NX, 3, PAD, 128), jnp.float32),
-            pltpu.SemaphoreType.DMA((NX,)),
-        ],
-        in_specs=[SMEM] + [VMEM] * 8 + [HBM] * 4 + [VMEM] * 4,
-        limit=14,
-    )
-    message, packed = tie((message, seen[3]))
+        [pltpu.VMEM((PAD, D), jnp.bfloat16), pltpu.VMEM((2 * NX, 3, PAD, 128), jnp.float32)],
+    )
+    message, packed = tie((message, packed))
 
     def pair(array, other):
         return lax.ppermute(array, "tensor", [(t, other(t // 2) * 2 + t % 2) for t in range(2 * NX)])
 
     far = pair(packed, lambda c: c ^ 1)
-    (back,) = attention(1, message)
-    back, far = tie((back, far))
+    (back,) = attention(1, message, lambda: load(slice(3, 4), 1, HELD))
+    back, far, loaded = tie((back, far, seen[1]))
     far_par = swap(far)
     first, normed_two = call(
         whole_out_kernel,
-        (idx, back, stream, out_bias, ln2_gain, ln2_bias, *everything),
+        (idx, back, stream, out_bias, ln2_gain, ln2_bias, loaded, *near),
         [block(jnp.float32), block()],
-        [
-            pltpu.VMEM((2 * NX, PAD, 128), jnp.bfloat16),
-            pltpu.VMEM((NX, D, 128), jnp.bfloat16),
-            pltpu.SemaphoreType.DMA((NX,)),
-        ],
-        in_specs=[SMEM] + [VMEM] * 5 + [HBM] * 4 + [VMEM] * 4,
+        [pltpu.VMEM((PAD, D), jnp.bfloat16)],
     )
     weights = (fc1_weight, fc1_par, fc1_bias, fc1_bias_par, fc2_weight, fc2_par, far, far_par)
     partial = []

time: 225 us -> 232 us (1.031)
  waiting for transfers between devices: 58.5 us -> 80.6 us
  blocking collectives: 71.1 us -> 59 us
  starting transfers between devices: 48.9 us -> 37.3 us
  local copies, waits for them, and re-layouts: 0.08 us -> 7.11 us
    all_to_all x2 -> x1, blocking collectives: 29.4 us -> 14.7 us  [attention(): back = lax.all_to_all(mixed, 'tm', 0, 0, tiled=True)]
    ppermute x12 -> x9, waiting for transfers between devices: 47.3 us -> 58.4 us  [shift(): return lax.ppermute(array, 'tensor', pairs)]
    all_to_all x0 -> x1, waiting for transfers between devices: none -> 8.23 us  [attention(): back = lax.all_to_all(mixed, 'tm', 0, 0, tiled=True)]
    unnamed x34 -> x62, local copies, waits for them, and re-layouts: 0.08 us -> 7.11 us
    ppermute x14 -> x13, starting transfers between devices: 22.4 us -> 15.9 us  [swap(): return lax.ppermute(array, 'tensor', [(t, t ^ 1) for t in range(2 * NX)])]
    ppermute x12 -> x9, starting transfers between devices: 20.6 us -> 14.2 us  [shift(): return lax.ppermute(array, 'tensor', pairs)]
    all_to_all x0 -> x1, starting transfers between devices: none -> 4.36 us  [attention(): back = lax.all_to_all(mixed, 'tm', 0, 0, tiled=True)]
    ppermute x3, starting transfers between devices: 5.93 us -> 2.86 us  [pair(): lax.ppermute(array, 'tensor', [(t, other(t // 2) * 2 + t % 2) for t in ra...]
  transfers between devices with their start and end apart: 29 -> 26, of which waited for: 13 -> 10; matrix products, arithmetic and copies ran while one was open for 0% -> 0% of each run, Pallas kernels for 15% -> 13%
where the time goes in v1:
time: 232 us; the launch traced here: 228 us
  waiting for transfers between devices  80.6 us (35%)
  blocking collectives  59 us (25%)
  Pallas kernels  43.4 us (19%)
  starting transfers between devices  37.3 us (16%)
  local copies, waits for them, and re-layouts  7.11 us (3%)
    ppermute x9, waiting for transfers between devices, shift(): return lax.ppermute(array, 'tensor', pairs)  58.4 us
    all_to_all x2, blocking collectives, attention(): arrived = lax.all_to_all(message, 'tm', 0, 0, tiled=True)  44.4 us
    pallas_call x18, Pallas kernels, call(): pl.pallas_call(kernel, out_shape=out_shape, in_specs=in_specs or [SMEM] *...  43.4 us
    ppermute x13, starting transfers between devices, swap(): return lax.ppermute(array, 'tensor', [(t, t ^ 1) for t in range(2 * NX)])  15.9 us
    all_to_all x1, blocking collectives, attention(): back = lax.all_to_all(mixed, 'tm', 0, 0, tiled=True)  14.7 us
    ppermute x9, starting transfers between devices, shift(): return lax.ppermute(array, 'tensor', pairs)  14.2 us
    ppermute x13, waiting for transfers between devices, swap(): return lax.ppermute(array, 'tensor', [(t, t ^ 1) for t in range(2 * NX)])  8.44 us
    all_to_all x1, waiting for transfers between devices, attention(): back = lax.all_to_all(mixed, 'tm', 0, 0, tiled=True)  8.23 us
  transfers between devices with their start and end apart: 26, of which 10 were waited for; matrix products, arithmetic and copies ran while one was open for 0% of the time, Pallas kernels for 13%

profile of v1, /device:TPU:35, one launch (start us, length us, event | category | flops | bytes accessed | tf_op | source)
XLA Modules:
  0.0 227.9 jit_solution(18389624596397460485)
XLA Ops:
  2.9 6.1 %collective-permute-done.1.b_par = f32[3,2,128]{2,1,0:T(2,128)S(1)} collective-permute-done((f32[3,2,128]{2,1,0:T(2,128)S(1)}, f32[3,2,128]{2,1,0:T(2,128)S(1)}, u32[]{:S(2)}, u32[]{:S(2)}) %collective-permute-start.1) | collective-permute-done | bytes 3104 | tf_op jit(solution)/shard_map/ppermute | solution.py:439
  8.9 3.4 %shard_map.146 = (bf16[288,1024]{1,0:T(8,128)(2,1)S(1)}, bf16[32,56,128]{2,1,0:T(8,128)(2,1)S(1)}) custom-call(s32[4]{0:T(128)S(1)} %pad_add_fusion.idx, bf16[1,520,1024]{2,1,0:T(8,128)(2,1)} %x_ref.1, bf16[2,3,1024,128]{3,2,1,0:T(8,128)(2,1)} %w_ref.1, bf16[2,3,1024,128]{3,2,1,0:T(8,128)(2,1)} %collective-permute-done.w_par, f32[3,2,128]{2,1,0:T(2,128)} %bitcast.6, ...), custom_call_target="tpu_custom_call" | custom-call | tf_op jit(solution)/shard_map/pallas_call | solution.py:402
  12.3 25.7 %all_to_all.20.r_own = bf16[32,56,128]{2,1,0:T(8,128)(2,1)S(1)} all-to-all(bf16[32,56,128]{2,1,0:T(8,128)(2,1)S(1)} %get-tuple-element.51), channel_id=1, replica_groups=mesh['tm'=32,'tensor'=8] {'tm'}, dimensions={0} | all-to-all | bytes 917504 | tf_op jit(solution)/shard_map/all_to_all | solution.py:452
  38.0 2.4 %collective-permute-start.4 = (bf16[32,56,128]{2,1,0:T(8,128)(2,1)S(1)}, bf16[32,56,128]{2,1,0:T(8,128)(2,1)S(1)}, u32[]{:S(2)}, u32[]{:S(2)}) collective-permute-start(bf16[32,56,128]{2,1,0:T(8,128)(2,1)S(1)} %all_to_all.20.r_own), channel_id=1, source_target_pairs={{0,1},{1,0},{2,3},{3,2},{4,5},{5,4},{6,7},{7,6},{8,9},{9,8},{10,11... | collective-permute-start | bytes 1376264 | tf_op jit(solution)/shard_map/ppermute | solution.py:439
  45.2 25.8 %collective-permute-done.10.h1.refs_1_ = bf16[5,1032,128]{2,1,0:T(8,128)(2,1)S(1)} collective-permute-done((bf16[5,1032,128]{2,1,0:T(8,128)(2,1)S(1)}, bf16[5,1032,128]{2,1,0:T(8,128)(2,1)S(1)}, u32[]{:S(2)}, u32[]{:S(2)}) %collective-permute-start.10) | collective-permute-done | bytes 1320992 | tf_op jit(solution)/shard_map/ppermute | solution.py:436
  71.9 28.4 %collective-permute-done.11.h2.refs_2_ = bf16[5,1032,128]{2,1,0:T(8,128)(2,1)S(1)} collective-permute-done((bf16[5,1032,128]{2,1,0:T(8,128)(2,1)S(1)}, bf16[5,1032,128]{2,1,0:T(8,128)(2,1)S(1)}, u32[]{:S(2)}, u32[]{:S(2)}) %collective-permute-start.11) | collective-permute-done | bytes 1320992 | tf_op jit(solution)/shard_map/ppermute | solution.py:436
  103.5 4.3 %shard_map.148 = bf16[32,24,128]{2,1,0:T(8,128)(2,1)S(1)} custom-call(s32[4]{0:T(128)S(1)} %pad_add_fusion.idx, s32[16]{0:T(128)S(1)} %get-tuple-element.47.order, bf16[16,2176]{1,0:T(8,128)(2,1)S(1)} %get-tuple-element.48.mask, s32[32,128]{1,0:T(8,128)S(1)} %get-tuple-element.49.part_time, bf16[32,56,128]{2,1,0:T(8,128)(2,1)S(1)} %all_to_all.20.r_own, ...), custom_call_target="tpu_custom_call" | custom-call | tf_op jit(solution)/shard_map/pallas_call | solution.py:402
  107.8 14.7 %all_to_all.21.back = bf16[32,24,128]{2,1,0:T(8,128)(2,1)S(1)} all-to-all(bf16[32,24,128]{2,1,0:T(8,128)(2,1)S(1)} %shard_map.148), channel_id=1, replica_groups=mesh['tm'=32,'tensor'=8] {'tm'}, dimensions={0} | all-to-all | bytes 393216 | tf_op jit(solution)/shard_map/all_to_all | solution.py:473
  123.2 2.5 %collective-permute-start.7 = (bf16[288,256]{1,0:T(8,128)(2,1)S(1)}, bf16[288,256]{1,0:T(8,128)(2,1)S(1)}, u32[]{:S(2)}, u32[]{:S(2)}) collective-permute-start(bf16[288,256]{1,0:T(8,128)(2,1)S(1)} %shard_map.149.h0), channel_id=1, source_target_pairs={{0,6},{1,7},{2,0},{3,1},{4,2},{5,3},{6,4},{7,5},{8,14},{9,15},{10,... | collective-permute-start | bytes 442376 | tf_op jit(solution)/shard_map/ppermute | solution.py:436
  127.4 3.4 %shard_map.150 = (bf16[5,1,1032,128]{3,2,1,0:T(8,128)(2,1)S(1)}, bf16[2,1032,512]{2,1,0:T(8,128)(2,1)}) custom-call(bf16[5,1032,128]{2,1,0:T(8,128)(2,1)} %copy-done.6, bf16[5,1032,128]{2,1,0:T(8,128)(2,1)} %copy-done.27, bf16[5,1032,128]{2,1,0:T(8,128)(2,1)} %copy-done.28, bf16[5,1032,128]{2,1,0:T(8,128)(2,1)} %copy-done.29, ...), custom_call_target="tpu_custom_call" | custom-call | tf_op jit(solution)/shard_map/pallas_call | solution.py:402
  134.0 2.5 %shard_map.153 = (bf16[65,1024]{1,0:T(8,128)(2,1)S(1)}, bf16[65,1024]{1,0:T(8,128)(2,1)S(1)}) custom-call(bf16[288,1024]{1,0:T(8,128)(2,1)S(1)} %get-tuple-element.67.n, bf16[2,1024,512]{2,1,0:T(8,128)(2,1)S(1)} %copy-done.1, bf16[2,1024,512]{2,1,0:T(8,128)(2,1)S(1)} %collective-permute-done.5.w1_par, f32[2,512]{1,0:T(2,128)S(1)} %copy-done.18, ...), custom_call_target="tpu_custom_call" | custom-call | tf_op jit(solution)/shard_map/pallas_call | solution.py:402
  136.5 2.5 %shard_map.152 = (bf16[65,1024]{1,0:T(8,128)(2,1)S(1)}, bf16[65,1024]{1,0:T(8,128)(2,1)S(1)}) custom-call(bf16[288,1024]{1,0:T(8,128)(2,1)S(1)} %get-tuple-element.67.n, bf16[2,1024,512]{2,1,0:T(8,128)(2,1)S(1)} %copy-done.1, bf16[2,1024,512]{2,1,0:T(8,128)(2,1)S(1)} %collective-permute-done.5.w1_par, f32[2,512]{1,0:T(2,128)S(1)} %copy-done.18, ...), custom_call_target="tpu_custom_call" | custom-call | tf_op jit(solution)/shard_map/pallas_call | solution.py:402
  139.0 2.3 collective-permute-start.16
  147.3 3.3 %collective-permute-done.17.y2 = bf16[65,1024]{1,0:T(8,128)(2,1)S(1)} collective-permute-done((bf16[65,1024]{1,0:T(8,128)(2,1)S(1)}, bf16[65,1024]{1,0:T(8,128)(2,1)S(1)}, u32[]{:S(2)}, u32[]{:S(2)}) %collective-permute-start.17) | collective-permute-done | bytes 133152 | tf_op jit(solution)/shard_map/ppermute | solution.py:436
  150.6 2.7 %shard_map.155 = (bf16[65,1024]{1,0:T(8,128)(2,1)S(1)}, bf16[32,56,128]{2,1,0:T(8,128)(2,1)S(1)}) custom-call(s32[4]{0:T(128)S(1)} %pad_add_fusion.idx, f32[65,1024]{1,0:T(8,128)S(1)} %get-tuple-element.66.first, bf16[65,1024]{1,0:T(8,128)(2,1)S(1)} %get-tuple-element.71.y0, bf16[65,1024]{1,0:T(8,128)(2,1)S(1)} %collective-permute-done.16.y1, ...), custom_call_target="tpu_custom_call" | custom-call | tf_op jit(solution)/shard_map/pallas_call | solution.py:402
  154.6 18.7 %all_to_all.22.r_own = bf16[32,56,128]{2,1,0:T(8,128)(2,1)S(1)} all-to-all(bf16[32,56,128]{2,1,0:T(8,128)(2,1)S(1)} %get-tuple-element.77), channel_id=1, replica_groups=mesh['tm'=32,'tensor'=8] {'tm'}, dimensions={0} | all-to-all | bytes 917504 | tf_op jit(solution)/shard_map/all_to_all | solution.py:452
  173.3 3.5 %collective-permute-start.19 = (bf16[32,56,128]{2,1,0:T(8,128)(2,1)S(1)}, bf16[32,56,128]{2,1,0:T(8,128)(2,1)S(1)}, u32[]{:S(2)}, u32[]{:S(2)}) collective-permute-start(bf16[32,56,128]{2,1,0:T(8,128)(2,1)S(1)} %all_to_all.22.r_own), channel_id=1, source_target_pairs={{0,1},{1,0},{2,3},{3,2},{4,5},{5,4},{6,7},{7,6},{8,9},{9,8},{10,11... | collective-permute-start | bytes 1376264 | tf_op jit(solution)/shard_map/ppermute | solution.py:439
  178.3 5.0 %shard_map.156 = bf16[32,24,128]{2,1,0:T(8,128)(2,1)} custom-call(s32[4]{0:T(128)S(1)} %pad_add_fusion.idx, s32[16]{0:T(128)S(1)} %get-tuple-element.47.order, bf16[16,2176]{1,0:T(8,128)(2,1)S(1)} %get-tuple-element.48.mask, s32[32,128]{1,0:T(8,128)S(1)} %get-tuple-element.49.part_time, bf16[32,56,128]{2,1,0:T(8,128)(2,1)S(1)} %all_to_all.22.r_own, ...), custom_call_target="tpu_custom_call" | custom-call | tf_op jit(solution)/shard_map/pallas_call | solution.py:402
  183.2 4.4 %all-to-all-start.3 = ((bf16[32,24,128]{2,1,0:T(8,128)(2,1)}), bf16[32,24,128]{2,1,0:T(8,128)(2,1)}, u32[]{:S(2)}, u32[]{:S(2)}) async-start(bf16[32,24,128]{2,1,0:T(8,128)(2,1)} %shard_map.156), calls=%async_computation.3 | async-start | bytes 393216 | tf_op jit(solution)/shard_map/all_to_all | solution.py:473
  190.1 8.2 %all-to-all-done.3.back = bf16[32,24,128]{2,1,0:T(8,128)(2,1)} async-done(((bf16[32,24,128]{2,1,0:T(8,128)(2,1)}), bf16[32,24,128]{2,1,0:T(8,128)(2,1)}, u32[]{:S(2)}, u32[]{:S(2)}) %all-to-all-start.3) | async-done | bytes 196640 | tf_op jit(solution)/shard_map/all_to_all | solution.py:473
  199.2 3.2 %collective-permute-start.21 = (bf16[2,1032,512]{2,1,0:T(8,128)(2,1)}, bf16[2,1032,512]{2,1,0:T(8,128)(2,1)S(1)}, u32[]{:S(2)}, u32[]{:S(2)}) collective-permute-start(bf16[2,1032,512]{2,1,0:T(8,128)(2,1)} %collective-permute-done.20.far), channel_id=1, source_target_pairs={{0,1},{1,0},{2,3},{3,2},{4,5},{5,4},{6,7},{7,6},{8,9},{9,8},{10,11... | collective-permute-start | bytes 6340616 | tf_op jit(solution)/shard_map/ppermute | solution.py:439
  210.0 4.7 %collective-permute-done.22.n = bf16[65,1024]{1,0:T(8,128)(2,1)S(1)} collective-permute-done((bf16[65,1024]{1,0:T(8,128)(2,1)S(1)}, bf16[65,1024]{1,0:T(8,128)(2,1)S(1)}, u32[]{:S(2)}, u32[]{:S(2)}) %collective-permute-start.22) | collective-permute-done | bytes 133152 | tf_op jit(solution)/shard_map/ppermute | solution.py:576
  214.7 4.1 %shard_map.160 = bf16[65,1024]{1,0:T(8,128)(2,1)S(1)} custom-call(bf16[65,1024]{1,0:T(8,128)(2,1)S(1)} %collective-permute-done.22.n, bf16[2,1024,512]{2,1,0:T(8,128)(2,1)S(1)} %copy-done.1, bf16[2,1024,512]{2,1,0:T(8,128)(2,1)S(1)} %copy-done.5, f32[2,512]{1,0:T(2,128)S(1)} %copy-done.18, f32[2,512]{1,0:T(2,128)S(1)} %collective-permute-done.6.b1_par, ...), custom_call_target="tpu_custom_call" | custom-call | tf_op jit(solution)/shard_map/pallas_call | solution.py:402
  219.5 4.1 %shard_map.159.y0 = bf16[65,1024]{1,0:T(8,128)(2,1)S(1)} custom-call(bf16[65,1024]{1,0:T(8,128)(2,1)S(1)} %get-tuple-element.85.n, bf16[2,1024,512]{2,1,0:T(8,128)(2,1)S(1)} %copy-done.1, bf16[2,1024,512]{2,1,0:T(8,128)(2,1)S(1)} %copy-done.5, f32[2,512]{1,0:T(2,128)S(1)} %copy-done.18, f32[2,512]{1,0:T(2,128)S(1)} %collective-permute-done.6.b1_par, ...), custom_call_target="tpu_custom_call" | custom-call | tf_op jit(solution)/shard_map/pallas_call | solution.py:402
  (112 shorter events, 41.8 us)
Async XLA Ops:
  0.0 12.3 %collective-permute-start.2 = (bf16[2,512,1024]{2,1,0:T(8,128)(2,1)}, bf16[2,512,1024]{2,1,0:T(8,128)(2,1)}, u32[]{:S(2)}, u32[]{:S(2)}) collective-permute-start(bf16[2,512,1024]{2,1,0:T(8,128)(2,1)} %w2_own.7), channel_id=1, source_target_pairs={{0,1},{1,0},{2,3},{3,2},{4,5},{5,4},{6,7},{7,6},{8,9},{9,8},{10,11... | collective-permute-start | bytes 6291464 | tf_op jit(solution)/shard_map/ppermute | solution.py:439
  0.7 8.3 %collective-permute-start = (bf16[2,3,1024,128]{3,2,1,0:T(8,128)(2,1)}, bf16[2,3,1024,128]{3,2,1,0:T(8,128)(2,1)}, u32[]{:S(2)}, u32[]{:S(2)}) collective-permute-start(bf16[2,3,1024,128]{3,2,1,0:T(8,128)(2,1)} %w_ref.1), channel_id=1, source_target_pairs={{0,1},{1,0},{2,3},{3,2},{4,5},{5,4},{6,7},{7,6},{8,9},{9,8},{10,11... | collective-permute-start | bytes 4718600 | tf_op jit(solution)/shard_map/ppermute | solution.py:439
  2.1 10.2 %collective-permute-start.3 = (bf16[5,1032,128]{2,1,0:T(8,128)(2,1)S(1)}, bf16[5,1032,128]{2,1,0:T(8,128)(2,1)}, u32[]{:S(2)}, u32[]{:S(2)}) collective-permute-start(bf16[5,1032,128]{2,1,0:T(8,128)(2,1)S(1)} %shard_map.147.h0.refs_0_), channel_id=1, source_target_pairs={{0,1},{1,0},{2,3},{3,2},{4,5},{5,4},{6,7},{7,6},{8,9},{9,8},{10,11... | collective-permute-start | bytes 3962888 | tf_op jit(solution)/shard_map/ppermute | solution.py:439
  2.7 6.3 %collective-permute-start.1 = (f32[3,2,128]{2,1,0:T(2,128)S(1)}, f32[3,2,128]{2,1,0:T(2,128)S(1)}, u32[]{:S(2)}, u32[]{:S(2)}) collective-permute-start(f32[3,2,128]{2,1,0:T(2,128)S(1)} %bitcast.7), channel_id=1, source_target_pairs={{0,1},{1,0},{2,3},{3,2},{4,5},{5,4},{6,7},{7,6},{8,9},{9,8},{10,11... | collective-permute-start | bytes 9224 | tf_op jit(solution)/shard_map/ppermute | solution.py:439
  38.0 6.4 %collective-permute-start.4 = (bf16[32,56,128]{2,1,0:T(8,128)(2,1)S(1)}, bf16[32,56,128]{2,1,0:T(8,128)(2,1)S(1)}, u32[]{:S(2)}, u32[]{:S(2)}) collective-permute-start(bf16[32,56,128]{2,1,0:T(8,128)(2,1)S(1)} %all_to_all.20.r_own), channel_id=1, source_target_pairs={{0,1},{1,0},{2,3},{3,2},{4,5},{5,4},{6,7},{7,6},{8,9},{9,8},{10,11... | collective-permute-start | bytes 1376264 | tf_op jit(solution)/shard_map/ppermute | solution.py:439
  40.5 30.6 %collective-permute-start.10 = (bf16[5,1032,128]{2,1,0:T(8,128)(2,1)S(1)}, bf16[5,1032,128]{2,1,0:T(8,128)(2,1)S(1)}, u32[]{:S(2)}, u32[]{:S(2)}) collective-permute-start(bf16[5,1032,128]{2,1,0:T(8,128)(2,1)S(1)} %shard_map.147.h0.refs_0_), channel_id=1, source_target_pairs={{0,6},{1,7},{2,0},{3,1},{4,2},{5,3},{6,4},{7,5},{8,14},{9,15},{10,... | collective-permute-start | bytes 3962888 | tf_op jit(solution)/shard_map/ppermute | solution.py:436
  40.7 59.5 %collective-permute-start.11 = (bf16[5,1032,128]{2,1,0:T(8,128)(2,1)S(1)}, bf16[5,1032,128]{2,1,0:T(8,128)(2,1)S(1)}, u32[]{:S(2)}, u32[]{:S(2)}) collective-permute-start(bf16[5,1032,128]{2,1,0:T(8,128)(2,1)S(1)} %shard_map.147.h0.refs_0_), channel_id=1, source_target_pairs={{0,4},{1,5},{2,6},{3,7},{4,0},{5,1},{6,2},{7,3},{8,12},{9,13},{10,... | collective-permute-start | bytes 3962888 | tf_op jit(solution)/shard_map/ppermute | solution.py:436
  42.9 58.3 %collective-permute-start.12 = (bf16[5,1032,128]{2,1,0:T(8,128)(2,1)S(1)}, bf16[5,1032,128]{2,1,0:T(8,128)(2,1)S(1)}, u32[]{:S(2)}, u32[]{:S(2)}) collective-permute-start(bf16[5,1032,128]{2,1,0:T(8,128)(2,1)S(1)} %shard_map.147.h0.refs_0_), channel_id=1, source_target_pairs={{0,2},{1,3},{2,4},{3,5},{4,6},{5,7},{6,0},{7,1},{8,10},{9,11},{10,... | collective-permute-start | bytes 3962888 | tf_op jit(solution)/shard_map/ppermute | solution.py:436
  44.4 63.4 %collective-permute-start.5 = (bf16[2,1024,512]{2,1,0:T(8,128)(2,1)S(1)}, bf16[2,1024,512]{2,1,0:T(8,128)(2,1)S(1)}, u32[]{:S(2)}, u32[]{:S(2)}) collective-permute-start(bf16[2,1024,512]{2,1,0:T(8,128)(2,1)S(1)} %copy-done), channel_id=1, source_target_pairs={{0,1},{1,0},{2,3},{3,2},{4,5},{5,4},{6,7},{7,6},{8,9},{9,8},{10,11... | collective-permute-start | bytes 6291464 | tf_op jit(solution)/shard_map/ppermute | solution.py:439
  71.0 54.6 %collective-permute-start.13 = (bf16[5,1032,128]{2,1,0:T(8,128)(2,1)S(1)}, bf16[5,1032,128]{2,1,0:T(8,128)(2,1)S(1)}, u32[]{:S(2)}, u32[]{:S(2)}) collective-permute-start(bf16[5,1032,128]{2,1,0:T(8,128)(2,1)S(1)} %collective-permute-done.10.h1.refs_1_), channel_id=1, source_target_pairs={{0,1},{1,0},{2,3},{3,2},{4,5},{5,4},{6,7},{7,6},{8,9},{9,8},{10,11... | collective-permute-start | bytes 3962888 | tf_op jit(solution)/shard_map/ppermute | solution.py:439
  100.3 30.5 %collective-permute-start.14 = (bf16[5,1032,128]{2,1,0:T(8,128)(2,1)S(1)}, bf16[5,1032,128]{2,1,0:T(8,128)(2,1)S(1)}, u32[]{:S(2)}, u32[]{:S(2)}) collective-permute-start(bf16[5,1032,128]{2,1,0:T(8,128)(2,1)S(1)} %collective-permute-done.11.h2.refs_2_), channel_id=1, source_target_pairs={{0,1},{1,0},{2,3},{3,2},{4,5},{5,4},{6,7},{7,6},{8,9},{9,8},{10,11... | collective-permute-start | bytes 3962888 | tf_op jit(solution)/shard_map/ppermute | solution.py:439
  101.1 29.6 %collective-permute-start.15 = (bf16[5,1032,128]{2,1,0:T(8,128)(2,1)S(1)}, bf16[5,1032,128]{2,1,0:T(8,128)(2,1)S(1)}, u32[]{:S(2)}, u32[]{:S(2)}) collective-permute-start(bf16[5,1032,128]{2,1,0:T(8,128)(2,1)S(1)} %collective-permute-done.12.h3.refs_3_), channel_id=1, source_target_pairs={{0,1},{1,0},{2,3},{3,2},{4,5},{5,4},{6,7},{7,6},{8,9},{9,8},{10,11... | collective-permute-start | bytes 3962888 | tf_op jit(solution)/shard_map/ppermute | solution.py:439
  102.0 5.8 %collective-permute-start.6 = (f32[2,512]{1,0:T(2,128)S(1)}, f32[2,512]{1,0:T(2,128)S(1)}, u32[]{:S(2)}, u32[]{:S(2)}) collective-permute-start(f32[2,512]{1,0:T(2,128)S(1)} %copy-done.17), channel_id=1, source_target_pairs={{0,1},{1,0},{2,3},{3,2},{4,5},{5,4},{6,7},{7,6},{8,9},{9,8},{10,11... | collective-permute-start | bytes 12296 | tf_op jit(solution)/shard_map/ppermute | solution.py:439
  123.2 7.6 %collective-permute-start.7 = (bf16[288,256]{1,0:T(8,128)(2,1)S(1)}, bf16[288,256]{1,0:T(8,128)(2,1)S(1)}, u32[]{:S(2)}, u32[]{:S(2)}) collective-permute-start(bf16[288,256]{1,0:T(8,128)(2,1)S(1)} %shard_map.149.h0), channel_id=1, source_target_pairs={{0,6},{1,7},{2,0},{3,1},{4,2},{5,3},{6,4},{7,5},{8,14},{9,15},{10,... | collective-permute-start | bytes 442376 | tf_op jit(solution)/shard_map/ppermute | solution.py:436
  125.7 6.0 %collective-permute-start.8 = (bf16[288,256]{1,0:T(8,128)(2,1)S(1)}, bf16[288,256]{1,0:T(8,128)(2,1)S(1)}, u32[]{:S(2)}, u32[]{:S(2)}) collective-permute-start(bf16[288,256]{1,0:T(8,128)(2,1)S(1)} %shard_map.149.h0), channel_id=1, source_target_pairs={{0,4},{1,5},{2,6},{3,7},{4,0},{5,1},{6,2},{7,3},{8,12},{9,13},{10,... | collective-permute-start | bytes 442376 | tf_op jit(solution)/shard_map/ppermute | solution.py:436
  125.7 6.0 %collective-permute-start.9 = (bf16[288,256]{1,0:T(8,128)(2,1)S(1)}, bf16[288,256]{1,0:T(8,128)(2,1)S(1)}, u32[]{:S(2)}, u32[]{:S(2)}) collective-permute-start(bf16[288,256]{1,0:T(8,128)(2,1)S(1)} %shard_map.149.h0), channel_id=1, source_target_pairs={{0,2},{1,3},{2,4},{3,5},{4,6},{5,7},{6,0},{7,1},{8,10},{9,11},{10,... | collective-permute-start | bytes 442376 | tf_op jit(solution)/shard_map/ppermute | solution.py:436
  139.0 8.2 %collective-permute-start.16 = (bf16[65,1024]{1,0:T(8,128)(2,1)S(1)}, bf16[65,1024]{1,0:T(8,128)(2,1)S(1)}, u32[]{:S(2)}, u32[]{:S(2)}) collective-permute-start(bf16[65,1024]{1,0:T(8,128)(2,1)S(1)} %get-tuple-element.72), channel_id=1, source_target_pairs={{0,2},{1,3},{2,4},{3,5},{4,6},{5,7},{6,0},{7,1},{8,10},{9,11},{10,... | collective-permute-start | bytes 399368 | tf_op jit(solution)/shard_map/ppermute | solution.py:436
  141.3 6.0 %collective-permute-start.18 = (bf16[65,1024]{1,0:T(8,128)(2,1)S(1)}, bf16[65,1024]{1,0:T(8,128)(2,1)S(1)}, u32[]{:S(2)}, u32[]{:S(2)}) collective-permute-start(bf16[65,1024]{1,0:T(8,128)(2,1)S(1)} %get-tuple-element.74), channel_id=1, source_target_pairs={{0,6},{1,7},{2,0},{3,1},{4,2},{5,3},{6,4},{7,5},{8,14},{9,15},{10,... | collective-permute-start | bytes 399368 | tf_op jit(solution)/shard_map/ppermute | solution.py:436
  143.3 7.3 %collective-permute-start.17 = (bf16[65,1024]{1,0:T(8,128)(2,1)S(1)}, bf16[65,1024]{1,0:T(8,128)(2,1)S(1)}, u32[]{:S(2)}, u32[]{:S(2)}) collective-permute-start(bf16[65,1024]{1,0:T(8,128)(2,1)S(1)} %get-tuple-element.73), channel_id=1, source_target_pairs={{0,4},{1,5},{2,6},{3,7},{4,0},{5,1},{6,2},{7,3},{8,12},{9,13},{10,... | collective-permute-start | bytes 399368 | tf_op jit(solution)/shard_map/ppermute | solution.py:436
  153.4 45.8 %collective-permute-start.20 = (bf16[2,1032,512]{2,1,0:T(8,128)(2,1)}, bf16[2,1032,512]{2,1,0:T(8,128)(2,1)}, u32[]{:S(2)}, u32[]{:S(2)}) collective-permute-start(bf16[2,1032,512]{2,1,0:T(8,128)(2,1)} %get-tuple-element.80), channel_id=1, source_target_pairs={{0,2},{1,3},{2,0},{3,1},{4,6},{5,7},{6,4},{7,5},{8,10},{9,11},{10,... | collective-permute-start | bytes 6340616 | tf_op jit(solution)/shard_map/ppermute | solution.py:576
  173.3 5.0 %collective-permute-start.19 = (bf16[32,56,128]{2,1,0:T(8,128)(2,1)S(1)}, bf16[32,56,128]{2,1,0:T(8,128)(2,1)S(1)}, u32[]{:S(2)}, u32[]{:S(2)}) collective-permute-start(bf16[32,56,128]{2,1,0:T(8,128)(2,1)S(1)} %all_to_all.22.r_own), channel_id=1, source_target_pairs={{0,1},{1,0},{2,3},{3,2},{4,5},{5,4},{6,7},{7,6},{8,9},{9,8},{10,11... | collective-permute-start | bytes 1376264 | tf_op jit(solution)/shard_map/ppermute | solution.py:439
  183.2 15.1 %all-to-all-start.3 = ((bf16[32,24,128]{2,1,0:T(8,128)(2,1)}), bf16[32,24,128]{2,1,0:T(8,128)(2,1)}, u32[]{:S(2)}, u32[]{:S(2)}) async-start(bf16[32,24,128]{2,1,0:T(8,128)(2,1)} %shard_map.156), calls=%async_computation.3 | async-start | bytes 393216 | tf_op jit(solution)/shard_map/all_to_all | solution.py:473
  199.2 15.5 %collective-permute-start.21 = (bf16[2,1032,512]{2,1,0:T(8,128)(2,1)}, bf16[2,1032,512]{2,1,0:T(8,128)(2,1)S(1)}, u32[]{:S(2)}, u32[]{:S(2)}) collective-permute-start(bf16[2,1032,512]{2,1,0:T(8,128)(2,1)} %collective-permute-done.20.far), channel_id=1, source_target_pairs={{0,1},{1,0},{2,3},{3,2},{4,5},{5,4},{6,7},{7,6},{8,9},{9,8},{10,11... | collective-permute-start | bytes 6340616 | tf_op jit(solution)/shard_map/ppermute | solution.py:439
  209.2 5.5 %collective-permute-start.22 = (bf16[65,1024]{1,0:T(8,128)(2,1)S(1)}, bf16[65,1024]{1,0:T(8,128)(2,1)S(1)}, u32[]{:S(2)}, u32[]{:S(2)}) collective-permute-start(bf16[65,1024]{1,0:T(8,128)(2,1)S(1)} %get-tuple-element.85.n), channel_id=1, source_target_pairs={{0,6},{1,7},{2,4},{3,5},{4,2},{5,3},{6,0},{7,1},{8,14},{9,15},{10,... | collective-permute-start | bytes 399368 | tf_op jit(solution)/shard_map/ppermute | solution.py:576
  (33 other events, 706.6 us)

commit v2 on v1

--- a/solution.py
+++ b/solution.py
@@ -20,7 +20,7 @@
 SCALE = 0.125 * LOG2E
 NEG = -1e30
 
-GROUPS = ((1, 3), (2, 0))
+GROUPS = ((1, 3, 2, 0),)
 
 
 def lanes(shape):
@@ -79,7 +79,7 @@
 
 
 def load_kernel(planes, *refs):
-    held, (out, sems) = refs[:5], refs[5:]
+    *held, out, sems = refs
     copies = [pltpu.make_async_copy(ref.at[planes], out.at[c], sems.at[c]) for c, ref in enumerate(held)]
     for copy in copies:
         copy.start()
@@ -87,12 +87,10 @@
         copy.wait()
 
 
-def load_far_kernel(h0, h1, h2, h3, h4, w1_ref, b1_ref, w2_ref, out, packed, bias, sems):
+def load_mlp_kernel(w1_ref, b1_ref, w2_ref, packed, w1, w2, bias, sems):
     copies = [
-        pltpu.make_async_copy(ref.at[4:5], out.at[c], sems.at[4 + c])
-        for c, ref in enumerate((h0, h1, h2, h3, h4))
-    ]
-    copies += [
+        pltpu.make_async_copy(w1_ref.at[0], w1, sems.at[4]),
+        pltpu.make_async_copy(w2_ref.at[0], w2, sems.at[5]),
         pltpu.make_async_copy(w1_ref.at[1], packed.at[0, 0:D], sems.at[0]),
         pltpu.make_async_copy(w2_ref.at[1, :, 0:512], packed.at[1, 0:512], sems.at[1]),
         pltpu.make_async_copy(w2_ref.at[1, :, 512:D], packed.at[1, 512:D], sems.at[2]),
@@ -247,29 +245,56 @@
         par = r_par[at, 0:32, :].reshape(64, 128)
         place(128 * t + 128, jnp.concatenate([own, par], axis=0))
 
-    def attend(lhs, rows, n, buf):
+    def dots(lhs, rows, n, buf):
         score[buf, 0:rows, 0:n] = jnp.dot(lhs, kt[:, 0:n], preferred_element_type=jnp.float32)
+
+    def soft(rows, n, buf):
         for r in range(0, rows, 16):
             now = score[buf, r : r + 16, 0:n]
             now = jnp.exp2(now - jnp.max(now, axis=1, keepdims=True))
             prob[buf, r : r + 16, 0:n] = now.astype(jnp.bfloat16)
-        mixed = jnp.dot(prob[buf, 0:rows, 0:n], vals[0:n, :], preferred_element_type=jnp.float32)
-        return mixed / pltpu.roll(mixed, 64, 1)
+
+    def mix(rows, n, buf):
+        return jnp.dot(prob[buf, 0:rows, 0:n], vals[0:n, :], preferred_element_type=jnp.float32)
 
     row = lax.broadcasted_iota(jnp.int32, (256, 128), 0)
-    for i in range(4):
+    lowh = lanes((128, 128)) < 64
+
+    def lhs_of(i):
         packed = jnp.concatenate(
             [r_own[pl.ds(2 * order[4 * i + t], 2), 32:48, :].reshape(32, 128) for t in range(4)], axis=0
         ).astype(jnp.float32)
         packed = jnp.concatenate([packed, pltpu.roll(packed, 64, 1)], axis=0)
         which = jnp.where(lanes((256, 128)) == 4 * i + (row % 128) // 32, 1.0, 0.0)
-        res = attend(queries(packed, which), 256, 128 + 512 * (i + 1), i % 2)
-        merged = jnp.where(low, pltpu.roll(res[:128], 64, 1), res[128:]).astype(jnp.bfloat16)
+        return queries(packed, which)
+
+    def put(i, mixed):
+        first, second = mixed[:128], mixed[128:]
+        value = jnp.where(lowh, pltpu.roll(first, 64, 1), second)
+        total = jnp.where(lowh, first, pltpu.roll(second, 64, 1))
+        merged = (value / total).astype(jnp.bfloat16)
         for t in range(4):
             out[pl.ds(2 * order[4 * i + t], 2), 0:16, :] = merged[32 * t : 32 * t + 32].reshape(2, 16, 128)
+
+    n_of = [128 + 128 * 4 * (i + 1) for i in range(4)]
     packed = jnp.sum(jnp.where(sub == 1, tail_own, 0.0), axis=1)
     which = jnp.where(lanes((PARTS, 128)) == part_time[...], 1.0, 0.0)
-    res = pltpu.roll(attend(queries(packed, which), PARTS, KEYS, 0), 64, 1)
+    cond = queries(packed, which)
+    steps = [(lhs_of(i), 256, n_of[i]) for i in range(4)] + [(cond, PARTS, KEYS)]
+    done = {}
+    dots(*steps[0], 0)
+    for i in range(len(steps) + 1):
+        if i + 1 < len(steps):
+            dots(*steps[i + 1], (i + 1) % 3)
+        if i < len(steps):
+            soft(*steps[i][1:], i % 3)
+        if i >= 1:
+            done[i - 1] = mix(*steps[i - 1][1:], (i - 1) % 3)
+            if i - 1 < len(steps) - 1:
+                put(i - 1, done[i - 1])
+
+    res = done[4]
+    res = pltpu.roll(res / pltpu.roll(res, 64, 1), 64, 1)
     out[:, 16:24, :] = jnp.broadcast_to(res[:, None, :], (PARTS, 8, 128)).astype(jnp.bfloat16)
 
 
@@ -305,13 +330,13 @@
 
 
 def every_out_kernel(h0, h1, h2, h3, xrows, o_bias, gain, bias, *rest):
-    w, *near, first, normed, lhs = rest
+    w, w_par, first, normed, lhs = rest
     for s, heads in enumerate((h0, h1, h2, h3)):
         for r in range(NX):
             at = PAD * ((r - s) % NX)
             lhs[PAD * r : PAD * r + PAD, 256 * s : 256 * s + 256] = heads[at : at + PAD, :]
     weight = jnp.concatenate(
-        [blocks_of(p) for s in range(NX) for p in (w.at[s, 0], near[s - 1].at[4] if s else w.at[4, 0])], axis=0
+        [blocks_of(p) for s in range(NX) for p in (w.at[s, 0], w_par.at[s, 0])], axis=0
     )
     total = jnp.dot(lhs[...], weight, preferred_element_type=jnp.float32)
     rows = xrows[...].astype(jnp.float32) + total + o_bias[0:1, :]
@@ -341,52 +366,71 @@
     for c, s in enumerate(group):
         rows[PAD * c : PAD * c + PAD, :] = n[PAD * s : PAD * s + PAD, :]
     total = None
-    for w1, b1, w2 in ((w1_own, b1_own, w2_own), (w1_par, b1_par, w2_par)):
-        inner = jnp.dot(rows[...], w1[0], preferred_element_type=jnp.float32) + b1[0:1, :]
+    for w1, b1, w2 in ((w1_own, b1_own, w2_own), (w1_par.at[0], b1_par, w2_par.at[0])):
+        inner = jnp.dot(rows[...], w1[...], preferred_element_type=jnp.float32) + b1[0:1, :]
         inner = (0.5 * inner * (1.0 + lax.erf(inner * 0.7071067811865476))).astype(jnp.bfloat16)
-        part = jnp.dot(inner, w2[0], preferred_element_type=jnp.float32)
+        part = jnp.dot(inner, w2[...], preferred_element_type=jnp.float32)
         total = part if total is None else total + part
     for c, y in enumerate(outs):
         y[...] = total[PAD * c : PAD * c + 65].astype(jnp.bfloat16)
 
 
-def pair_mlp_kernel(n, w1_own, w1_par, b1_own, b1_par, w2_own, w2_par, far, far_par, y, rows):
-    rows[0:65, :] = n[...]
-
-    def hidden(w1, b1):
-        inner = jnp.dot(rows[...], w1, preferred_element_type=jnp.float32) + b1
-        return (0.5 * inner * (1.0 + lax.erf(inner * 0.7071067811865476))).astype(jnp.bfloat16)
-
-    total = None
-    for w1, b1, w2 in ((w1_own, b1_own, w2_own), (w1_par, b1_par, w2_par)):
-        part = jnp.dot(hidden(w1[1], b1[1:2, :]), w2[1], preferred_element_type=jnp.float32)
-        total = part if total is None else total + part
-    for w in (far, far_par):
+def hidden(rows, w1, b1):
+    inner = jnp.dot(rows, w1, preferred_element_type=jnp.float32) + b1
+    return (0.5 * inner * (1.0 + lax.erf(inner * 0.7071067811865476))).astype(jnp.bfloat16)
+
+
+def add_mlp(total, rows, *shares):
+    for w in shares:
         bias = jnp.sum(w[0, D:HELD, :].astype(jnp.float32), axis=0, keepdims=True)
-        inner = hidden(w[0, 0:D, :], bias)
-        total += jnp.concatenate(
+        inner = hidden(rows, w[0, 0:D, :], bias)
+        part = jnp.concatenate(
             [
                 jnp.dot(inner, w[1, 512 * j : 512 * j + 512, :], preferred_element_type=jnp.float32)
                 for j in range(2)
             ],
             axis=1,
         )
-    y[...] = total[:65].astype(jnp.bfloat16)
-
-
-def last_kernel(idx, first, y0, y1, o_bias, stream, send):
+        total = part if total is None else total + part
+    return total
+
+
+def core_mlp(rows, w1_par, b1_par, w2_par):
+    return jnp.dot(hidden(rows, w1_par[1], b1_par[1:2, :]), w2_par[1], preferred_element_type=jnp.float32)
+
+
+def near_mlp_kernel(first, n, packed, w1_par, b1_par, w2_par, o_bias, total, rows):
+    rows[0:65, :] = n[...]
+    share = add_mlp(core_mlp(rows[...], w1_par, b1_par, w2_par), rows[...], packed)
+    total[...] = first[...] + share[:65] + o_bias[1:2, :]
+
+
+def far_mlp_kernel(idx, n, near, far, far_par, keep, send, rows):
     k = idx[1]
-    summed = y0[...].astype(jnp.float32) + y1[...].astype(jnp.float32)
-    rows = (first[...] + summed + o_bias[1:2, :]).astype(jnp.bfloat16)
-    stream[...] = rows
-    send[...] = jnp.where(k == 0, rows[32:64], rows[0:32])
-
-
-def place_kernel(idx, stream, recv, out):
+    rows[0:65, :] = n[...]
+    share = add_mlp(None, rows[...], far, far_par)
+    total = near[...] + share[:65]
+    keep[...] = total
+    send[...] = jnp.where(k == 0, total[32:64], total[0:32])
+
+
+def pair_mlp_kernel(idx, n, packed, w1_par, b1_par, w2_par, far, far_par, here, there, rows):
     k = idx[1]
-    out[0, 0:32, :] = jnp.where(k == 0, stream[0:32, :], recv[...])
-    out[0, 32:64, :] = jnp.where(k == 0, recv[...], stream[32:64, :])
-    out[0, 64:65, :] = stream[64:65, :]
+    rows[0:65, :] = n[...]
+    total = core_mlp(rows[...], w1_par, b1_par, w2_par)
+    total = add_mlp(total, rows[...], packed, far, far_par).astype(jnp.bfloat16)
+    here[0:32, :] = jnp.where(k == 0, total[0:32], total[32:64])
+    here[32:40, :] = total[64:72]
+    there[...] = jnp.where(k == 0, total[32:64], total[0:32])
+
+
+def last_kernel(idx, keep, other, here, there, out):
+    k = idx[1]
+    mine = jnp.where(k == 0, keep[0:32, :], keep[32:64, :]) + here[0:32, :].astype(jnp.float32)
+    theirs = other[...] + there[...].astype(jnp.float32)
+    out[0, 0:32, :] = jnp.where(k == 0, mine, theirs).astype(jnp.bfloat16)
+    out[0, 32:64, :] = jnp.where(k == 0, theirs, mine).astype(jnp.bfloat16)
+    out[0, 64:65, :] = (keep[64:65, :] + here[32:33, :].astype(jnp.float32)).astype(jnp.bfloat16)
 
 
 VMEM = pl.BlockSpec(memory_space=pltpu.VMEM)
@@ -448,7 +492,7 @@
 
     seen = []
 
-    def attention(layer, message, beside, *late):
+    def attention(layer, message, beside, *late, ahead=()):
         arrived = lax.all_to_all(message, "tm", 0, 0, tiled=True)
         arrived, *late = tie((arrived, *late))
         arrived_par = swap(arrived)
@@ -463,13 +507,13 @@
             [
                 pltpu.VMEM((256, KEYS), jnp.bfloat16),
                 pltpu.VMEM((KEYS, 128), jnp.bfloat16),
-                pltpu.VMEM((2, 256, KEYS), jnp.float32),
-                pltpu.VMEM((2, 256, KEYS), jnp.bfloat16),
+                pltpu.VMEM((3, 256, KEYS), jnp.float32),
+                pltpu.VMEM((3, 256, KEYS), jnp.bfloat16),
             ],
             scalars=2,
             limit=24,
         )
-        mixed, *late = tie((mixed, *late))
+        mixed, *late = tie((mixed, *late, *ahead))
         back = lax.all_to_all(mixed, "tm", 0, 0, tiled=True)
         return tie((back, *late))
 
@@ -479,9 +523,6 @@
         return [pltpu.with_memory_space_constraint(a, pltpu.HBM) for a in arrays]
 
     biases = jnp.transpose(qkv_bias, (1, 0, 2))
-    qkv_par = swap(qkv_weight)
-    biases_par = swap(biases)
-    fc2_par = swap(fc2_weight)
     idx = jnp.stack([x, k, k == (part // 4) % 2, k == part // 16]).astype(jnp.int32)
     held = call(
         pack_kernel,
@@ -490,6 +531,10 @@
         [pltpu.VMEM((3, LAYERS, 128), jnp.float32), pltpu.SemaphoreType.DMA((18,))],
         in_specs=[HBM] * 3,
     )
+    held, late_qkv, late_biases, late_fc2 = tie((held, qkv_weight, biases, fc2_weight))
+    qkv_par = swap(late_qkv)
+    biases_par = swap(late_biases)
+    fc2_par = swap(late_fc2)
     helds = spread(held)
     held_par = swap(held)
     xrows, message = call(
@@ -508,7 +553,7 @@
         in_specs=[SMEM, HBM, HBM, HBM, HBM, VMEM, HBM, HBM],
         limit=12,
     )
-    message, fc2_par, held_par = tie((message, fc2_par, held_par))
+    message = tie(message)
 
     def tables():
         return call(
@@ -523,31 +568,39 @@
             out_specs=[SMEM, VMEM, VMEM],
         )
 
-    def load(planes, count, rows):
+    def load(planes, count, refs):
         return call(
             functools.partial(load_kernel, planes),
-            far_refs,
-            jax.ShapeDtypeStruct((5, count, rows, 128), jnp.bfloat16),
-            [pltpu.SemaphoreType.DMA((5,))],
-            in_specs=[HBM] * 5,
+            refs,
+            jax.ShapeDtypeStruct((len(refs), count, HELD, 128), jnp.bfloat16),
+            [pltpu.SemaphoreType.DMA((len(refs),))],
+            in_specs=[HBM] * len(refs),
         )
 
-    back, fc1_par, fc1_bias_par = attention(0, message, tables, fc1_weight, fc1_bias)
+    back, fc1_par, fc1_bias_par, fc2_par, held_par = attention(
+        0, message, tables, fc1_weight, fc1_bias, ahead=(fc2_par, held_par)
+    )
     heads = call(heads_kernel, (idx, back), jax.ShapeDtypeStruct((NX * PAD, 256), jnp.bfloat16))
     heads = spread(heads)
+    packed, w1, w2 = call(
+        load_mlp_kernel,
+        in_hbm(fc1_weight, fc1_bias, fc2_weight),
+        [
+            jax.ShapeDtypeStruct((2, HELD, 512), jnp.bfloat16),
+            jax.ShapeDtypeStruct((D, 512), jnp.bfloat16),
+            jax.ShapeDtypeStruct((512, D), jnp.bfloat16),
+        ],
+        [pltpu.VMEM((LAYERS, 512), jnp.float32), pltpu.SemaphoreType.DMA((6,))],
+        in_specs=[HBM] * 3,
+    )
+    loaded = load(slice(4, 5), 1, in_hbm(*helds))
+    loaded_par = swap(loaded)
     held_pars = [held_par] + [swap(helds[s]) for s in (1, 2, 3)]
     far_refs = in_hbm(*helds, held_pars[0])
     near = held_pars[1:]
-    loaded, packed = call(
-        load_far_kernel,
-        (*far_refs, *in_hbm(fc1_weight, fc1_bias, fc2_weight)),
-        [jax.ShapeDtypeStruct((5, 1, HELD, 128), jnp.bfloat16), jax.ShapeDtypeStruct((2, HELD, 512), jnp.bfloat16)],
-        [pltpu.VMEM((LAYERS, 512), jnp.float32), pltpu.SemaphoreType.DMA((9,))],
-        in_specs=[HBM] * 8,
-    )
     first, normed_two = call(
         every_out_kernel,
-        (*heads, xrows, out_bias, ln2_gain, ln2_bias, loaded, *near),
+        (*heads, xrows, out_bias, ln2_gain, ln2_bias, loaded, loaded_par),
         [block(jnp.float32), block(rows=NX * PAD)],
         [pltpu.VMEM((NX * PAD, D), jnp.bfloat16)],
         scalars=0,
@@ -556,13 +609,18 @@
     for group in GROUPS:
         done = call(
             functools.partial(mlp_kernel, group),
-            (normed_two, fc1_weight, fc1_par, fc1_bias, fc1_bias_par, fc2_weight, fc2_par),
+            (normed_two, w1, fc1_par, fc1_bias, fc1_bias_par, w2, fc2_par),
             [block()] * len(group),
             [pltpu.VMEM((PAD * len(group), D), jnp.bfloat16)],
             scalars=0,
         )
         partial.update(zip(group, done))
-    loaded = load(slice(0, 3), 3, HELD)
+
+    def pair(array, other):
+        return lax.ppermute(array, "tensor", [(t, other(t // 2) * 2 + t % 2) for t in range(2 * NX)])
+
+    far = pair(packed, lambda c: c ^ 1)
+    loaded = load(slice(0, 3), 3, far_refs)
     partial = collect(partial)
     stream, message = call(
         turn_kernel,
@@ -570,13 +628,7 @@
         [block(), message_shape],
         [pltpu.VMEM((PAD, D), jnp.bfloat16), pltpu.VMEM((2 * NX, 3, PAD, 128), jnp.float32)],
     )
-    message, packed = tie((message, packed))
-
-    def pair(array, other):
-        return lax.ppermute(array, "tensor", [(t, other(t // 2) * 2 + t % 2) for t in range(2 * NX)])
-
-    far = pair(packed, lambda c: c ^ 1)
-    (back,) = attention(1, message, lambda: load(slice(3, 4), 1, HELD))
+    (back,) = attention(1, message, lambda: load(slice(3, 4), 1, far_refs))
     back, far, loaded = tie((back, far, seen[1]))
     far_par = swap(far)
     first, normed_two = call(
@@ -585,24 +637,30 @@
         [block(jnp.float32), block()],
         [pltpu.VMEM((PAD, D), jnp.bfloat16)],
     )
-    weights = (fc1_weight, fc1_par, fc1_bias, fc1_bias_par, fc2_weight, fc2_par, far, far_par)
-    partial = []
-    for n in (normed_two, pair(normed_two, lambda c: 3 - c)):
-        partial.append(
-            call(
-                pair_mlp_kernel,
-                (n, *weights),
-                block(),
-                [pltpu.VMEM((PAD, D), jnp.bfloat16)],
-                scalars=0,
-            )
-        )
-    added = pair(partial[1], lambda c: 3 - c)
-    stream, send = call(
-        last_kernel, (idx, first, partial[0], added, fc2_bias), [block(), block(rows=32)]
-    )
-    recv = swap(send)
-    return call(place_kernel, (idx, stream, recv), jax.ShapeDtypeStruct((1, BLOCK, D), jnp.bfloat16))
+    moved = pair(normed_two, lambda c: 3 - c)
+    pad = [pltpu.VMEM((PAD, D), jnp.bfloat16)]
+    weights = (packed, fc1_par, fc1_bias_par, fc2_par)
+    total = call(
+        near_mlp_kernel,
+        (first, normed_two, *weights, fc2_bias),
+        block(jnp.float32),
+        pad,
+        scalars=0,
+    )
+    keep, send = call(
+        far_mlp_kernel,
+        (idx, normed_two, total, far, far_par),
+        [block(jnp.float32), block(jnp.float32, 32)],
+        pad,
+    )
+    other = swap(send)
+    here, there = call(pair_mlp_kernel, (idx, moved, *weights, far, far_par), [block(rows=40), block(rows=32)], pad)
+    here = pair(here, lambda c: 3 - c)
+    cross = [(t, (3 - t // 2) * 2 + 1 - t % 2) for t in range(2 * NX)]
+    there = lax.ppermute(there, "tensor", cross)
+    return call(
+        last_kernel, (idx, keep, other, here, there), jax.ShapeDtypeStruct((1, BLOCK, D), jnp.bfloat16)
+    )
 
 
 def solution(mesh):

time: 232 us -> 275 us (1.19)
  the two profiles are of different devices: /device:TPU:35 before, /device:TPU:1 now
where the time goes in v2:
time: 275 us; the launch traced here: 274 us
  waiting for transfers between devices  138 us (50%)
  starting transfers between devices  53 us (19%)
  Pallas kernels  41.4 us (15%)
  blocking collectives  34.5 us (13%)
  local copies, waits for them, and re-layouts  7.19 us (3%)
    ppermute x9, waiting for transfers between devices, shift(): return lax.ppermute(array, 'tensor', pairs)  103 us
    pallas_call x18, Pallas kernels, call(): pl.pallas_call(kernel, out_shape=out_shape, in_specs=in_specs or [SMEM] *...  41.4 us
    all_to_all x1, blocking collectives, attention(): arrived = lax.all_to_all(message, 'tm', 0, 0, tiled=True)  19.8 us
    ppermute x14, starting transfers between devices, swap(): return lax.ppermute(array, 'tensor', [(t, t ^ 1) for t in range(2 * NX)])  19.3 us
    all_to_all x1, blocking collectives, attention(): back = lax.all_to_all(mixed, 'tm', 0, 0, tiled=True)  14.7 us
    ppermute x9, starting transfers between devices, shift(): return lax.ppermute(array, 'tensor', pairs)  13.7 us
    all_to_all x1, waiting for transfers between devices, attention(): arrived = lax.all_to_all(message, 'tm', 0, 0, tiled=True)  11.8 us
    ppermute x14, waiting for transfers between devices, swap(): return lax.ppermute(array, 'tensor', [(t, t ^ 1) for t in range(2 * NX)])  11.6 us
  transfers between devices with their start and end apart: 29, of which 13 were waited for; matrix products, arithmetic and copies ran while one was open for 0% of the time, Pallas kernels for 13%

profile of v2, /device:TPU:1, one launch (start us, length us, event | category | flops | bytes accessed | tf_op | source)
XLA Modules:
  0.0 274.3 jit_solution(12058732450061403092)
XLA Ops:
  1.9 3.2 %collective-permute-start = (bf16[2,3,1024,128]{3,2,1,0:T(8,128)(2,1)S(1)}, bf16[2,3,1024,128]{3,2,1,0:T(8,128)(2,1)}, u32[]{:S(2)}, u32[]{:S(2)}) collective-permute-start(bf16[2,3,1024,128]{3,2,1,0:T(8,128)(2,1)S(1)} %copy-done.25), channel_id=1, source_target_pairs={{0,1},{1,0},{2,3},{3,2},{4,5},{5,4},{6,7},{7,6},{8,9},{9,8},{10,11... | collective-permute-start | bytes 4718600 | tf_op jit(solution)/shard_map/ppermute | solution.py:483
  5.2 3.0 %collective-permute-done.1.b_par = f32[3,2,128]{2,1,0:T(2,128)S(1)} collective-permute-done((f32[3,2,128]{2,1,0:T(2,128)S(1)}, f32[3,2,128]{2,1,0:T(2,128)S(1)}, u32[]{:S(2)}, u32[]{:S(2)}) %collective-permute-start.1) | collective-permute-done | bytes 3104 | tf_op jit(solution)/shard_map/ppermute | solution.py:483
  8.2 4.1 %shard_map.147 = (bf16[288,1024]{1,0:T(8,128)(2,1)S(1)}, bf16[32,56,128]{2,1,0:T(8,128)(2,1)}) custom-call(s32[4]{0:T(128)S(1)} %pad_add_fusion.idx, bf16[1,520,1024]{2,1,0:T(8,128)(2,1)} %x_ref.1, bf16[2,3,1024,128]{3,2,1,0:T(8,128)(2,1)} %w_own.1, bf16[2,3,1024,128]{3,2,1,0:T(8,128)(2,1)} %collective-permute-done.w_par, f32[3,2,128]{2,1,0:T(2,128)} %bitcast.6, ...), custom_call_target="tpu_custom_call" | custom-call | tf_op jit(solution)/shard_map/pallas_call | solution.py:446
  13.2 9.6 %all-to-all-start = ((bf16[32,56,128]{2,1,0:T(8,128)(2,1)}), bf16[32,56,128]{2,1,0:T(8,128)(2,1)}, u32[]{:S(2)}, u32[]{:S(2)}) async-start(bf16[32,56,128]{2,1,0:T(8,128)(2,1)} %get-tuple-element.58), calls=%async_computation | async-start | bytes 917504 | tf_op jit(solution)/shard_map/all_to_all | solution.py:496
  24.1 11.8 %all-to-all-done.r_own = bf16[32,56,128]{2,1,0:T(8,128)(2,1)} async-done(((bf16[32,56,128]{2,1,0:T(8,128)(2,1)}), bf16[32,56,128]{2,1,0:T(8,128)(2,1)}, u32[]{:S(2)}, u32[]{:S(2)}) %all-to-all-start) | async-done | bytes 458784 | tf_op jit(solution)/shard_map/all_to_all | solution.py:496
  35.9 3.1 %collective-permute-start.2 = (bf16[32,56,128]{2,1,0:T(8,128)(2,1)}, bf16[32,56,128]{2,1,0:T(8,128)(2,1)S(1)}, u32[]{:S(2)}, u32[]{:S(2)}) collective-permute-start(bf16[32,56,128]{2,1,0:T(8,128)(2,1)} %all-to-all-done.r_own), channel_id=1, source_target_pairs={{0,1},{1,0},{2,3},{3,2},{4,5},{5,4},{6,7},{7,6},{8,9},{9,8},{10,11... | collective-permute-start | bytes 1376264 | tf_op jit(solution)/shard_map/ppermute | solution.py:483
  41.1 2.7 %collective-permute-start.11 = (bf16[5,1032,128]{2,1,0:T(8,128)(2,1)S(1)}, bf16[5,1032,128]{2,1,0:T(8,128)(2,1)S(1)}, u32[]{:S(2)}, u32[]{:S(2)}) collective-permute-start(bf16[5,1032,128]{2,1,0:T(8,128)(2,1)S(1)} %shard_map.146.refs_0_), channel_id=1, source_target_pairs={{0,4},{1,5},{2,6},{3,7},{4,0},{5,1},{6,2},{7,3},{8,12},{9,13},{10,... | collective-permute-start | bytes 3962888 | tf_op jit(solution)/shard_map/ppermute | solution.py:480
  44.7 9.4 %collective-permute-done.12.refs_3_ = bf16[5,1032,128]{2,1,0:T(8,128)(2,1)} collective-permute-done((bf16[5,1032,128]{2,1,0:T(8,128)(2,1)S(1)}, bf16[5,1032,128]{2,1,0:T(8,128)(2,1)}, u32[]{:S(2)}, u32[]{:S(2)}) %collective-permute-start.12) | collective-permute-done | bytes 1320992 | tf_op jit(solution)/shard_map/ppermute | solution.py:480
  55.8 27.5 %collective-permute-done.11.refs_2_ = bf16[5,1032,128]{2,1,0:T(8,128)(2,1)S(1)} collective-permute-done((bf16[5,1032,128]{2,1,0:T(8,128)(2,1)S(1)}, bf16[5,1032,128]{2,1,0:T(8,128)(2,1)S(1)}, u32[]{:S(2)}, u32[]{:S(2)}) %collective-permute-start.11) | collective-permute-done | bytes 1320992 | tf_op jit(solution)/shard_map/ppermute | solution.py:480
  83.3 18.1 %collective-permute-done.10.refs_1_ = bf16[5,1032,128]{2,1,0:T(8,128)(2,1)S(1)} collective-permute-done((bf16[5,1032,128]{2,1,0:T(8,128)(2,1)S(1)}, bf16[5,1032,128]{2,1,0:T(8,128)(2,1)S(1)}, u32[]{:S(2)}, u32[]{:S(2)}) %collective-permute-start.10) | collective-permute-done | bytes 1320992 | tf_op jit(solution)/shard_map/ppermute | solution.py:480
  105.4 5.5 %collective-permute-done.4.b1_par = f32[2,512]{1,0:T(2,128)S(1)} collective-permute-done((f32[2,512]{1,0:T(2,128)S(1)}, f32[2,512]{1,0:T(2,128)S(1)}, u32[]{:S(2)}, u32[]{:S(2)}) %collective-permute-start.4) | collective-permute-done | bytes 4128 | tf_op jit(solution)/shard_map/ppermute | solution.py:483
  112.5 3.9 %shard_map.148 = bf16[32,24,128]{2,1,0:T(8,128)(2,1)S(1)} custom-call(s32[4]{0:T(128)S(1)} %pad_add_fusion.idx, s32[16]{0:T(128)S(1)} %get-tuple-element.53.order, bf16[16,2176]{1,0:T(8,128)(2,1)S(1)} %get-tuple-element.54.mask, s32[32,128]{1,0:T(8,128)S(1)} %get-tuple-element.55.part_time, bf16[32,56,128]{2,1,0:T(8,128)(2,1)} %all-to-all-done.r_own, ...), custom_call_target="tpu_custom_call" | custom-call | tf_op jit(solution)/shard_map/pallas_call | solution.py:446
  116.4 14.7 %all_to_all.20.back = bf16[32,24,128]{2,1,0:T(8,128)(2,1)S(1)} all-to-all(bf16[32,24,128]{2,1,0:T(8,128)(2,1)S(1)} %shard_map.148), channel_id=1, replica_groups=mesh['tm'=32,'tensor'=8] {'tm'}, dimensions={0} | all-to-all | bytes 393216 | tf_op jit(solution)/shard_map/all_to_all | solution.py:517
  135.4 3.6 %shard_map.152 = (bf16[2,1032,512]{2,1,0:T(8,128)(2,1)}, bf16[1024,512]{1,0:T(8,128)(2,1)S(1)}, bf16[512,1024]{1,0:T(8,128)(2,1)S(1)}) custom-call(bf16[2,1024,512]{2,1,0:T(8,128)(2,1)} %w1_ref.1, f32[2,512]{1,0:T(2,128)} %b1_own.1, bf16[2,512,1024]{2,1,0:T(8,128)(2,1)} %w2_ref.1), custom_call_target="tpu_custom_call" | custom-call | tf_op jit(solution)/shard_map/pallas_call | solution.py:446
  140.0 46.4 %collective-permute-done.7.h1 = bf16[288,256]{1,0:T(8,128)(2,1)S(1)} collective-permute-done((bf16[288,256]{1,0:T(8,128)(2,1)S(1)}, bf16[288,256]{1,0:T(8,128)(2,1)S(1)}, u32[]{:S(2)}, u32[]{:S(2)}) %collective-permute-start.7) | collective-permute-done | bytes 147488 | tf_op jit(solution)/shard_map/ppermute | solution.py:480
  196.7 2.8 %shard_map.155 = (bf16[65,1024]{1,0:T(8,128)(2,1)S(1)}, bf16[32,56,128]{2,1,0:T(8,128)(2,1)S(1)}) custom-call(s32[4]{0:T(128)S(1)} %pad_add_fusion.idx, f32[65,1024]{1,0:T(8,128)S(1)} %get-tuple-element.75.first, bf16[65,1024]{1,0:T(8,128)(2,1)S(1)} %get-tuple-element.82.y0, bf16[65,1024]{1,0:T(8,128)(2,1)S(1)} %collective-permute-done.14.y1, ...), custom_call_target="tpu_custom_call" | custom-call | tf_op jit(solution)/shard_map/pallas_call | solution.py:446
  199.4 19.8 %all_to_all.21.r_own = bf16[32,56,128]{2,1,0:T(8,128)(2,1)S(1)} all-to-all(bf16[32,56,128]{2,1,0:T(8,128)(2,1)S(1)} %get-tuple-element.87), channel_id=1, replica_groups=mesh['tm'=32,'tensor'=8] {'tm'}, dimensions={0} | all-to-all | bytes 917504 | tf_op jit(solution)/shard_map/all_to_all | solution.py:496
  219.2 5.5 %collective-permute-start.20 = (bf16[32,56,128]{2,1,0:T(8,128)(2,1)S(1)}, bf16[32,56,128]{2,1,0:T(8,128)(2,1)S(1)}, u32[]{:S(2)}, u32[]{:S(2)}) collective-permute-start(bf16[32,56,128]{2,1,0:T(8,128)(2,1)S(1)} %all_to_all.21.r_own), channel_id=1, source_target_pairs={{0,1},{1,0},{2,3},{3,2},{4,5},{5,4},{6,7},{7,6},{8,9},{9,8},{10,11... | collective-permute-start | bytes 1376264 | tf_op jit(solution)/shard_map/ppermute | solution.py:483
  226.2 4.1 %shard_map.156 = bf16[32,24,128]{2,1,0:T(8,128)(2,1)} custom-call(s32[4]{0:T(128)S(1)} %pad_add_fusion.idx, s32[16]{0:T(128)S(1)} %get-tuple-element.53.order, bf16[16,2176]{1,0:T(8,128)(2,1)S(1)} %get-tuple-element.54.mask, s32[32,128]{1,0:T(8,128)S(1)} %get-tuple-element.55.part_time, bf16[32,56,128]{2,1,0:T(8,128)(2,1)S(1)} %all_to_all.21.r_own, ...), custom_call_target="tpu_custom_call" | custom-call | tf_op jit(solution)/shard_map/pallas_call | solution.py:446
  230.3 5.3 %all-to-all-start.3 = ((bf16[32,24,128]{2,1,0:T(8,128)(2,1)}), bf16[32,24,128]{2,1,0:T(8,128)(2,1)}, u32[]{:S(2)}, u32[]{:S(2)}) async-start(bf16[32,24,128]{2,1,0:T(8,128)(2,1)} %shard_map.156), calls=%async_computation.3 | async-start | bytes 393216 | tf_op jit(solution)/shard_map/all_to_all | solution.py:517
  236.9 8.1 %all-to-all-done.3.back = bf16[32,24,128]{2,1,0:T(8,128)(2,1)} async-done(((bf16[32,24,128]{2,1,0:T(8,128)(2,1)}), bf16[32,24,128]{2,1,0:T(8,128)(2,1)}, u32[]{:S(2)}, u32[]{:S(2)}) %all-to-all-start.3) | async-done | bytes 196640 | tf_op jit(solution)/shard_map/all_to_all | solution.py:517
  245.0 2.9 %collective-permute-start.22 = (bf16[2,1032,512]{2,1,0:T(8,128)(2,1)}, bf16[2,1032,512]{2,1,0:T(8,128)(2,1)S(1)}, u32[]{:S(2)}, u32[]{:S(2)}) collective-permute-start(bf16[2,1032,512]{2,1,0:T(8,128)(2,1)} %collective-permute-done.21.far), channel_id=1, source_target_pairs={{0,1},{1,0},{2,3},{3,2},{4,5},{5,4},{6,7},{7,6},{8,9},{9,8},{10,11... | collective-permute-start | bytes 6340616 | tf_op jit(solution)/shard_map/ppermute | solution.py:483
  262.1 4.1 %shard_map.161 = (bf16[40,1024]{1,0:T(8,128)(2,1)S(1)}, bf16[32,1024]{1,0:T(8,128)(2,1)S(1)}) custom-call(s32[4]{0:T(128)S(1)} %pad_add_fusion.idx, bf16[65,1024]{1,0:T(8,128)(2,1)S(1)} %collective-permute-done.24.n, bf16[2,1032,512]{2,1,0:T(8,128)(2,1)} %get-tuple-element.90.packed, bf16[2,1024,512]{2,1,0:T(8,128)(2,1)S(1)} %copy-done.2, ...), custom_call_target="tpu_custom_call" | custom-call | tf_op jit(solution)/shard_map/pallas_call | solution.py:446
  269.3 3.7 %collective-permute-done.26.there = bf16[32,1024]{1,0:T(8,128)(2,1)S(1)} collective-permute-done((bf16[32,1024]{1,0:T(8,128)(2,1)S(1)}, bf16[32,1024]{1,0:T(8,128)(2,1)S(1)}, u32[]{:S(2)}, u32[]{:S(2)}) %collective-permute-start.26) | collective-permute-done | bytes 65568 | tf_op jit(solution)/shard_map/ppermute | solution.py:660
  (111 shorter events, 51.0 us)
Async XLA Ops:
  1.9 6.4 %collective-permute-start = (bf16[2,3,1024,128]{3,2,1,0:T(8,128)(2,1)S(1)}, bf16[2,3,1024,128]{3,2,1,0:T(8,128)(2,1)}, u32[]{:S(2)}, u32[]{:S(2)}) collective-permute-start(bf16[2,3,1024,128]{3,2,1,0:T(8,128)(2,1)S(1)} %copy-done.25), channel_id=1, source_target_pairs={{0,1},{1,0},{2,3},{3,2},{4,5},{5,4},{6,7},{7,6},{8,9},{9,8},{10,11... | collective-permute-start | bytes 4718600 | tf_op jit(solution)/shard_map/ppermute | solution.py:483
  13.2 22.8 %all-to-all-start = ((bf16[32,56,128]{2,1,0:T(8,128)(2,1)}), bf16[32,56,128]{2,1,0:T(8,128)(2,1)}, u32[]{:S(2)}, u32[]{:S(2)}) async-start(bf16[32,56,128]{2,1,0:T(8,128)(2,1)} %get-tuple-element.58), calls=%async_computation | async-start | bytes 917504 | tf_op jit(solution)/shard_map/all_to_all | solution.py:496
  22.8 31.3 %collective-permute-start.12 = (bf16[5,1032,128]{2,1,0:T(8,128)(2,1)S(1)}, bf16[5,1032,128]{2,1,0:T(8,128)(2,1)}, u32[]{:S(2)}, u32[]{:S(2)}) collective-permute-start(bf16[5,1032,128]{2,1,0:T(8,128)(2,1)S(1)} %shard_map.146.refs_0_), channel_id=1, source_target_pairs={{0,2},{1,3},{2,4},{3,5},{4,6},{5,7},{6,0},{7,1},{8,10},{9,11},{10,... | collective-permute-start | bytes 3962888 | tf_op jit(solution)/shard_map/ppermute | solution.py:480
  39.0 66.3 %collective-permute-start.5 = (bf16[2,512,1024]{2,1,0:T(8,128)(2,1)}, bf16[2,512,1024]{2,1,0:T(8,128)(2,1)S(1)}, u32[]{:S(2)}, u32[]{:S(2)}) collective-permute-start(bf16[2,512,1024]{2,1,0:T(8,128)(2,1)} %w2_ref.1), channel_id=1, source_target_pairs={{0,1},{1,0},{2,3},{3,2},{4,5},{5,4},{6,7},{7,6},{8,9},{9,8},{10,11... | collective-permute-start | bytes 6291464 | tf_op jit(solution)/shard_map/ppermute | solution.py:483
  40.7 75.7 %collective-permute-start.3 = (bf16[2,1024,512]{2,1,0:T(8,128)(2,1)}, bf16[2,1024,512]{2,1,0:T(8,128)(2,1)S(1)}, u32[]{:S(2)}, u32[]{:S(2)}) collective-permute-start(bf16[2,1024,512]{2,1,0:T(8,128)(2,1)} %w1_ref.1), channel_id=1, source_target_pairs={{0,1},{1,0},{2,3},{3,2},{4,5},{5,4},{6,7},{7,6},{8,9},{9,8},{10,11... | collective-permute-start | bytes 6291464 | tf_op jit(solution)/shard_map/ppermute | solution.py:483
  41.1 42.2 %collective-permute-start.11 = (bf16[5,1032,128]{2,1,0:T(8,128)(2,1)S(1)}, bf16[5,1032,128]{2,1,0:T(8,128)(2,1)S(1)}, u32[]{:S(2)}, u32[]{:S(2)}) collective-permute-start(bf16[5,1032,128]{2,1,0:T(8,128)(2,1)S(1)} %shard_map.146.refs_0_), channel_id=1, source_target_pairs={{0,4},{1,5},{2,6},{3,7},{4,0},{5,1},{6,2},{7,3},{8,12},{9,13},{10,... | collective-permute-start | bytes 3962888 | tf_op jit(solution)/shard_map/ppermute | solution.py:480
  43.8 57.6 %collective-permute-start.10 = (bf16[5,1032,128]{2,1,0:T(8,128)(2,1)S(1)}, bf16[5,1032,128]{2,1,0:T(8,128)(2,1)S(1)}, u32[]{:S(2)}, u32[]{:S(2)}) collective-permute-start(bf16[5,1032,128]{2,1,0:T(8,128)(2,1)S(1)} %shard_map.146.refs_0_), channel_id=1, source_target_pairs={{0,6},{1,7},{2,0},{3,1},{4,2},{5,3},{6,4},{7,5},{8,14},{9,15},{10,... | collective-permute-start | bytes 3962888 | tf_op jit(solution)/shard_map/ppermute | solution.py:480
  54.1 50.8 %collective-permute-start.6 = (bf16[5,1032,128]{2,1,0:T(8,128)(2,1)S(1)}, bf16[5,1032,128]{2,1,0:T(8,128)(2,1)S(1)}, u32[]{:S(2)}, u32[]{:S(2)}) collective-permute-start(bf16[5,1032,128]{2,1,0:T(8,128)(2,1)S(1)} %shard_map.146.refs_0_), channel_id=1, source_target_pairs={{0,1},{1,0},{2,3},{3,2},{4,5},{5,4},{6,7},{7,6},{8,9},{9,8},{10,11... | collective-permute-start | bytes 3962888 | tf_op jit(solution)/shard_map/ppermute | solution.py:483
  103.7 29.2 %collective-permute-start.13 = (bf16[4,1,1032,128]{3,2,1,0:T(8,128)(2,1)S(1)}, bf16[4,1,1032,128]{3,2,1,0:T(8,128)(2,1)S(1)}, u32[]{:S(2)}, u32[]{:S(2)}) collective-permute-start(bf16[4,1,1032,128]{3,2,1,0:T(8,128)(2,1)S(1)} %shard_map.150.rest_0_), channel_id=1, source_target_pairs={{0,1},{1,0},{2,3},{3,2},{4,5},{5,4},{6,7},{7,6},{8,9},{9,8},{10,11... | collective-permute-start | bytes 3170312 | tf_op jit(solution)/shard_map/ppermute | solution.py:483
  104.8 84.5 %collective-permute-start.19 = (bf16[5,1032,128]{2,1,0:T(8,128)(2,1)}, bf16[5,1032,128]{2,1,0:T(8,128)(2,1)S(1)}, u32[]{:S(2)}, u32[]{:S(2)}) collective-permute-start(bf16[5,1032,128]{2,1,0:T(8,128)(2,1)} %collective-permute-done.12.refs_3_), channel_id=1, source_target_pairs={{0,1},{1,0},{2,3},{3,2},{4,5},{5,4},{6,7},{7,6},{8,9},{9,8},{10,11... | collective-permute-start | bytes 3962888 | tf_op jit(solution)/shard_map/ppermute | solution.py:483
  104.9 86.9 %collective-permute-start.18 = (bf16[5,1032,128]{2,1,0:T(8,128)(2,1)}, bf16[5,1032,128]{2,1,0:T(8,128)(2,1)S(1)}, u32[]{:S(2)}, u32[]{:S(2)}) collective-permute-start(bf16[5,1032,128]{2,1,0:T(8,128)(2,1)} %copy-done.23), channel_id=1, source_target_pairs={{0,1},{1,0},{2,3},{3,2},{4,5},{5,4},{6,7},{7,6},{8,9},{9,8},{10,11... | collective-permute-start | bytes 3962888 | tf_op jit(solution)/shard_map/ppermute | solution.py:483
  110.9 85.2 %collective-permute-start.17 = (bf16[5,1032,128]{2,1,0:T(8,128)(2,1)}, bf16[5,1032,128]{2,1,0:T(8,128)(2,1)S(1)}, u32[]{:S(2)}, u32[]{:S(2)}) collective-permute-start(bf16[5,1032,128]{2,1,0:T(8,128)(2,1)} %copy-done.24), channel_id=1, source_target_pairs={{0,1},{1,0},{2,3},{3,2},{4,5},{5,4},{6,7},{7,6},{8,9},{9,8},{10,11... | collective-permute-start | bytes 3962888 | tf_op jit(solution)/shard_map/ppermute | solution.py:483
  131.8 7.2 %collective-permute-start.9 = (bf16[288,256]{1,0:T(8,128)(2,1)S(1)}, bf16[288,256]{1,0:T(8,128)(2,1)S(1)}, u32[]{:S(2)}, u32[]{:S(2)}) collective-permute-start(bf16[288,256]{1,0:T(8,128)(2,1)S(1)} %shard_map.149.h0), channel_id=1, source_target_pairs={{0,2},{1,3},{2,4},{3,5},{4,6},{5,7},{6,0},{7,1},{8,10},{9,11},{10,... | collective-permute-start | bytes 442376 | tf_op jit(solution)/shard_map/ppermute | solution.py:480
  132.9 6.6 %collective-permute-start.8 = (bf16[288,256]{1,0:T(8,128)(2,1)S(1)}, bf16[288,256]{1,0:T(8,128)(2,1)S(1)}, u32[]{:S(2)}, u32[]{:S(2)}) collective-permute-start(bf16[288,256]{1,0:T(8,128)(2,1)S(1)} %shard_map.149.h0), channel_id=1, source_target_pairs={{0,4},{1,5},{2,6},{3,7},{4,0},{5,1},{6,2},{7,3},{8,12},{9,13},{10,... | collective-permute-start | bytes 442376 | tf_op jit(solution)/shard_map/ppermute | solution.py:480
  139.0 106.0 %collective-permute-start.21 = (bf16[2,1032,512]{2,1,0:T(8,128)(2,1)}, bf16[2,1032,512]{2,1,0:T(8,128)(2,1)}, u32[]{:S(2)}, u32[]{:S(2)}) collective-permute-start(bf16[2,1032,512]{2,1,0:T(8,128)(2,1)} %get-tuple-element.90.packed), channel_id=1, source_target_pairs={{0,2},{1,3},{2,0},{3,1},{4,6},{5,7},{6,4},{7,5},{8,10},{9,11},{10,... | collective-permute-start | bytes 6340616 | tf_op jit(solution)/shard_map/ppermute | solution.py:620
  139.5 46.9 %collective-permute-start.7 = (bf16[288,256]{1,0:T(8,128)(2,1)S(1)}, bf16[288,256]{1,0:T(8,128)(2,1)S(1)}, u32[]{:S(2)}, u32[]{:S(2)}) collective-permute-start(bf16[288,256]{1,0:T(8,128)(2,1)S(1)} %shard_map.149.h0), channel_id=1, source_target_pairs={{0,6},{1,7},{2,0},{3,1},{4,2},{5,3},{6,4},{7,5},{8,14},{9,15},{10,... | collective-permute-start | bytes 442376 | tf_op jit(solution)/shard_map/ppermute | solution.py:480
  189.2 6.9 %collective-permute-start.14 = (bf16[65,1024]{1,0:T(8,128)(2,1)S(1)}, bf16[65,1024]{1,0:T(8,128)(2,1)S(1)}, u32[]{:S(2)}, u32[]{:S(2)}) collective-permute-start(bf16[65,1024]{1,0:T(8,128)(2,1)S(1)} %get-tuple-element.83), channel_id=1, source_target_pairs={{0,2},{1,3},{2,4},{3,5},{4,6},{5,7},{6,0},{7,1},{8,10},{9,11},{10,... | collective-permute-start | bytes 399368 | tf_op jit(solution)/shard_map/ppermute | solution.py:480
  189.3 6.8 %collective-permute-start.15 = (bf16[65,1024]{1,0:T(8,128)(2,1)S(1)}, bf16[65,1024]{1,0:T(8,128)(2,1)S(1)}, u32[]{:S(2)}, u32[]{:S(2)}) collective-permute-start(bf16[65,1024]{1,0:T(8,128)(2,1)S(1)} %get-tuple-element.84), channel_id=1, source_target_pairs={{0,4},{1,5},{2,6},{3,7},{4,0},{5,1},{6,2},{7,3},{8,12},{9,13},{10,... | collective-permute-start | bytes 399368 | tf_op jit(solution)/shard_map/ppermute | solution.py:480
  219.2 6.9 %collective-permute-start.20 = (bf16[32,56,128]{2,1,0:T(8,128)(2,1)S(1)}, bf16[32,56,128]{2,1,0:T(8,128)(2,1)S(1)}, u32[]{:S(2)}, u32[]{:S(2)}) collective-permute-start(bf16[32,56,128]{2,1,0:T(8,128)(2,1)S(1)} %all_to_all.21.r_own), channel_id=1, source_target_pairs={{0,1},{1,0},{2,3},{3,2},{4,5},{5,4},{6,7},{7,6},{8,9},{9,8},{10,11... | collective-permute-start | bytes 1376264 | tf_op jit(solution)/shard_map/ppermute | solution.py:483
  230.3 14.7 %all-to-all-start.3 = ((bf16[32,24,128]{2,1,0:T(8,128)(2,1)}), bf16[32,24,128]{2,1,0:T(8,128)(2,1)}, u32[]{:S(2)}, u32[]{:S(2)}) async-start(bf16[32,24,128]{2,1,0:T(8,128)(2,1)} %shard_map.156), calls=%async_computation.3 | async-start | bytes 393216 | tf_op jit(solution)/shard_map/all_to_all | solution.py:517
  245.0 14.1 %collective-permute-start.22 = (bf16[2,1032,512]{2,1,0:T(8,128)(2,1)}, bf16[2,1032,512]{2,1,0:T(8,128)(2,1)S(1)}, u32[]{:S(2)}, u32[]{:S(2)}) collective-permute-start(bf16[2,1032,512]{2,1,0:T(8,128)(2,1)} %collective-permute-done.21.far), channel_id=1, source_target_pairs={{0,1},{1,0},{2,3},{3,2},{4,5},{5,4},{6,7},{7,6},{8,9},{9,8},{10,11... | collective-permute-start | bytes 6340616 | tf_op jit(solution)/shard_map/ppermute | solution.py:483
  254.6 7.5 %collective-permute-start.24 = (bf16[65,1024]{1,0:T(8,128)(2,1)S(1)}, bf16[65,1024]{1,0:T(8,128)(2,1)S(1)}, u32[]{:S(2)}, u32[]{:S(2)}) collective-permute-start(bf16[65,1024]{1,0:T(8,128)(2,1)S(1)} %get-tuple-element.94.n), channel_id=1, source_target_pairs={{0,6},{1,7},{2,4},{3,5},{4,2},{5,3},{6,0},{7,1},{8,14},{9,15},{10,... | collective-permute-start | bytes 399368 | tf_op jit(solution)/shard_map/ppermute | solution.py:620
  261.7 11.3 %collective-permute-start.23 = (f32[32,1024]{1,0:T(8,128)S(1)}, f32[32,1024]{1,0:T(8,128)S(1)}, u32[]{:S(2)}, u32[]{:S(2)}) collective-permute-start(f32[32,1024]{1,0:T(8,128)S(1)} %get-tuple-element.98), channel_id=1, source_target_pairs={{0,1},{1,0},{2,3},{3,2},{4,5},{5,4},{6,7},{7,6},{8,9},{9,8},{10,11... | collective-permute-start | bytes 393224 | tf_op jit(solution)/shard_map/ppermute | solution.py:483
  266.2 6.9 %collective-permute-start.25 = (bf16[40,1024]{1,0:T(8,128)(2,1)S(1)}, bf16[40,1024]{1,0:T(8,128)(2,1)S(1)}, u32[]{:S(2)}, u32[]{:S(2)}) collective-permute-start(bf16[40,1024]{1,0:T(8,128)(2,1)S(1)} %get-tuple-element.99), channel_id=1, source_target_pairs={{0,6},{1,7},{2,4},{3,5},{4,2},{5,3},{6,0},{7,1},{8,14},{9,15},{10,... | collective-permute-start | bytes 245768 | tf_op jit(solution)/shard_map/ppermute | solution.py:620
  (33 other events, 746.2 us)

commit v3 on v2

--- a/solution.py
+++ b/solution.py
@@ -23,6 +23,10 @@
 GROUPS = ((1, 3, 2, 0),)
 
 
+def core_index():
+    return lax.rem(lax.axis_index("tensor"), 2)
+
+
 def lanes(shape):
     return lax.broadcasted_iota(jnp.int32, shape, len(shape) - 1)
 
@@ -38,27 +42,24 @@
     return off * lax.rsqrt(spread + 1e-06) * gain + bias
 
 
-def pack_kernel(w_ref, wo_ref, bias_ref, held, biases, sems):
+def pack_kernel(w_ref, wo_ref, bias_ref, x_ref, held, wide, raw, w, biases, sems):
     copies = [
         pltpu.make_async_copy(w_ref.at[1], held.at[0:3, 0:D, :], sems.at[0]),
         pltpu.make_async_copy(bias_ref, biases, sems.at[1]),
     ]
-    for layer in range(LAYERS):
-        for j in range(8):
-            cols = slice(128 * j, 128 * j + 128)
-            copies.append(
-                pltpu.make_async_copy(
-                    wo_ref.at[layer, :, cols], held.at[4 - layer, cols, :], sems.at[2 + 8 * layer + j]
-                )
-            )
+    for j in range(8):
+        cols = slice(128 * j, 128 * j + 128)
+        copies.append(pltpu.make_async_copy(wo_ref.at[0, :, cols], held.at[3, cols, :], sems.at[2 + j]))
+        copies.append(pltpu.make_async_copy(wo_ref.at[1, :, cols], wide.at[cols, :], sems.at[10 + j]))
+    copies.append(pltpu.make_async_copy(x_ref.at[0], raw, sems.at[18]))
+    copies.append(pltpu.make_async_copy(w_ref.at[0], w, sems.at[19]))
     for copy in copies:
         copy.start()
     for copy in copies:
         copy.wait()
     for i in range(3):
         held[i, D:HELD, :] = split_rows(biases[i, 1:2, :])
-    for i in (3, 4):
-        held[i, D:HELD, :] = jnp.zeros((8, 128), jnp.bfloat16)
+    held[3, D:HELD, :] = jnp.zeros((8, 128), jnp.bfloat16)
 
 
 def tables_kernel(frame_time, cond_count, order, mask, row_time):
@@ -78,30 +79,37 @@
         mask[:, 128 * t + 128 : 128 * t + 256] = seen.astype(jnp.bfloat16)
 
 
-def load_kernel(planes, *refs):
-    *held, out, sems = refs
-    copies = [pltpu.make_async_copy(ref.at[planes], out.at[c], sems.at[c]) for c, ref in enumerate(held)]
+def plane_kernel(h0, h1, h2, h3, out):
+    for c, held in enumerate((h0, h1, h2, h3)):
+        out[c] = held[3, 0:D]
+
+
+def stack_kernel(w0, w1, w2, w3, out):
+    for c, w in enumerate((w0, w1, w2, w3)):
+        out[c] = w[...]
+
+
+def load_mlp_kernel(w1_ref, b1_ref, w2_ref, packed_a, packed_b, w1, w2, bias, sems):
+    copies = [
+        pltpu.make_async_copy(w1_ref.at[0], w1, sems.at[0]),
+        pltpu.make_async_copy(w2_ref.at[0], w2, sems.at[1]),
+        pltpu.make_async_copy(b1_ref, bias, sems.at[2]),
+    ]
+    for h, packed in enumerate((packed_a, packed_b)):
+        units = slice(256 * h, 256 * h + 256)
+        copies.append(pltpu.make_async_copy(w1_ref.at[1, :, units], packed.at[0, 0:D], sems.at[3 + 5 * h]))
+        for j in range(4):
+            cols = slice(256 * j, 256 * j + 256)
+            copies.append(
+                pltpu.make_async_copy(w2_ref.at[1, units, cols], packed.at[1, cols], sems.at[4 + 5 * h + j])
+            )
     for copy in copies:
         copy.start()
     for copy in copies:
         copy.wait()
-
-
-def load_mlp_kernel(w1_ref, b1_ref, w2_ref, packed, w1, w2, bias, sems):
-    copies = [
-        pltpu.make_async_copy(w1_ref.at[0], w1, sems.at[4]),
-        pltpu.make_async_copy(w2_ref.at[0], w2, sems.at[5]),
-        pltpu.make_async_copy(w1_ref.at[1], packed.at[0, 0:D], sems.at[0]),
-        pltpu.make_async_copy(w2_ref.at[1, :, 0:512], packed.at[1, 0:512], sems.at[1]),
-        pltpu.make_async_copy(w2_ref.at[1, :, 512:D], packed.at[1, 512:D], sems.at[2]),
-        pltpu.make_async_copy(b1_ref, bias, sems.at[3]),
-    ]
-    for copy in copies:
-        copy.start()
-    for copy in copies:
-        copy.wait()
-    packed[0, D:HELD, :] = split_rows(bias[1:2, :])
-    packed[1, D:HELD, :] = jnp.zeros((8, 512), jnp.bfloat16)
+    for h, packed in enumerate((packed_a, packed_b)):
+        packed[0, D:HELD, :] = split_rows(bias[1:2, 256 * h : 256 * h + 256])
+        packed[1, D:HELD, :] = jnp.zeros((8, 256), jnp.bfloat16)
 
 
 def split_rows(row):
@@ -144,23 +152,10 @@
             out[slot + hl, 48:56, :] = tail.astype(jnp.bfloat16)
 
 
-def start_kernel(
-    idx, x_ref, w_own, w_par, b_own, b_par, g_ref, b_ref, xrows, out, raw, wide, rows, w, biases, norms, sems
-):
-    x, k = idx[0], idx[1]
-    first = [
-        pltpu.make_async_copy(x_ref.at[0], raw, sems.at[0]),
-        pltpu.make_async_copy(g_ref, norms.at[0], sems.at[1]),
-        pltpu.make_async_copy(b_ref, norms.at[1], sems.at[2]),
-        pltpu.make_async_copy(b_own, biases, sems.at[3]),
-    ]
-    weights = [pltpu.make_async_copy(ref.at[0], w.at[c], sems.at[4 + c]) for c, ref in enumerate((w_own, w_par))]
-    for copy in first + weights:
-        copy.start()
-    for copy in first:
-        copy.wait()
-    wide[...] = raw[...].astype(jnp.float32)
-    gain, bias = norms[0, 0:1, :], norms[1, 0:1, :]
+def start_kernel(x_ref, w_own, w_par, b_own, b_par, g_ref, b_ref, xrows, out, wide, rows):
+    x, k = lax.axis_index("tensor") // 2, core_index()
+    wide[...] = x_ref[...].astype(jnp.float32)
+    gain, bias = g_ref[0:1, :], b_ref[0:1, :]
     for s in range(NX):
         chip = lax.rem(x + s, NX)
         for b in range(2):
@@ -172,20 +167,18 @@
         at = PAD * s + 64
         rows[at : at + 8, :] = norm(part, gain, bias).astype(jnp.bfloat16)
         xrows[at : at + 8, :] = part.astype(jnp.bfloat16)
-    for copy in weights:
-        copy.wait()
-    both = jnp.concatenate([w[c, i] for c in range(2) for i in range(3)], axis=1)
+    both = jnp.concatenate([w[i] for w in (w_own, w_par.at[0]) for i in range(3)], axis=1)
     both = jnp.dot(rows[...], both, preferred_element_type=jnp.float32)
-    for c, (side, row) in enumerate(((k, biases), (1 - k, b_par))):
+    for c, (side, row) in enumerate(((k, b_own), (1 - k, b_par))):
         places = [(s * 8 + b * 4 + 2 * side, PAD * s + 32 * b) for s in range(NX) for b in range(2)]
         tails = [(s * 8 + k * 4 + 2 * side, PAD * s + 64) for s in range(NX)]
         parts = [both[:, 384 * c + 128 * i : 384 * c + 128 * i + 128] + row[i, 0:1, :] for i in range(3)]
         emit(out, *parts, places, tails)
 
 
-def turn_kernel(idx, first, y0, y1, y2, y3, o_bias, gain, bias, *rest):
-    w, *near, stream, out, rows, acc = rest
-    k = idx[1]
+def turn_kernel(first, y0, y1, y2, y3, o_bias, gain, bias, *rest):
+    owns, pars, (stream, out, rows, acc) = rest[:NX], rest[NX : 2 * NX], rest[2 * NX :]
+    k = core_index()
     summed = (y0[...].astype(jnp.float32) + y1[...].astype(jnp.float32)) + (
         y2[...].astype(jnp.float32) + y3[...].astype(jnp.float32)
     )
@@ -202,10 +195,8 @@
                 at = 384 * c + 128 * i
                 acc[slot, i] = total[:, at : at + 128] + row
 
-    project((3, 5), near[0:2])
-    project((7, 1), (near[2], w.at[4]))
-    project((0, 2), (w.at[0], w.at[1]))
-    project((4, 6), (w.at[2], w.at[3]))
+    for s in range(NX):
+        project((2 * s, 2 * s + 1), (owns[s], pars[s]))
 
     def one(c, carry):
         base = c // 2 * 4 + 2 * lax.rem(k + c, 2)
@@ -215,8 +206,10 @@
     lax.fori_loop(0, 2 * NX, one, 0)
 
 
-def attn_kernel(layer, idx, order, mask, part_time, r_own, r_par, out, kt, vals, score, prob):
-    mine = idx[2 + layer]
+def attn_kernel(layer, order, mask, part_time, r_own, r_par, out, kt, vals, score, prob):
+    slot = lax.axis_index("tm")
+    slot_core = lax.rem(slot // 4, 2) if layer == 0 else slot // 16
+    mine = jnp.where(core_index() == slot_core, 1, 0)
     low = lanes((128, 128)) < 64
 
     def place(at, block):
@@ -316,8 +309,8 @@
     dst[at + 64 : at + 72, :] = lo[16:24]
 
 
-def heads_kernel(idx, back, out):
-    k = idx[1]
+def heads_kernel(back, out):
+    k = core_index()
     for c, side in enumerate((k, 1 - k)):
         for s in range(NX):
             slots = [s * 8 + b * 4 + 2 * side for b in range(2)]
@@ -336,7 +329,7 @@
             at = PAD * ((r - s) % NX)
             lhs[PAD * r : PAD * r + PAD, 256 * s : 256 * s + 256] = heads[at : at + PAD, :]
     weight = jnp.concatenate(
-        [blocks_of(p) for s in range(NX) for p in (w.at[s, 0], w_par.at[s, 0])], axis=0
+        [blocks_of(p) for s in range(NX) for p in (w.at[s], w_par.at[s])], axis=0
     )
     total = jnp.dot(lhs[...], weight, preferred_element_type=jnp.float32)
     rows = xrows[...].astype(jnp.float32) + total + o_bias[0:1, :]
@@ -344,16 +337,16 @@
     normed[...] = norm(rows, gain[0:1, :], bias[0:1, :]).astype(jnp.bfloat16)
 
 
-def whole_out_kernel(idx, back, own, o_bias, gain, bias, *rest):
-    w, *near, first, normed, heads = rest
-    k = idx[1]
+def whole_out_kernel(back, own, o_bias, gain, bias, *rest):
+    w, w_par, first, normed, heads = rest
+    k = core_index()
     for s in range(NX):
         for c, side in enumerate((k, 1 - k)):
             base = s * 4 + 2 * side
             at = 256 * s + 128 * c
             gather_heads(heads.at[:, at : at + 128], 0, back, [base, 16 + base], k * 16 + base)
     weight = jnp.concatenate(
-        [blocks_of(p) for s in range(NX) for p in (w.at[s, 0], near[s - 1].at[3] if s else w.at[4, 0])], axis=0
+        [blocks_of(p.at[s]) for s in range(NX) for p in (w, w_par)], axis=0
     )
     total = jnp.dot(heads[...], weight, preferred_element_type=jnp.float32)
     rows = own[...].astype(jnp.float32) + total[:65] + o_bias[1:2, :]
@@ -386,8 +379,8 @@
         inner = hidden(rows, w[0, 0:D, :], bias)
         part = jnp.concatenate(
             [
-                jnp.dot(inner, w[1, 512 * j : 512 * j + 512, :], preferred_element_type=jnp.float32)
-                for j in range(2)
+                jnp.dot(inner, w[1, 256 * j : 256 * j + 256, :], preferred_element_type=jnp.float32)
+                for j in range(4)
             ],
             axis=1,
         )
@@ -399,33 +392,40 @@
     return jnp.dot(hidden(rows, w1_par[1], b1_par[1:2, :]), w2_par[1], preferred_element_type=jnp.float32)
 
 
-def near_mlp_kernel(first, n, packed, w1_par, b1_par, w2_par, o_bias, total, rows):
+def own_mlp_kernel(first, n, o_bias, w1_par, b1_par, w2_par, own_a, own_b, far_a, total, rows):
     rows[0:65, :] = n[...]
-    share = add_mlp(core_mlp(rows[...], w1_par, b1_par, w2_par), rows[...], packed)
+    share = core_mlp(rows[...], w1_par, b1_par, w2_par)
+    share = add_mlp(share, rows[...], own_a, own_b, far_a)
     total[...] = first[...] + share[:65] + o_bias[1:2, :]
 
 
-def far_mlp_kernel(idx, n, near, far, far_par, keep, send, rows):
-    k = idx[1]
+def half_mlp_kernel(total, n, far_b, far_a_par, out, rows):
     rows[0:65, :] = n[...]
-    share = add_mlp(None, rows[...], far, far_par)
-    total = near[...] + share[:65]
+    out[...] = total[...] + add_mlp(None, rows[...], far_b, far_a_par)[:65]
+
+
+def moved_mlp_kernel(n, w1_par, b1_par, w2_par, own_a, own_b, far_a, far_a_par, far_b, total, rows):
+    rows[0:65, :] = n[...]
+    share = core_mlp(rows[...], w1_par, b1_par, w2_par)
+    total[...] = add_mlp(share, rows[...], own_a, own_b, far_a, far_a_par, far_b)
+
+
+def end_mlp_kernel(mine, moved, n, m, far_b_par, keep, send, here, there, rows):
+    k = core_index()
+    rows[0:65, :] = n[...]
+    rows[PAD : PAD + 65, :] = m[...]
+    share = add_mlp(None, rows[...], far_b_par)
+    total = mine[...] + share[:65]
     keep[...] = total
     send[...] = jnp.where(k == 0, total[32:64], total[0:32])
-
-
-def pair_mlp_kernel(idx, n, packed, w1_par, b1_par, w2_par, far, far_par, here, there, rows):
-    k = idx[1]
-    rows[0:65, :] = n[...]
-    total = core_mlp(rows[...], w1_par, b1_par, w2_par)
-    total = add_mlp(total, rows[...], packed, far, far_par).astype(jnp.bfloat16)
+    total = (moved[...] + share[PAD:]).astype(jnp.bfloat16)
     here[0:32, :] = jnp.where(k == 0, total[0:32], total[32:64])
     here[32:40, :] = total[64:72]
     there[...] = jnp.where(k == 0, total[32:64], total[0:32])
 
 
-def last_kernel(idx, keep, other, here, there, out):
-    k = idx[1]
+def last_kernel(keep, other, here, there, out):
+    k = core_index()
     mine = jnp.where(k == 0, keep[0:32, :], keep[32:64, :]) + here[0:32, :].astype(jnp.float32)
     theirs = other[...] + there[...].astype(jnp.float32)
     out[0, 0:32, :] = jnp.where(k == 0, mine, theirs).astype(jnp.bfloat16)
@@ -442,7 +442,7 @@
     return jax.ShapeDtypeStruct((rows, D), dtype)
 
 
-def call(kernel, args, out_shape, scratch=(), scalars=1, limit=8, out_specs=None, in_specs=None, aliases=None):
+def call(kernel, args, out_shape, scratch=(), scalars=0, limit=8, out_specs=None, in_specs=None, aliases=None):
     return pl.pallas_call(
         kernel,
         out_shape=out_shape,
@@ -471,10 +471,6 @@
     fc2_weight,
     fc2_bias,
 ):
-    part = lax.axis_index("tm")
-    pos = lax.axis_index("tensor")
-    x, k = pos // 2, pos % 2
-
     def shift(array, s):
         pairs = [(t, ((t // 2 + s) % NX) * 2 + t % 2) for t in range(2 * NX)]
         return lax.ppermute(array, "tensor", pairs)
@@ -497,12 +493,14 @@
         arrived, *late = tie((arrived, *late))
         arrived_par = swap(arrived)
         seen.append(beside())
+        if layer == 1:
+            late = [seen[1]]
         order, mask, row_time = seen[0]
         arrived, arrived_par, *late = tie((arrived, arrived_par, *late))
         late = [swap(a) for a in late]
         mixed = call(
             functools.partial(attn_kernel, layer),
-            (idx, order, mask, row_time, arrived, arrived_par),
+            (order, mask, row_time, arrived, arrived_par),
             jax.ShapeDtypeStruct((PARTS, 24, 128), jnp.bfloat16),
             [
                 pltpu.VMEM((256, KEYS), jnp.bfloat16),
@@ -510,7 +508,7 @@
                 pltpu.VMEM((3, 256, KEYS), jnp.float32),
                 pltpu.VMEM((3, 256, KEYS), jnp.bfloat16),
             ],
-            scalars=2,
+            scalars=1,
             limit=24,
         )
         mixed, *late = tie((mixed, *late, *ahead))
@@ -523,13 +521,17 @@
         return [pltpu.with_memory_space_constraint(a, pltpu.HBM) for a in arrays]
 
     biases = jnp.transpose(qkv_bias, (1, 0, 2))
-    idx = jnp.stack([x, k, k == (part // 4) % 2, k == part // 16]).astype(jnp.int32)
-    held = call(
+    held, wide, raw, w_own = call(
         pack_kernel,
-        in_hbm(qkv_weight, out_weight, biases),
-        jax.ShapeDtypeStruct((5, HELD, 128), jnp.bfloat16),
-        [pltpu.VMEM((3, LAYERS, 128), jnp.float32), pltpu.SemaphoreType.DMA((18,))],
-        in_specs=[HBM] * 3,
+        in_hbm(qkv_weight, out_weight, biases, frames_in),
+        [
+            jax.ShapeDtypeStruct((4, HELD, 128), jnp.bfloat16),
+            jax.ShapeDtypeStruct((D, 128), jnp.bfloat16),
+            block(rows=8 * BLOCK),
+            jax.ShapeDtypeStruct((3, D, 128), jnp.bfloat16),
+        ],
+        [pltpu.VMEM((3, LAYERS, 128), jnp.float32), pltpu.SemaphoreType.DMA((20,))],
+        in_specs=[HBM] * 4,
     )
     held, late_qkv, late_biases, late_fc2 = tie((held, qkv_weight, biases, fc2_weight))
     qkv_par = swap(late_qkv)
@@ -539,19 +541,9 @@
     held_par = swap(held)
     xrows, message = call(
         start_kernel,
-        (idx, *in_hbm(frames_in, qkv_weight, qkv_par, biases), biases_par, *in_hbm(ln1_gain, ln1_bias)),
+        (raw, w_own, qkv_par, biases, biases_par, ln1_gain, ln1_bias),
         [block(rows=NX * PAD), message_shape],
-        [
-            pltpu.VMEM((8 * BLOCK, D), jnp.bfloat16),
-            pltpu.VMEM((8 * BLOCK, D), jnp.float32),
-            pltpu.VMEM((NX * PAD, D), jnp.bfloat16),
-            pltpu.VMEM((2, 3, D, 128), jnp.bfloat16),
-            pltpu.VMEM((3, LAYERS, 128), jnp.float32),
-            pltpu.VMEM((2, LAYERS, D), jnp.float32),
-            pltpu.SemaphoreType.DMA((6,)),
-        ],
-        in_specs=[SMEM, HBM, HBM, HBM, HBM, VMEM, HBM, HBM],
-        limit=12,
+        [pltpu.VMEM((8 * BLOCK, D), jnp.float32), pltpu.VMEM((NX * PAD, D), jnp.bfloat16)],
     )
     message = tie(message)
 
@@ -568,36 +560,29 @@
             out_specs=[SMEM, VMEM, VMEM],
         )
 
-    def load(planes, count, refs):
-        return call(
-            functools.partial(load_kernel, planes),
-            refs,
-            jax.ShapeDtypeStruct((len(refs), count, HELD, 128), jnp.bfloat16),
-            [pltpu.SemaphoreType.DMA((len(refs),))],
-            in_specs=[HBM] * len(refs),
-        )
-
     back, fc1_par, fc1_bias_par, fc2_par, held_par = attention(
         0, message, tables, fc1_weight, fc1_bias, ahead=(fc2_par, held_par)
     )
-    heads = call(heads_kernel, (idx, back), jax.ShapeDtypeStruct((NX * PAD, 256), jnp.bfloat16))
+    heads = call(heads_kernel, (back,), jax.ShapeDtypeStruct((NX * PAD, 256), jnp.bfloat16))
+    loaded = call(plane_kernel, helds, jax.ShapeDtypeStruct((NX, D, 128), jnp.bfloat16))
+    loaded_par = swap(loaded)
+    heads, wide = tie((heads, wide))
     heads = spread(heads)
-    packed, w1, w2 = call(
+    wides = spread(wide)
+    packed_a, packed_b, w1, w2 = call(
         load_mlp_kernel,
         in_hbm(fc1_weight, fc1_bias, fc2_weight),
         [
-            jax.ShapeDtypeStruct((2, HELD, 512), jnp.bfloat16),
+            jax.ShapeDtypeStruct((2, HELD, 256), jnp.bfloat16),
+            jax.ShapeDtypeStruct((2, HELD, 256), jnp.bfloat16),
             jax.ShapeDtypeStruct((D, 512), jnp.bfloat16),
             jax.ShapeDtypeStruct((512, D), jnp.bfloat16),
         ],
-        [pltpu.VMEM((LAYERS, 512), jnp.float32), pltpu.SemaphoreType.DMA((6,))],
+        [pltpu.VMEM((LAYERS, 512), jnp.float32), pltpu.SemaphoreType.DMA((13,))],
         in_specs=[HBM] * 3,
     )
-    loaded = load(slice(4, 5), 1, in_hbm(*helds))
-    loaded_par = swap(loaded)
     held_pars = [held_par] + [swap(helds[s]) for s in (1, 2, 3)]
-    far_refs = in_hbm(*helds, held_pars[0])
-    near = held_pars[1:]
+    everything = (*helds, *held_pars)
     first, normed_two = call(
         every_out_kernel,
         (*heads, xrows, out_bias, ln2_gain, ln2_bias, loaded, loaded_par),
@@ -619,47 +604,49 @@
     def pair(array, other):
         return lax.ppermute(array, "tensor", [(t, other(t // 2) * 2 + t % 2) for t in range(2 * NX)])
 
-    far = pair(packed, lambda c: c ^ 1)
-    loaded = load(slice(0, 3), 3, far_refs)
+    far_a = pair(packed_a, lambda c: c ^ 1)
+    far_b = pair(packed_b, lambda c: c ^ 1)
     partial = collect(partial)
     stream, message = call(
         turn_kernel,
-        (idx, first, *partial, fc2_bias, ln1_gain, ln1_bias, loaded, *near),
+        (first, *partial, fc2_bias, ln1_gain, ln1_bias, *everything),
         [block(), message_shape],
         [pltpu.VMEM((PAD, D), jnp.bfloat16), pltpu.VMEM((2 * NX, 3, PAD, 128), jnp.float32)],
     )
-    (back,) = attention(1, message, lambda: load(slice(3, 4), 1, far_refs))
-    back, far, loaded = tie((back, far, seen[1]))
-    far_par = swap(far)
+
+    def stack():
+        return call(stack_kernel, wides, jax.ShapeDtypeStruct((NX, D, 128), jnp.bfloat16))
+
+    back, out_par = attention(1, message, stack)
     first, normed_two = call(
         whole_out_kernel,
-        (idx, back, stream, out_bias, ln2_gain, ln2_bias, loaded, *near),
+        (back, stream, out_bias, ln2_gain, ln2_bias, seen[1], out_par),
         [block(jnp.float32), block()],
         [pltpu.VMEM((PAD, D), jnp.bfloat16)],
     )
     moved = pair(normed_two, lambda c: 3 - c)
     pad = [pltpu.VMEM((PAD, D), jnp.bfloat16)]
-    weights = (packed, fc1_par, fc1_bias_par, fc2_par)
-    total = call(
-        near_mlp_kernel,
-        (first, normed_two, *weights, fc2_bias),
-        block(jnp.float32),
-        pad,
-        scalars=0,
-    )
-    keep, send = call(
-        far_mlp_kernel,
-        (idx, normed_two, total, far, far_par),
-        [block(jnp.float32), block(jnp.float32, 32)],
-        pad,
-    )
+    shared = (fc1_par, fc1_bias_par, fc2_par, packed_a, packed_b, far_a)
+    far_a_par = swap(far_a)
+    total = call(own_mlp_kernel, (first, normed_two, fc2_bias, *shared), block(jnp.float32), pad)
+    total, last_half = tie((total, far_b))
+    far_b_par = swap(last_half)
+    total = call(half_mlp_kernel, (total, normed_two, far_b, far_a_par), block(jnp.float32), pad)
+    passed = call(
+        moved_mlp_kernel, (moved, *shared, far_a_par, far_b), block(jnp.float32, PAD), pad
+    )
+    keep, send, here, there = call(
+        end_mlp_kernel,
+        (total, passed, normed_two, moved, far_b_par),
+        [block(jnp.float32), block(jnp.float32, 32), block(rows=40), block(rows=32)],
+        [pltpu.VMEM((2 * PAD, D), jnp.bfloat16)],
+    )
+    here = pair(here, lambda c: 3 - c)
     other = swap(send)
-    here, there = call(pair_mlp_kernel, (idx, moved, *weights, far, far_par), [block(rows=40), block(rows=32)], pad)
-    here = pair(here, lambda c: 3 - c)
     cross = [(t, (3 - t // 2) * 2 + 1 - t % 2) for t in range(2 * NX)]
     there = lax.ppermute(there, "tensor", cross)
     return call(
-        last_kernel, (idx, keep, other, here, there), jax.ShapeDtypeStruct((1, BLOCK, D), jnp.bfloat16)
+        last_kernel, (keep, other, here, there), jax.ShapeDtypeStruct((1, BLOCK, D), jnp.bfloat16)
     )
 
 

time: 275 us -> 245 us (0.89)
  the two profiles are of different devices: /device:TPU:1 before, /device:TPU:35 now
where the time goes in v3:
time: 245 us; the launch traced here: 241 us
  waiting for transfers between devices  108 us (44%)
  blocking collectives  56.1 us (23%)
  starting transfers between devices  39.5 us (16%)
  Pallas kernels  31.7 us (13%)
  local copies, waits for them, and re-layouts  5.57 us (2%)
    ppermute x12, waiting for transfers between devices, shift(): return lax.ppermute(array, 'tensor', pairs)  64.6 us
    all_to_all x2, blocking collectives, attention(): arrived = lax.all_to_all(message, 'tm', 0, 0, tiled=True)  41.3 us
    ppermute x4, waiting for transfers between devices, pair(): lax.ppermute(array, 'tensor', [(t, other(t // 2) * 2 + t % 2) for t in ra...  32.6 us
    pallas_call x18, Pallas kernels, call(): pl.pallas_call(kernel, out_shape=out_shape, in_specs=in_specs or [SMEM] *...  31.7 us
    ppermute x16, starting transfers between devices, swap(): return lax.ppermute(array, 'tensor', [(t, t ^ 1) for t in range(2 * NX)])  17.2 us
    all_to_all x1, blocking collectives, attention(): back = lax.all_to_all(mixed, 'tm', 0, 0, tiled=True)  14.9 us
    ppermute x12, starting transfers between devices, shift(): return lax.ppermute(array, 'tensor', pairs)  13.8 us
    ppermute x16, waiting for transfers between devices, swap(): return lax.ppermute(array, 'tensor', [(t, t ^ 1) for t in range(2 * NX)])  7.05 us
  transfers between devices with their start and end apart: 34, of which 19 were waited for; matrix products, arithmetic and copies ran while one was open for 0% of the time, Pallas kernels for 10%

profile of v3, /device:TPU:35, one launch (start us, length us, event | category | flops | bytes accessed | tf_op | source)
XLA Modules:
  0.0 241.3 jit_solution(15222752841964898245)
XLA Ops:
  3.1 3.0 %collective-permute-done.1.b_par = f32[3,2,128]{2,1,0:T(2,128)S(1)} collective-permute-done((f32[3,2,128]{2,1,0:T(2,128)S(1)}, f32[3,2,128]{2,1,0:T(2,128)S(1)}, u32[]{:S(2)}, u32[]{:S(2)}) %collective-permute-start.1) | collective-permute-done | bytes 3104 | tf_op jit(solution)/shard_map/ppermute | solution.py:479
  7.5 25.7 %all_to_all.20.r_own = bf16[32,56,128]{2,1,0:T(8,128)(2,1)S(1)} all-to-all(bf16[32,56,128]{2,1,0:T(8,128)(2,1)S(1)} %get-tuple-element.72), channel_id=1, replica_groups=mesh['tm'=32,'tensor'=8] {'tm'}, dimensions={0} | all-to-all | bytes 917504 | tf_op jit(solution)/shard_map/all_to_all | solution.py:492
  33.2 2.4 %collective-permute-start.2 = (bf16[32,56,128]{2,1,0:T(8,128)(2,1)S(1)}, bf16[32,56,128]{2,1,0:T(8,128)(2,1)S(1)}, u32[]{:S(2)}, u32[]{:S(2)}) collective-permute-start(bf16[32,56,128]{2,1,0:T(8,128)(2,1)S(1)} %all_to_all.20.r_own), channel_id=1, source_target_pairs={{0,1},{1,0},{2,3},{3,2},{4,5},{5,4},{6,7},{7,6},{8,9},{9,8},{10,11... | collective-permute-start | bytes 1376264 | tf_op jit(solution)/shard_map/ppermute | solution.py:479
  40.1 20.4 %collective-permute-done.10.h1.rest_1_ = bf16[4,1032,128]{2,1,0:T(8,128)(2,1)S(1)} collective-permute-done((bf16[4,1032,128]{2,1,0:T(8,128)(2,1)S(1)}, bf16[4,1032,128]{2,1,0:T(8,128)(2,1)S(1)}, u32[]{:S(2)}, u32[]{:S(2)}) %collective-permute-start.10) | collective-permute-done | bytes 1056800 | tf_op jit(solution)/shard_map/ppermute | solution.py:476
  61.4 22.6 %collective-permute-done.11.h2.rest_2_ = bf16[4,1032,128]{2,1,0:T(8,128)(2,1)S(1)} collective-permute-done((bf16[4,1032,128]{2,1,0:T(8,128)(2,1)S(1)}, bf16[4,1032,128]{2,1,0:T(8,128)(2,1)S(1)}, u32[]{:S(2)}, u32[]{:S(2)}) %collective-permute-start.11) | collective-permute-done | bytes 1056800 | tf_op jit(solution)/shard_map/ppermute | solution.py:476
  84.0 2.4 %collective-permute-done.12.h3.rest_3_ = bf16[4,1032,128]{2,1,0:T(8,128)(2,1)S(1)} collective-permute-done((bf16[4,1032,128]{2,1,0:T(8,128)(2,1)S(1)}, bf16[4,1032,128]{2,1,0:T(8,128)(2,1)S(1)}, u32[]{:S(2)}, u32[]{:S(2)}) %collective-permute-start.12) | collective-permute-done | bytes 1056800 | tf_op jit(solution)/shard_map/ppermute | solution.py:476
  88.2 3.2 %collective-permute-done.4.b1_par = f32[2,512]{1,0:T(2,128)S(1)} collective-permute-done((f32[2,512]{1,0:T(2,128)S(1)}, f32[2,512]{1,0:T(2,128)S(1)}, u32[]{:S(2)}, u32[]{:S(2)}) %collective-permute-start.4) | collective-permute-done | bytes 4128 | tf_op jit(solution)/shard_map/ppermute | solution.py:479
  93.0 3.4 %shard_map.148 = bf16[32,24,128]{2,1,0:T(8,128)(2,1)S(1)} custom-call(s32[16]{0:T(128)S(1)} %get-tuple-element.64.order, bf16[16,2176]{1,0:T(8,128)(2,1)S(1)} %get-tuple-element.65.mask, s32[32,128]{1,0:T(8,128)S(1)} %get-tuple-element.66.part_time, bf16[32,56,128]{2,1,0:T(8,128)(2,1)S(1)} %all_to_all.20.r_own, ...), custom_call_target="tpu_custom_call" | custom-call | tf_op jit(solution)/shard_map/pallas_call | solution.py:446
  96.5 14.9 %all_to_all.21.back = bf16[32,24,128]{2,1,0:T(8,128)(2,1)S(1)} all-to-all(bf16[32,24,128]{2,1,0:T(8,128)(2,1)S(1)} %shard_map.148), channel_id=1, replica_groups=mesh['tm'=32,'tensor'=8] {'tm'}, dimensions={0} | all-to-all | bytes 393216 | tf_op jit(solution)/shard_map/all_to_all | solution.py:515
  116.6 3.3 %shard_map.152 = (bf16[2,1032,256]{2,1,0:T(8,128)(2,1)S(1)}, bf16[2,1032,256]{2,1,0:T(8,128)(2,1)}, bf16[1024,512]{1,0:T(8,128)(2,1)S(1)}, bf16[512,1024]{1,0:T(8,128)(2,1)S(1)}) custom-call(bf16[2,1024,512]{2,1,0:T(8,128)(2,1)} %w1_ref.1, f32[2,512]{1,0:T(2,128)} %b1_own.1, bf16[2,512,1024]{2,1,0:T(8,128)(2,1)} %w2_ref.1), custom_call_target="tpu_custom_call" | custom-call | tf_op jit(solution)/shard_map/pallas_call | solution.py:446
  128.1 2.7 %collective-permute-done.15.y2 = bf16[65,1024]{1,0:T(8,128)(2,1)S(1)} collective-permute-done((bf16[65,1024]{1,0:T(8,128)(2,1)S(1)}, bf16[65,1024]{1,0:T(8,128)(2,1)S(1)}, u32[]{:S(2)}, u32[]{:S(2)}) %collective-permute-start.15) | collective-permute-done | bytes 133152 | tf_op jit(solution)/shard_map/ppermute | solution.py:476
  134.8 15.6 %all_to_all.22.r_own = bf16[32,56,128]{2,1,0:T(8,128)(2,1)S(1)} all-to-all(bf16[32,56,128]{2,1,0:T(8,128)(2,1)S(1)} %get-tuple-element.103), channel_id=1, replica_groups=mesh['tm'=32,'tensor'=8] {'tm'}, dimensions={0} | all-to-all | bytes 917504 | tf_op jit(solution)/shard_map/all_to_all | solution.py:492
  150.4 6.8 %collective-permute-start.20 = (bf16[32,56,128]{2,1,0:T(8,128)(2,1)S(1)}, bf16[32,56,128]{2,1,0:T(8,128)(2,1)S(1)}, u32[]{:S(2)}, u32[]{:S(2)}) collective-permute-start(bf16[32,56,128]{2,1,0:T(8,128)(2,1)S(1)} %all_to_all.22.r_own), channel_id=1, source_target_pairs={{0,1},{1,0},{2,3},{3,2},{4,5},{5,4},{6,7},{7,6},{8,9},{9,8},{10,11... | collective-permute-start | bytes 1376264 | tf_op jit(solution)/shard_map/ppermute | solution.py:479
  161.6 3.4 %collective-permute-done.21.w1 = bf16[1024,128]{1,0:T(8,128)(2,1)S(1)} collective-permute-done((bf16[1024,128]{1,0:T(8,128)(2,1)S(1)}, bf16[1024,128]{1,0:T(8,128)(2,1)S(1)}, u32[]{:S(2)}, u32[]{:S(2)}) %collective-permute-start.21) | collective-permute-done | bytes 262176 | tf_op jit(solution)/shard_map/ppermute | solution.py:476
  165.0 6.8 %collective-permute-done.22.w2 = bf16[1024,128]{1,0:T(8,128)(2,1)S(1)} collective-permute-done((bf16[1024,128]{1,0:T(8,128)(2,1)S(1)}, bf16[1024,128]{1,0:T(8,128)(2,1)S(1)}, u32[]{:S(2)}, u32[]{:S(2)}) %collective-permute-start.22) | collective-permute-done | bytes 262176 | tf_op jit(solution)/shard_map/ppermute | solution.py:476
  174.5 2.6 %collective-permute-start.25 = (bf16[2,1032,256]{2,1,0:T(8,128)(2,1)S(1)}, bf16[2,1032,256]{2,1,0:T(8,128)(2,1)}, u32[]{:S(2)}, u32[]{:S(2)}) collective-permute-start(bf16[2,1032,256]{2,1,0:T(8,128)(2,1)S(1)} %get-tuple-element.115.own_a), channel_id=1, source_target_pairs={{0,2},{1,3},{2,0},{3,1},{4,6},{5,7},{6,4},{7,5},{8,10},{9,11},{10,... | collective-permute-start | bytes 3170312 | tf_op jit(solution)/shard_map/ppermute | solution.py:605
  177.1 4.1 %shard_map.156 = bf16[32,24,128]{2,1,0:T(8,128)(2,1)} custom-call(s32[16]{0:T(128)S(1)} %get-tuple-element.64.order, bf16[16,2176]{1,0:T(8,128)(2,1)S(1)} %get-tuple-element.65.mask, s32[32,128]{1,0:T(8,128)S(1)} %get-tuple-element.66.part_time, bf16[32,56,128]{2,1,0:T(8,128)(2,1)S(1)} %all_to_all.22.r_own, ...), custom_call_target="tpu_custom_call" | custom-call | tf_op jit(solution)/shard_map/pallas_call | solution.py:446
  182.3 4.0 %all-to-all-start.3 = ((bf16[32,24,128]{2,1,0:T(8,128)(2,1)}), bf16[32,24,128]{2,1,0:T(8,128)(2,1)S(1)}, u32[]{:S(2)}, u32[]{:S(2)}) async-start(bf16[32,24,128]{2,1,0:T(8,128)(2,1)} %shard_map.156), calls=%async_computation.3 | async-start | bytes 393216 | tf_op jit(solution)/shard_map/all_to_all | solution.py:515
  186.3 14.6 %collective-permute-done.25.far_a = bf16[2,1032,256]{2,1,0:T(8,128)(2,1)} collective-permute-done((bf16[2,1032,256]{2,1,0:T(8,128)(2,1)S(1)}, bf16[2,1032,256]{2,1,0:T(8,128)(2,1)}, u32[]{:S(2)}, u32[]{:S(2)}) %collective-permute-start.25) | collective-permute-done | bytes 1056800 | tf_op jit(solution)/shard_map/ppermute | solution.py:605
  205.7 2.9 %shard_map.158.total = f32[65,1024]{1,0:T(8,128)S(1)} custom-call(f32[65,1024]{1,0:T(8,128)S(1)} %get-tuple-element.113.first, bf16[65,1024]{1,0:T(8,128)(2,1)S(1)} %get-tuple-element.114.n, f32[2,1024]{1,0:T(2,128)S(1)} %copy-done.11, bf16[2,1024,512]{2,1,0:T(8,128)(2,1)S(1)} %copy-done.1, f32[2,512]{1,0:T(2,128)S(1)} %collective-permute-done.4.b1_par, ...), custom_call_target="tpu_custom_call" | custom-call | tf_op jit(solution)/shard_map/pallas_call | solution.py:446
  208.7 14.9 %collective-permute-done.26.far_b = bf16[2,1032,256]{2,1,0:T(8,128)(2,1)} collective-permute-done((bf16[2,1032,256]{2,1,0:T(8,128)(2,1)}, bf16[2,1032,256]{2,1,0:T(8,128)(2,1)}, u32[]{:S(2)}, u32[]{:S(2)}) %collective-permute-start.26) | collective-permute-done | bytes 1056800 | tf_op jit(solution)/shard_map/ppermute | solution.py:605
  226.4 3.2 %collective-permute-done.28.n.m = bf16[65,1024]{1,0:T(8,128)(2,1)S(1)} collective-permute-done((bf16[65,1024]{1,0:T(8,128)(2,1)S(1)}, bf16[65,1024]{1,0:T(8,128)(2,1)S(1)}, u32[]{:S(2)}, u32[]{:S(2)}) %collective-permute-start.28) | collective-permute-done | bytes 133152 | tf_op jit(solution)/shard_map/ppermute | solution.py:605
  229.6 3.9 %shard_map.160.moved = f32[72,1024]{1,0:T(8,128)S(1)} custom-call(bf16[65,1024]{1,0:T(8,128)(2,1)S(1)} %collective-permute-done.28.n.m, bf16[2,1024,512]{2,1,0:T(8,128)(2,1)S(1)} %copy-done.1, f32[2,512]{1,0:T(2,128)S(1)} %collective-permute-done.4.b1_par, bf16[2,512,1024]{2,1,0:T(8,128)(2,1)S(1)} %collective-permute-done.5.w2_par, ...), custom_call_target="tpu_custom_call" | custom-call | tf_op jit(solution)/shard_map/pallas_call | solution.py:446
  236.7 3.8 %collective-permute-done.32.there = bf16[32,1024]{1,0:T(8,128)(2,1)S(1)} collective-permute-done((bf16[32,1024]{1,0:T(8,128)(2,1)S(1)}, bf16[32,1024]{1,0:T(8,128)(2,1)S(1)}, u32[]{:S(2)}, u32[]{:S(2)}) %collective-permute-start.32) | collective-permute-done | bytes 65568 | tf_op jit(solution)/shard_map/ppermute | solution.py:647
  (105 shorter events, 50.3 us)
Async XLA Ops:
  35.7 24.8 %collective-permute-start.10 = (bf16[4,1032,128]{2,1,0:T(8,128)(2,1)S(1)}, bf16[4,1032,128]{2,1,0:T(8,128)(2,1)S(1)}, u32[]{:S(2)}, u32[]{:S(2)}) collective-permute-start(bf16[4,1032,128]{2,1,0:T(8,128)(2,1)S(1)} %get-tuple-element.81.h0.rest_0_), channel_id=1, source_target_pairs={{0,6},{1,7},{2,0},{3,1},{4,2},{5,3},{6,4},{7,5},{8,14},{9,15},{10,... | collective-permute-start | bytes 3170312 | tf_op jit(solution)/shard_map/ppermute | solution.py:476
  35.9 52.2 %collective-permute-start.5 = (bf16[2,512,1024]{2,1,0:T(8,128)(2,1)S(1)}, bf16[2,512,1024]{2,1,0:T(8,128)(2,1)S(1)}, u32[]{:S(2)}, u32[]{:S(2)}) collective-permute-start(bf16[2,512,1024]{2,1,0:T(8,128)(2,1)S(1)} %copy-done.18), channel_id=1, source_target_pairs={{0,1},{1,0},{2,3},{3,2},{4,5},{5,4},{6,7},{7,6},{8,9},{9,8},{10,11... | collective-permute-start | bytes 6291464 | tf_op jit(solution)/shard_map/ppermute | solution.py:479
  37.1 59.3 %collective-permute-start.3 = (bf16[2,1024,512]{2,1,0:T(8,128)(2,1)S(1)}, bf16[2,1024,512]{2,1,0:T(8,128)(2,1)S(1)}, u32[]{:S(2)}, u32[]{:S(2)}) collective-permute-start(bf16[2,1024,512]{2,1,0:T(8,128)(2,1)S(1)} %copy-done.17), channel_id=1, source_target_pairs={{0,1},{1,0},{2,3},{3,2},{4,5},{5,4},{6,7},{7,6},{8,9},{9,8},{10,11... | collective-permute-start | bytes 6291464 | tf_op jit(solution)/shard_map/ppermute | solution.py:479
  37.5 46.6 %collective-permute-start.11 = (bf16[4,1032,128]{2,1,0:T(8,128)(2,1)S(1)}, bf16[4,1032,128]{2,1,0:T(8,128)(2,1)S(1)}, u32[]{:S(2)}, u32[]{:S(2)}) collective-permute-start(bf16[4,1032,128]{2,1,0:T(8,128)(2,1)S(1)} %get-tuple-element.81.h0.rest_0_), channel_id=1, source_target_pairs={{0,4},{1,5},{2,6},{3,7},{4,0},{5,1},{6,2},{7,3},{8,12},{9,13},{10,... | collective-permute-start | bytes 3170312 | tf_op jit(solution)/shard_map/ppermute | solution.py:476
  39.3 47.1 %collective-permute-start.12 = (bf16[4,1032,128]{2,1,0:T(8,128)(2,1)S(1)}, bf16[4,1032,128]{2,1,0:T(8,128)(2,1)S(1)}, u32[]{:S(2)}, u32[]{:S(2)}) collective-permute-start(bf16[4,1032,128]{2,1,0:T(8,128)(2,1)S(1)} %get-tuple-element.81.h0.rest_0_), channel_id=1, source_target_pairs={{0,2},{1,3},{2,4},{3,5},{4,6},{5,7},{6,0},{7,1},{8,10},{9,11},{10,... | collective-permute-start | bytes 3170312 | tf_op jit(solution)/shard_map/ppermute | solution.py:476
  60.5 27.2 %collective-permute-start.6 = (bf16[4,1032,128]{2,1,0:T(8,128)(2,1)S(1)}, bf16[4,1032,128]{2,1,0:T(8,128)(2,1)S(1)}, u32[]{:S(2)}, u32[]{:S(2)}) collective-permute-start(bf16[4,1032,128]{2,1,0:T(8,128)(2,1)S(1)} %get-tuple-element.81.h0.rest_0_), channel_id=1, source_target_pairs={{0,1},{1,0},{2,3},{3,2},{4,5},{5,4},{6,7},{7,6},{8,9},{9,8},{10,11... | collective-permute-start | bytes 3170312 | tf_op jit(solution)/shard_map/ppermute | solution.py:479
  86.5 26.4 %collective-permute-start.13 = (bf16[4,1024,128]{2,1,0:T(8,128)(2,1)S(1)}, bf16[4,1024,128]{2,1,0:T(8,128)(2,1)S(1)}, u32[]{:S(2)}, u32[]{:S(2)}) collective-permute-start(bf16[4,1024,128]{2,1,0:T(8,128)(2,1)S(1)} %shard_map.150.rest_0_), channel_id=1, source_target_pairs={{0,1},{1,0},{2,3},{3,2},{4,5},{5,4},{6,7},{7,6},{8,9},{9,8},{10,11... | collective-permute-start | bytes 3145736 | tf_op jit(solution)/shard_map/ppermute | solution.py:479
  87.6 39.6 %collective-permute-start.17 = (bf16[4,1032,128]{2,1,0:T(8,128)(2,1)S(1)}, bf16[4,1032,128]{2,1,0:T(8,128)(2,1)S(1)}, u32[]{:S(2)}, u32[]{:S(2)}) collective-permute-start(bf16[4,1032,128]{2,1,0:T(8,128)(2,1)S(1)} %collective-permute-done.10.h1.rest_1_), channel_id=1, source_target_pairs={{0,1},{1,0},{2,3},{3,2},{4,5},{5,4},{6,7},{7,6},{8,9},{9,8},{10,11... | collective-permute-start | bytes 3170312 | tf_op jit(solution)/shard_map/ppermute | solution.py:479
  88.1 39.1 %collective-permute-start.18 = (bf16[4,1032,128]{2,1,0:T(8,128)(2,1)S(1)}, bf16[4,1032,128]{2,1,0:T(8,128)(2,1)S(1)}, u32[]{:S(2)}, u32[]{:S(2)}) collective-permute-start(bf16[4,1032,128]{2,1,0:T(8,128)(2,1)S(1)} %collective-permute-done.11.h2.rest_2_), channel_id=1, source_target_pairs={{0,1},{1,0},{2,3},{3,2},{4,5},{5,4},{6,7},{7,6},{8,9},{9,8},{10,11... | collective-permute-start | bytes 3170312 | tf_op jit(solution)/shard_map/ppermute | solution.py:479
  91.4 35.8 %collective-permute-start.19 = (bf16[4,1032,128]{2,1,0:T(8,128)(2,1)S(1)}, bf16[4,1032,128]{2,1,0:T(8,128)(2,1)S(1)}, u32[]{:S(2)}, u32[]{:S(2)}) collective-permute-start(bf16[4,1032,128]{2,1,0:T(8,128)(2,1)S(1)} %collective-permute-done.12.h3.rest_3_), channel_id=1, source_target_pairs={{0,1},{1,0},{2,3},{3,2},{4,5},{5,4},{6,7},{7,6},{8,9},{9,8},{10,11... | collective-permute-start | bytes 3170312 | tf_op jit(solution)/shard_map/ppermute | solution.py:479
  112.9 7.4 %collective-permute-start.8 = (bf16[288,256]{1,0:T(8,128)(2,1)S(1)}, bf16[288,256]{1,0:T(8,128)(2,1)S(1)}, u32[]{:S(2)}, u32[]{:S(2)}) collective-permute-start(bf16[288,256]{1,0:T(8,128)(2,1)S(1)} %shard_map.149.h0), channel_id=1, source_target_pairs={{0,4},{1,5},{2,6},{3,7},{4,0},{5,1},{6,2},{7,3},{8,12},{9,13},{10,... | collective-permute-start | bytes 442376 | tf_op jit(solution)/shard_map/ppermute | solution.py:476
  115.5 5.8 %collective-permute-start.9 = (bf16[288,256]{1,0:T(8,128)(2,1)S(1)}, bf16[288,256]{1,0:T(8,128)(2,1)S(1)}, u32[]{:S(2)}, u32[]{:S(2)}) collective-permute-start(bf16[288,256]{1,0:T(8,128)(2,1)S(1)} %shard_map.149.h0), channel_id=1, source_target_pairs={{0,2},{1,3},{2,4},{3,5},{4,6},{5,7},{6,0},{7,1},{8,10},{9,11},{10,... | collective-permute-start | bytes 442376 | tf_op jit(solution)/shard_map/ppermute | solution.py:476
  125.2 5.6 %collective-permute-start.15 = (bf16[65,1024]{1,0:T(8,128)(2,1)S(1)}, bf16[65,1024]{1,0:T(8,128)(2,1)S(1)}, u32[]{:S(2)}, u32[]{:S(2)}) collective-permute-start(bf16[65,1024]{1,0:T(8,128)(2,1)S(1)} %get-tuple-element.100), channel_id=1, source_target_pairs={{0,4},{1,5},{2,6},{3,7},{4,0},{5,1},{6,2},{7,3},{8,12},{9,13},{10,... | collective-permute-start | bytes 399368 | tf_op jit(solution)/shard_map/ppermute | solution.py:476
  150.4 21.9 %collective-permute-start.20 = (bf16[32,56,128]{2,1,0:T(8,128)(2,1)S(1)}, bf16[32,56,128]{2,1,0:T(8,128)(2,1)S(1)}, u32[]{:S(2)}, u32[]{:S(2)}) collective-permute-start(bf16[32,56,128]{2,1,0:T(8,128)(2,1)S(1)} %all_to_all.22.r_own), channel_id=1, source_target_pairs={{0,1},{1,0},{2,3},{3,2},{4,5},{5,4},{6,7},{7,6},{8,9},{9,8},{10,11... | collective-permute-start | bytes 1376264 | tf_op jit(solution)/shard_map/ppermute | solution.py:479
  157.1 7.9 %collective-permute-start.21 = (bf16[1024,128]{1,0:T(8,128)(2,1)S(1)}, bf16[1024,128]{1,0:T(8,128)(2,1)S(1)}, u32[]{:S(2)}, u32[]{:S(2)}) collective-permute-start(bf16[1024,128]{1,0:T(8,128)(2,1)S(1)} %get-tuple-element.104.w0), channel_id=1, source_target_pairs={{0,6},{1,7},{2,0},{3,1},{4,2},{5,3},{6,4},{7,5},{8,14},{9,15},{10,... | collective-permute-start | bytes 786440 | tf_op jit(solution)/shard_map/ppermute | solution.py:476
  158.3 13.5 %collective-permute-start.22 = (bf16[1024,128]{1,0:T(8,128)(2,1)S(1)}, bf16[1024,128]{1,0:T(8,128)(2,1)S(1)}, u32[]{:S(2)}, u32[]{:S(2)}) collective-permute-start(bf16[1024,128]{1,0:T(8,128)(2,1)S(1)} %get-tuple-element.104.w0), channel_id=1, source_target_pairs={{0,4},{1,5},{2,6},{3,7},{4,0},{5,1},{6,2},{7,3},{8,12},{9,13},{10,... | collective-permute-start | bytes 786440 | tf_op jit(solution)/shard_map/ppermute | solution.py:476
  159.5 12.7 %collective-permute-start.23 = (bf16[1024,128]{1,0:T(8,128)(2,1)S(1)}, bf16[1024,128]{1,0:T(8,128)(2,1)S(1)}, u32[]{:S(2)}, u32[]{:S(2)}) collective-permute-start(bf16[1024,128]{1,0:T(8,128)(2,1)S(1)} %get-tuple-element.104.w0), channel_id=1, source_target_pairs={{0,2},{1,3},{2,4},{3,5},{4,6},{5,7},{6,0},{7,1},{8,10},{9,11},{10,... | collective-permute-start | bytes 786440 | tf_op jit(solution)/shard_map/ppermute | solution.py:476
  172.3 9.0 %collective-permute-start.24 = (bf16[4,1024,128]{2,1,0:T(8,128)(2,1)S(1)}, bf16[4,1024,128]{2,1,0:T(8,128)(2,1)S(1)}, u32[]{:S(2)}, u32[]{:S(2)}) collective-permute-start(bf16[4,1024,128]{2,1,0:T(8,128)(2,1)S(1)} %shard_map.155.rest_0_), channel_id=1, source_target_pairs={{0,1},{1,0},{2,3},{3,2},{4,5},{5,4},{6,7},{7,6},{8,9},{9,8},{10,11... | collective-permute-start | bytes 3145736 | tf_op jit(solution)/shard_map/ppermute | solution.py:479
  174.5 26.4 %collective-permute-start.25 = (bf16[2,1032,256]{2,1,0:T(8,128)(2,1)S(1)}, bf16[2,1032,256]{2,1,0:T(8,128)(2,1)}, u32[]{:S(2)}, u32[]{:S(2)}) collective-permute-start(bf16[2,1032,256]{2,1,0:T(8,128)(2,1)S(1)} %get-tuple-element.115.own_a), channel_id=1, source_target_pairs={{0,2},{1,3},{2,0},{3,1},{4,6},{5,7},{6,4},{7,5},{8,10},{9,11},{10,... | collective-permute-start | bytes 3170312 | tf_op jit(solution)/shard_map/ppermute | solution.py:605
  177.1 46.4 %collective-permute-start.26 = (bf16[2,1032,256]{2,1,0:T(8,128)(2,1)}, bf16[2,1032,256]{2,1,0:T(8,128)(2,1)}, u32[]{:S(2)}, u32[]{:S(2)}) collective-permute-start(bf16[2,1032,256]{2,1,0:T(8,128)(2,1)} %get-tuple-element.116.own_b), channel_id=1, source_target_pairs={{0,2},{1,3},{2,0},{3,1},{4,6},{5,7},{6,4},{7,5},{8,10},{9,11},{10,... | collective-permute-start | bytes 3170312 | tf_op jit(solution)/shard_map/ppermute | solution.py:605
  182.3 19.4 %all-to-all-start.3 = ((bf16[32,24,128]{2,1,0:T(8,128)(2,1)}), bf16[32,24,128]{2,1,0:T(8,128)(2,1)S(1)}, u32[]{:S(2)}, u32[]{:S(2)}) async-start(bf16[32,24,128]{2,1,0:T(8,128)(2,1)} %shard_map.156), calls=%async_computation.3 | async-start | bytes 393216 | tf_op jit(solution)/shard_map/all_to_all | solution.py:515
  200.9 23.2 %collective-permute-start.27 = (bf16[2,1032,256]{2,1,0:T(8,128)(2,1)}, bf16[2,1032,256]{2,1,0:T(8,128)(2,1)}, u32[]{:S(2)}, u32[]{:S(2)}) collective-permute-start(bf16[2,1032,256]{2,1,0:T(8,128)(2,1)} %collective-permute-done.25.far_a), channel_id=1, source_target_pairs={{0,1},{1,0},{2,3},{3,2},{4,5},{5,4},{6,7},{7,6},{8,9},{9,8},{10,11... | collective-permute-start | bytes 3170312 | tf_op jit(solution)/shard_map/ppermute | solution.py:479
  223.6 9.9 %collective-permute-start.29 = (bf16[2,1032,256]{2,1,0:T(8,128)(2,1)}, bf16[2,1032,256]{2,1,0:T(8,128)(2,1)S(1)}, u32[]{:S(2)}, u32[]{:S(2)}) collective-permute-start(bf16[2,1032,256]{2,1,0:T(8,128)(2,1)} %collective-permute-done.26.far_b), channel_id=1, source_target_pairs={{0,1},{1,0},{2,3},{3,2},{4,5},{5,4},{6,7},{7,6},{8,9},{9,8},{10,11... | collective-permute-start | bytes 3170312 | tf_op jit(solution)/shard_map/ppermute | solution.py:479
  234.1 6.5 %collective-permute-start.30 = (f32[32,1024]{1,0:T(8,128)S(1)}, f32[32,1024]{1,0:T(8,128)S(1)}, u32[]{:S(2)}, u32[]{:S(2)}) collective-permute-start(f32[32,1024]{1,0:T(8,128)S(1)} %get-tuple-element.120), channel_id=1, source_target_pairs={{0,1},{1,0},{2,3},{3,2},{4,5},{5,4},{6,7},{7,6},{8,9},{9,8},{10,11... | collective-permute-start | bytes 393224 | tf_op jit(solution)/shard_map/ppermute | solution.py:479
  (30 other events, 367.5 us)
